TPU v7x, 128 devices: a whole 4x4x4 slice. The times are simulated.
128 devices in a mesh: fsdp: 32 (over x_hi, z, y), tensor: 4 (over x_lo, core).
Axes of the slice: x: 4 (x_hi: 2, x_lo: 2; x = x_hi * 2 + x_lo), y: 4, z: 4, core: 2. Of those that a mesh axis runs over, the one named last changes fastest.
Arguments:
- activations: bfloat16 [32768, 5120], P('fsdp', 'tensor'), may hold values from -6 to 6
- cotangent: bfloat16 [32768, 5120], P('fsdp', 'tensor'), may hold values from -0.032958984 to 0.032958984
- weights: float32 [5120, 5120], P(None, ('tensor', 'fsdp')), may hold values from -0.025 to 0.025
- first_moment: float32 [5120, 5120], P(None, ('tensor', 'fsdp')), may hold values from -3 to 3
- second_moment: float32 [5120, 5120], P(None, ('tensor', 'fsdp')), may hold values from 0.01 to 1
Outputs:
- weights_new: float32 [5120, 5120], P('fsdp', 'tensor')
- first_new: float32 [5120, 5120], P('fsdp', 'tensor')
- second_new: float32 [5120, 5120], P('fsdp', 'tensor')
- weights_bf16: bfloat16 [5120, 5120], P(None, 'tensor')
All inputs are finite; a program needn't handle non-finite values.
Results may differ from a plain program's by a relative error of at most 0.014.
Values may be sent and summed in bfloat16 or wider, within the bound.
No kernel may reach another device: no remote copies, remote signals or barrier semaphores. Data moves between devices by JAX's collectives and lax.ppermute only.
A program may use at most 128 MiB of HBM per device.

v0:
```python
import functools

import jax
import jax.numpy as jnp
from jax import lax
from jax.experimental import pallas as pl
from jax.experimental.pallas import tpu as pltpu
from jax.sharding import Mesh, PartitionSpec as P

STEP = 20


beta_one = 0.9
beta_two = 0.95
adam_eps = 1e-08
learn_rate = 0.0003
decay_rate = 0.1

D = 5120
ROWS = 160
COLS = 1280
SIDE = 640
FSDP = ("xh", "z", "y")
SIDES = (("y", "z"), ("z", "y"))
VMEM_LIMIT = 12 * 1024 * 1024

XH, Z, Y, XL, CORE = range(5)


def f32(value):
    return value.astype(jnp.float32)


def bf16(value):
    return value.astype(jnp.bfloat16)


def shift(value, axis, step):
    count = lax.axis_size(axis)
    return lax.ppermute(value, axis, [(i, (i + step) % count) for i in range(count)])


def shape(*dims, dtype=jnp.bfloat16):
    return jax.ShapeDtypeStruct(dims, dtype)


def call(kernel, place, args, outs, scratch=(), out_space=pltpu.VMEM, aliased=0):
    vmem = pl.BlockSpec(memory_space=pltpu.VMEM)
    there = pl.BlockSpec(memory_space=out_space)
    held = len(args) - aliased
    return pl.pallas_call(
        kernel,
        out_shape=outs,
        in_specs=[pl.BlockSpec(memory_space=pltpu.SMEM)] + [vmem] * held + [there] * aliased,
        out_specs=[there] * len(outs),
        scratch_shapes=scratch,
        input_output_aliases={1 + held + i: i for i in range(aliased)},
        compiler_params=pltpu.CompilerParams(vmem_limit_bytes=VMEM_LIMIT),
    )(place, *args)


def in_rows(step):
    def run(i, carry):
        step(pl.ds(pl.multiple_of(i * 32, 32), 32))
        return carry

    lax.fori_loop(0, ROWS // 32, run, 0)


def multiply(features, cotangent, blocks):
    def one(low_z, carry):
        result = lax.dot_general(
            features[:, pl.ds(pl.multiple_of(low_z * SIDE, 128), SIDE)],
            cotangent[...],
            (((0,), (0,)), ((), ())),
            preferred_element_type=jnp.float32,
        )
        for s in range(2):
            for j in range(4):
                blocks[low_z, s, j] = bf16(result[j * ROWS : (j + 1) * ROWS, s * SIDE : (s + 1) * SIDE])
        return carry

    lax.fori_loop(0, 2, one, 0)


def first_product_kernel(place, features, cotangent, made):
    multiply(features, cotangent, made)


def product_kernel(place, made, features, cotangent, *refs):
    left, right, blocks = refs[:7], refs[7:14], refs[14]
    multiply(features, cotangent, blocks)

    def arrange(values, core, low_z):
        z_of = 2 * core + low_z
        ahead = lax.rem(z_of + 4 - place[Z], 4)

        def y_block(steps):
            return values[low_z, 0, lax.rem(place[Y] + steps, 4)]

        own, far_up, far_down, near_up, near_down, hold_up, hold_down = left
        own[z_of] = y_block(0)

        @pl.when(core == 0)
        def _():
            far_up[low_z] = y_block(2)
            near_down[low_z] = y_block(3)
            hold_up[low_z] = y_block(1)

        @pl.when(core == 1)
        def _():
            near_up[low_z] = y_block(1)
            far_down[low_z] = y_block(2)
            hold_down[low_z] = y_block(3)

        own, far_up, far_down, near_up, near_down, hold_up, hold_down = right

        @pl.when(ahead == 0)
        def _():
            own[...] = values[low_z, 1]

        for steps, low, high in ((1, hold_up, near_up), (2, far_up, far_down), (3, near_down, hold_down)):

            @pl.when(ahead == steps)
            def _():
                low[...] = values[low_z, 1, :2]
                high[...] = values[low_z, 1, 2:]

    def one(low_z, carry):
        arrange(made, place[CORE], low_z)
        arrange(blocks, 1 - place[CORE], low_z)
        return carry

    lax.fori_loop(0, 2, one, 0)


def products(place, cotangent, mine, other):
    made = call(first_product_kernel, place, (mine, cotangent), [shape(2, 2, 4, ROWS, SIDE)])[0]
    outs = call(
        product_kernel,
        place,
        (made, other, cotangent),
        [shape(n, ROWS, SIDE) for n in (4, 2, 2, 2, 2, 2, 2) * 2],
        [pltpu.VMEM((2, 2, 4, ROWS, SIDE), jnp.bfloat16)],
    )
    return outs[:7], outs[7:]


def add_kernel(place, *refs):
    def step(rows):
        for k in range(4):
            for j in range(2):
                refs[8 + k][j, rows] = bf16(f32(refs[2 * k][j, rows]) + f32(refs[2 * k + 1][j, rows]))

    in_rows(step)


def pass_on(place, pairs):
    return call(add_kernel, place, [a for pair in pairs for a in pair], [shape(2, ROWS, SIDE)] * 4)


def finish_kernel(place, *refs):
    def step(rows):
        for s, spot in enumerate((Z, Y)):
            own, near_down, last_up, near_up, last_down = refs[5 * s : 5 * s + 5]
            outs = refs[10 + 4 * s : 14 + 4 * s]
            for steps in range(4):
                to = lax.rem(place[spot] + steps, 4)
                first, second = jnp.minimum(to, 1), jnp.maximum(to - 2, 0)
                near = jnp.where(to < 2, f32(near_down[first, rows]), f32(near_up[second, rows]))
                last = jnp.where(to < 2, f32(last_up[first, rows]), f32(last_down[second, rows]))
                value = f32(own[to, rows]) + near + last
                outs[steps][rows] = value.astype(outs[steps].dtype)

    in_rows(step)


def finish(place, sides):
    kinds = [jnp.float32, jnp.bfloat16, jnp.bfloat16, jnp.bfloat16] * 2
    outs = call(
        finish_kernel, place, [a for side in sides for a in side], [shape(ROWS, SIDE, dtype=k) for k in kinds]
    )
    return outs[:4], outs[4:]


def total_kernel(place, *refs):
    def step(rows):
        for s in range(2):
            keep, one, two, three = refs[4 * s : 4 * s + 4]
            refs[8][rows, s * SIDE : (s + 1) * SIDE] = bf16(keep[rows] + f32(one[rows]) + f32(two[rows]) + f32(three[rows]))

    in_rows(step)


def total(place, parts):
    return call(total_kernel, place, parts, [shape(ROWS, COLS)])[0]


def reduced(place, messages):
    far, near = [], []
    for (axis, _), m in zip(SIDES, messages):
        far.append((shift(m[1], axis, 1), shift(m[2], axis, -1)))
    for (axis, _), m in zip(SIDES, messages):
        near.append((shift(m[3], axis, 1), shift(m[4], axis, -1)))
    last = pass_on(place, [(m[5 + k], f[k]) for m, f in zip(messages, far) for k in range(2)])
    sides = []
    for s, ((axis, _), m) in enumerate(zip(SIDES, messages)):
        last_up, last_down = shift(last[2 * s], axis, 1), shift(last[2 * s + 1], axis, -1)
        sides.append((m[0], near[s][1], last_up, near[s][0], last_down))
    parts = []
    ends = finish(place, sides)
    for (_, axis), (keep, *sent) in zip(SIDES, ends):
        parts += [keep, *(shift(block, axis, k + 1) for k, block in enumerate(sent))]
    return total(place, parts), ends[0][1]


def adam_update(weights, first_moment, second_moment, gradient):
    first_new = beta_one * first_moment + (1.0 - beta_one) * gradient
    second_new = beta_two * second_moment + (1.0 - beta_two) * gradient * gradient
    corrected = first_new / (1.0 - beta_one**STEP)
    scaled = jnp.sqrt(second_new / (1.0 - beta_two**STEP)) + adam_eps
    weights_new = weights - learn_rate * (corrected / scaled + decay_rate * weights)
    return (weights_new, first_new, second_new)


def adam_kernel(place, near, near_got, far, far_got, here, there, weights, first, second, left, right):
    def step(rows):
        for half in range(2):
            is_near = half == place[XL]
            gradient = f32(jnp.where(is_near, f32(near[rows]), f32(far[rows]))) + jnp.where(
                is_near, f32(near_got[rows]), f32(far_got[rows])
            )
            for s, side in enumerate((left, right)):
                old = [
                    jnp.where(place[XH] == s, f32(here[half, k, rows]), f32(there[half, k, rows])) for k in range(3)
                ]
                columns = slice(s * SIDE, (s + 1) * SIDE)
                new = adam_update(*old, gradient[:, columns])
                side[half, rows] = bf16(new[0])

                @pl.when(half == place[XH])
                def _():
                    for ref, value in zip((weights, first, second), new):
                        ref[rows, columns] = value

    in_rows(step)


def adam(place, gradients, here, there):
    return call(
        adam_kernel,
        place,
        (*gradients, here, there),
        [shape(ROWS, COLS, dtype=jnp.float32)] * 3 + [shape(2, ROWS, SIDE)] * 2,
    )


def line_kernel(place, *refs):
    for s, spot in enumerate((Z, Y)):
        low, high = refs[8 + 2 * s], refs[9 + 2 * s]
        for k in range(4):
            block = refs[4 * s + k]
            source = lax.rem(place[spot] + 4 - k, 4)

            @pl.when(source < 2)
            def _(block=block, source=source, low=low):
                for x in range(2):
                    low[x, source] = block[x]

            @pl.when(source >= 2)
            def _(block=block, source=source, high=high):
                for x in range(2):
                    high[x, source - 2] = block[x]


def line(place, blocks):
    outs = call(line_kernel, place, blocks, [shape(2, 2, ROWS, SIDE)] * 4)
    return outs[:2], outs[2:]


def lay_kernel(steps, place, *refs):
    out, sems = refs[-2], refs[-1]
    copies = []
    for s, spot in enumerate((Y, Z)):
        columns = pl.ds(s * SIDE, SIDE)
        for k, (half, ahead) in enumerate(steps):
            other, pair = lax.rem(place[spot] + ahead, 4), pl.ds(2 * half, 2)
            index = (slice(None), pair, other) if s == 0 else (slice(None), other, pair)
            number = s * len(steps) + k
            copies.append(
                pltpu.make_async_copy(refs[number], out.at[(*index, slice(None), columns)], sems.at[number])
            )
    for copy in copies:
        copy.start()
    for copy in copies:
        copy.wait()


def lay(place, steps, pieces, *out):
    return call(
        functools.partial(lay_kernel, steps),
        place,
        [*pieces, *out],
        [shape(2, 4, 4, ROWS, COLS)],
        [pltpu.SemaphoreType.DMA((len(pieces),))],
        pltpu.HBM,
        len(out),
    )[0]


def gathered(place, blocks):
    pieces = []
    for (_, axis), block in zip(SIDES, blocks):
        pieces += [block, *(shift(block, axis, k) for k in (1, 2, 3))]
    lines = line(place, pieces)
    first = [(shift(low, axis, 1), shift(high, axis, -1)) for (axis, _), (low, high) in zip(SIDES, lines)]
    second = [(shift(high, axis, 1), shift(low, axis, -1)) for (axis, _), (low, high) in zip(SIDES, lines)]
    far = [(shift(up, axis, 1), shift(down, axis, -1)) for (axis, _), (up, down) in zip(SIDES, first)]
    near = [piece for own, a, b in zip(lines, first, second) for piece in (*own, *a, *b)]
    out = lay(place, ((0, 0), (1, 0), (0, 3), (1, 1), (1, 3), (0, 1)), near)
    return lay(place, ((0, 2), (1, 2)), [piece for pair in far for piece in pair], out)


def state_kernel(place, got, out, turned):
    def half(h, carry):
        for source in range(16):
            turned[source * 40 : (source + 1) * 40, :480] = f32(got[source, h])
        flat = turned[...].T
        for k in range(3):
            out[h, k] = bf16(flat[k * ROWS : (k + 1) * ROWS])
        return carry

    turned[:, 480:] = jnp.zeros((SIDE, 32), jnp.float32)
    lax.fori_loop(0, 2, half, 0)


def send_kernel(place, *refs):
    states, out = refs[:3], refs[3]

    def four(g, carry):
        for j in range(4):
            block = 4 * g + j
            for k, state in enumerate(states):
                rows = state[:, pl.ds(pl.multiple_of(g * SIDE, 128), SIDE)]
                out[lax.rem(block, 16), lax.div(block, 16), :, k * ROWS : (k + 1) * ROWS] = bf16(
                    rows[:, j * ROWS : (j + 1) * ROWS]
                )
        return carry

    lax.fori_loop(0, 8, four, 0)


def sent_state(place, states):
    return call(send_kernel, place, [s.T for s in states], [shape(16, 2, 40, 3 * ROWS)])[0]


def moved_state(place, flat):
    got = lax.all_to_all(flat, ("z", "y"), 0, 0, tiled=True)
    return call(
        state_kernel, place, (got,), [shape(2, 3, ROWS, SIDE)], [pltpu.VMEM((SIDE, 512), jnp.float32)]
    )[0]


def step(activations, cotangent, weights, first_moment, second_moment):
    place = jnp.stack([lax.axis_index(a) for a in ("xh", "z", "y", "xl", "c")]).astype(jnp.int32)
    across = shift(activations, "xl", 1)
    beside = shift(activations, "c", 1)
    flat = sent_state(place, (weights, first_moment, second_moment))
    beside, flat = lax.optimization_barrier((beside, flat))
    messages = products(place, cotangent, activations, beside)
    here = moved_state(place, flat)
    near, sent = reduced(place, messages)

    across, here, _ = lax.optimization_barrier((across, here, sent))
    there = shift(here, "xh", 1)
    messages = products(place, cotangent, across, shift(across, "c", 1))
    far, _ = reduced(place, messages)
    near_got = shift(near, "xh", 1)
    far_got = shift(far, "xh", 1)
    weights_new, first_new, second_new, left, right = adam(place, (near, near_got, far, far_got), here, there)
    out = gathered(place, (left, right))
    return (weights_new, first_new, second_new, out.reshape(D, COLS))


def solution(mesh):
    wide = Mesh(mesh.devices.reshape(2, 4, 4, 2, 2), ("xh", "z", "y", "xl", "c"))
    tensor = ("xl", "c")
    columns = P(None, (*tensor, *FSDP))
    rows = P(FSDP, tensor)
    return jax.shard_map(
        step,
        mesh=wide,
        in_specs=(rows, rows, columns, columns, columns),
        out_specs=(rows, rows, rows, P(None, tensor)),
        check_vma=False,
    )
```

profile of v0, /device:TPU:0, one launch (start us, length us, event | category | flops | bytes accessed | tf_op | source)
XLA Modules:
  0.0 288.6 jit_solution(15295033243421271416)
XLA Ops:
  0.7 1.7 collective-permute-start.20
  2.5 1.7 copy-done
  4.2 1.7 copy-done.3
  6.0 4.4 %shard_map.84.made = bf16[2,2,4,160,640]{4,3,2,1,0:T(8,128)(2,1)S(1)} custom-call(s32[5]{0:T(128)S(1)} %stack.23.place, bf16[1024,1280]{1,0:T(8,128)(2,1)S(1)} %copy-done.3, bf16[1024,1280]{1,0:T(8,128)(2,1)S(1)} %copy-done), custom_call_target="tpu_custom_call" | custom-call | tf_op jit(solution)/shard_map/pallas_call | solution.py:51
  13.0 7.4 %shard_map.86 = (bf16[4,160,640]{2,1,0:T(8,128)(2,1)S(1)}, bf16[2,160,640]{2,1,0:T(8,128)(2,1)}, bf16[2,160,640]{2,1,0:T(8,128)(2,1)}, bf16[2,160,640]{2,1,0:T(8...) custom-call(s32[5]{0:T(128)S(1)} %stack.23.place, ...), custom_call_target="tpu_custom_call" | custom-call | tf_op jit(solution)/shard_map/pallas_call | solution.py:51
  27.5 1.6 collective-permute-start.2
  29.1 1.7 collective-permute-start.3
  30.7 1.9 collective-permute-start.4
  32.6 2.1 collective-permute-start.5
  34.8 4.9 %all-to-all-start = ((bf16[16,2,40,480]{3,2,1,0:T(8,128)(2,1)}), bf16[16,2,40,480]{3,2,1,0:T(8,128)(2,1)}, u32[]{:S(2)}, u32[]{:S(2)}) async-start(bf16[16,2,40,480]{3,2,1,0:T(8,128)(2,1)} %copy-done.2), calls=%async_computation | async-start | bytes 2621440 | tf_op jit(solution)/shard_map/all_to_all | solution.py:358
  40.6 2.2 collective-permute-start.1
  42.8 8.6 %collective-permute-done.4.refs_5_ = bf16[2,160,640]{2,1,0:T(8,128)(2,1)} collective-permute-done((bf16[2,160,640]{2,1,0:T(8,128)(2,1)}, bf16[2,160,640]{2,1,0:T(8,128)(2,1)}, u32[]{:S(2)}, u32[]{:S(2)}) %collective-permute-start.4) | collective-permute-done | bytes 409632 | tf_op jit(solution)/shard_map/ppermute | solution.py:40
  51.5 5.0 %collective-permute-start.9 = (bf16[2,160,640]{2,1,0:T(8,128)(2,1)}, bf16[2,160,640]{2,1,0:T(8,128)(2,1)S(1)}, u32[]{:S(2)}, u32[]{:S(2)}) collective-permute-start(bf16[2,160,640]{2,1,0:T(8,128)(2,1)} %copy-done.22), channel_id=1, source_target_pairs={{0,48},{16,0},{32,16},{48,32},{1,49},{17,1},{33,17},{49,33},{2,50}... | collective-permute-start | bytes 1228808 | tf_op jit(solution)/shard_map/ppermute | solution.py:40
  57.1 1.5 collective-permute-start.11
  62.6 1.8 shard_map.87
  65.4 2.3 collective-permute-start.8
  68.7 2.3 collective-permute-start.12
  71.0 4.3 %collective-permute-done.6.refs_2_ = bf16[2,160,640]{2,1,0:T(8,128)(2,1)S(1)} collective-permute-done((bf16[2,160,640]{2,1,0:T(8,128)(2,1)S(1)}, bf16[2,160,640]{2,1,0:T(8,128)(2,1)S(1)}, u32[]{:S(2)}, u32[]{:S(2)}) %collective-permute-start.6) | collective-permute-done | bytes 409632 | tf_op jit(solution)/shard_map/ppermute | solution.py:40
  76.2 2.5 collective-permute-done.10.refs_7_
  78.7 1.6 shard_map.88
  86.0 1.9 shard_map.90.here
  88.2 5.6 %shard_map.91.made = bf16[2,2,4,160,640]{4,3,2,1,0:T(8,128)(2,1)S(1)} custom-call(s32[5]{0:T(128)S(1)} %stack.23.place, bf16[1024,1280]{1,0:T(8,128)(2,1)} %collective-permute-done.20.features, bf16[1024,1280]{1,0:T(8,128)(2,1)S(1)} %copy-done.1), custom_call_target="tpu_custom_call" | custom-call | tf_op jit(solution)/shard_map/pallas_call | solution.py:51
  93.8 5.1 %shard_map.92 = (bf16[4,160,640]{2,1,0:T(8,128)(2,1)S(1)}, bf16[2,160,640]{2,1,0:T(8,128)(2,1)S(1)}, bf16[2,160,640]{2,1,0:T(8,128)(2,1)S(1)}, bf16[2,160,640]{2...) custom-call(s32[5]{0:T(128)S(1)} %stack.23.place, ...), custom_call_target="tpu_custom_call" | custom-call | tf_op jit(solution)/shard_map/pallas_call | solution.py:51
  100.1 2.2 collective-permute-start.24
  103.5 2.0 collective-permute-start.26
  106.0 6.1 %collective-permute-done.23.refs_1_ = bf16[2,160,640]{2,1,0:T(8,128)(2,1)S(1)} collective-permute-done((bf16[2,160,640]{2,1,0:T(8,128)(2,1)S(1)}, bf16[2,160,640]{2,1,0:T(8,128)(2,1)S(1)}, u32[]{:S(2)}, u32[]{:S(2)}) %collective-permute-start.23) | collective-permute-done | bytes 409632 | tf_op jit(solution)/shard_map/ppermute | solution.py:40
  112.4 3.0 %collective-permute-start.30 = (bf16[2,160,640]{2,1,0:T(8,128)(2,1)S(1)}, bf16[2,160,640]{2,1,0:T(8,128)(2,1)S(1)}, u32[]{:S(2)}, u32[]{:S(2)}) collective-permute-start(bf16[2,160,640]{2,1,0:T(8,128)(2,1)S(1)} %get-tuple-element.112), channel_id=1, source_target_pairs={{0,48},{16,0},{32,16},{48,32},{1,49},{17,1},{33,17},{49,33},{2,50}... | collective-permute-start | bytes 1228808 | tf_op jit(solution)/shard_map/ppermute | solution.py:40
  118.4 6.5 %collective-permute-done.14.refs_2_ = bf16[160,640]{1,0:T(8,128)(2,1)S(1)} collective-permute-done((bf16[160,640]{1,0:T(8,128)(2,1)S(1)}, bf16[160,640]{1,0:T(8,128)(2,1)S(1)}, u32[]{:S(2)}, u32[]{:S(2)}) %collective-permute-start.14) | collective-permute-done | bytes 204832 | tf_op jit(solution)/shard_map/ppermute | solution.py:40
  125.6 2.7 collective-permute-start.29
  128.3 5.3 %collective-permute-start.31 = (bf16[2,160,640]{2,1,0:T(8,128)(2,1)S(1)}, bf16[2,160,640]{2,1,0:T(8,128)(2,1)S(1)}, u32[]{:S(2)}, u32[]{:S(2)}) collective-permute-start(bf16[2,160,640]{2,1,0:T(8,128)(2,1)S(1)} %get-tuple-element.113), channel_id=1, source_target_pairs={{0,16},{16,32},{32,48},{48,0},{1,17},{17,33},{33,49},{49,1},{2,18}... | collective-permute-start | bytes 1228808 | tf_op jit(solution)/shard_map/ppermute | solution.py:40
  133.8 2.7 collective-permute-start.41
  136.5 5.1 %collective-permute-start.15 = (bf16[160,640]{1,0:T(8,128)(2,1)S(1)}, bf16[160,640]{1,0:T(8,128)(2,1)S(1)}, u32[]{:S(2)}, u32[]{:S(2)}) collective-permute-start(bf16[160,640]{1,0:T(8,128)(2,1)S(1)} %copy-done.34), channel_id=1, source_target_pairs={{0,48},{16,0},{32,16},{48,32},{1,49},{17,1},{33,17},{49,33},{2,50}... | collective-permute-start | bytes 614408 | tf_op jit(solution)/shard_map/ppermute | solution.py:40
  141.6 2.3 collective-permute-start.17
  145.6 1.6 shard_map.94
  148.0 3.6 %collective-permute-done.16.refs_5_ = bf16[160,640]{1,0:T(8,128)(2,1)S(1)} collective-permute-done((bf16[160,640]{1,0:T(8,128)(2,1)S(1)}, bf16[160,640]{1,0:T(8,128)(2,1)S(1)}, u32[]{:S(2)}, u32[]{:S(2)}) %collective-permute-start.16) | collective-permute-done | bytes 204832 | tf_op jit(solution)/shard_map/ppermute | solution.py:40
  151.7 2.7 collective-permute-start.35
  154.3 2.6 collective-permute-start.36
  157.7 5.5 %collective-permute-done.34.refs_1_ = bf16[160,640]{1,0:T(8,128)(2,1)S(1)} collective-permute-done((bf16[160,640]{1,0:T(8,128)(2,1)S(1)}, bf16[160,640]{1,0:T(8,128)(2,1)S(1)}, u32[]{:S(2)}, u32[]{:S(2)}) %collective-permute-start.34) | collective-permute-done | bytes 204832 | tf_op jit(solution)/shard_map/ppermute | solution.py:40
  163.2 1.6 collective-permute-start.39
  165.5 2.9 collective-permute-start.19
  168.4 2.0 collective-permute-done.38.refs_6_
  171.2 2.8 collective-permute-start.40
  174.0 4.4 %collective-permute-done.19.near_got = bf16[160,1280]{1,0:T(8,128)(2,1)S(1)} collective-permute-done((bf16[160,1280]{1,0:T(8,128)(2,1)S(1)}, bf16[160,1280]{1,0:T(8,128)(2,1)S(1)}, u32[]{:S(2)}, u32[]{:S(2)}) %collective-permute-start.19) | collective-permute-done | bytes 409632 | tf_op jit(solution)/shard_map/ppermute | solution.py:40
  178.4 6.2 %collective-permute-done.40.far_got = bf16[160,1280]{1,0:T(8,128)(2,1)S(1)} collective-permute-done((bf16[160,1280]{1,0:T(8,128)(2,1)S(1)}, bf16[160,1280]{1,0:T(8,128)(2,1)S(1)}, u32[]{:S(2)}, u32[]{:S(2)}) %collective-permute-start.40) | collective-permute-done | bytes 409632 | tf_op jit(solution)/shard_map/ppermute | solution.py:40
  184.6 4.6 %shard_map.96 = (f32[160,1280]{1,0:T(8,128)}, f32[160,1280]{1,0:T(8,128)}, f32[160,1280]{1,0:T(8,128)}, bf16[2,160,640]{2,1,0:T(8,128)(2,1)S(1)}, bf16[2,160,640]{2,1,0:T(8,128)(2,1)S(1)}) custom-call(s32[5]{0:T(128)S(1)} %stack.23.place, bf16[160,1280]{1,0:T(8,128)(2,1)S(1)} %shard_map.89.near, bf16[160,1280]{1,0:T(8,128)(2,1)S(1)} %collective-permute-done.19.near_got, ...), custom_call_target="tpu_custom_call" | custom-call | tf_op jit(solution)/shard_map/pallas_call | solution.py:51
  189.2 2.3 collective-permute-start.44
  191.4 1.7 collective-permute-start.43
  193.2 1.9 collective-permute-start.46
  195.1 6.4 %collective-permute-done.44.refs_3_ = bf16[2,160,640]{2,1,0:T(8,128)(2,1)S(1)} collective-permute-done((bf16[2,160,640]{2,1,0:T(8,128)(2,1)S(1)}, bf16[2,160,640]{2,1,0:T(8,128)(2,1)S(1)}, u32[]{:S(2)}, u32[]{:S(2)}) %collective-permute-start.44) | collective-permute-done | bytes 409632 | tf_op jit(solution)/shard_map/ppermute | solution.py:40
  202.4 2.9 %collective-permute-done.43.refs_2_ = bf16[2,160,640]{2,1,0:T(8,128)(2,1)S(1)} collective-permute-done((bf16[2,160,640]{2,1,0:T(8,128)(2,1)S(1)}, bf16[2,160,640]{2,1,0:T(8,128)(2,1)S(1)}, u32[]{:S(2)}, u32[]{:S(2)}) %collective-permute-start.43) | collective-permute-done | bytes 409632 | tf_op jit(solution)/shard_map/ppermute | solution.py:40
  205.3 5.6 %collective-permute-done.42.refs_1_ = bf16[2,160,640]{2,1,0:T(8,128)(2,1)S(1)} collective-permute-done((bf16[2,160,640]{2,1,0:T(8,128)(2,1)S(1)}, bf16[2,160,640]{2,1,0:T(8,128)(2,1)S(1)}, u32[]{:S(2)}, u32[]{:S(2)}) %collective-permute-start.42) | collective-permute-done | bytes 409632 | tf_op jit(solution)/shard_map/ppermute | solution.py:40
  210.9 2.1 collective-permute-done.45.refs_5_
  216.0 3.2 %collective-permute-start.50 = (bf16[2,2,160,640]{3,2,1,0:T(8,128)(2,1)S(1)}, bf16[2,2,160,640]{3,2,1,0:T(8,128)(2,1)S(1)}, u32[]{:S(2)}, u32[]{:S(2)}) collective-permute-start(bf16[2,2,160,640]{3,2,1,0:T(8,128)(2,1)S(1)} %get-tuple-element.131.refs_1_), channel_id=1, source_target_pairs={{0,12},{4,0},{8,4},{12,8},{1,13},{5,1},{9,5},{13,9},{2,14},{6,2},{... | collective-permute-start | bytes 2457608 | tf_op jit(solution)/shard_map/ppermute | solution.py:40
  219.3 3.0 %collective-permute-start.59 = (bf16[2,2,160,640]{3,2,1,0:T(8,128)(2,1)S(1)}, bf16[2,2,160,640]{3,2,1,0:T(8,128)(2,1)S(1)}, u32[]{:S(2)}, u32[]{:S(2)}) collective-permute-start(bf16[2,2,160,640]{3,2,1,0:T(8,128)(2,1)S(1)} %get-tuple-element.132.refs_6_), channel_id=1, source_target_pairs={{0,48},{16,0},{32,16},{48,32},{1,49},{17,1},{33,17},{49,33},{2,50}... | collective-permute-start | bytes 2457608 | tf_op jit(solution)/shard_map/ppermute | solution.py:40
  222.2 12.9 %collective-permute-done.57.refs_5_ = bf16[2,2,160,640]{3,2,1,0:T(8,128)(2,1)S(1)} collective-permute-done((bf16[2,2,160,640]{3,2,1,0:T(8,128)(2,1)S(1)}, bf16[2,2,160,640]{3,2,1,0:T(8,128)(2,1)S(1)}, u32[]{:S(2)}, u32[]{:S(2)}) %collective-permute-start.57) | collective-permute-done | bytes 819232 | tf_op jit(solution)/shard_map/ppermute | solution.py:40
  235.1 5.6 %collective-permute-start.52 = (bf16[2,2,160,640]{3,2,1,0:T(8,128)(2,1)S(1)}, bf16[2,2,160,640]{3,2,1,0:T(8,128)(2,1)S(1)}, u32[]{:S(2)}, u32[]{:S(2)}) collective-permute-start(bf16[2,2,160,640]{3,2,1,0:T(8,128)(2,1)S(1)} %get-tuple-element.132.refs_6_), channel_id=1, source_target_pairs={{0,16},{16,32},{32,48},{48,0},{1,17},{17,33},{33,49},{49,1},{2,18}... | collective-permute-start | bytes 2457608 | tf_op jit(solution)/shard_map/ppermute | solution.py:40
  240.7 10.4 %collective-permute-done.56.refs_4_ = bf16[2,2,160,640]{3,2,1,0:T(8,128)(2,1)S(1)} collective-permute-done((bf16[2,2,160,640]{3,2,1,0:T(8,128)(2,1)S(1)}, bf16[2,2,160,640]{3,2,1,0:T(8,128)(2,1)S(1)}, u32[]{:S(2)}, u32[]{:S(2)}) %collective-permute-start.56) | collective-permute-done | bytes 819232 | tf_op jit(solution)/shard_map/ppermute | solution.py:40
  251.1 6.3 %collective-permute-start.58 = (bf16[2,2,160,640]{3,2,1,0:T(8,128)(2,1)S(1)}, bf16[2,2,160,640]{3,2,1,0:T(8,128)(2,1)S(1)}, u32[]{:S(2)}, u32[]{:S(2)}) collective-permute-start(bf16[2,2,160,640]{3,2,1,0:T(8,128)(2,1)S(1)} %get-tuple-element.133.refs_7_), channel_id=1, source_target_pairs={{0,16},{16,32},{32,48},{48,0},{1,17},{17,33},{33,49},{49,1},{2,18}... | collective-permute-start | bytes 2457608 | tf_op jit(solution)/shard_map/ppermute | solution.py:40
  257.4 3.2 %collective-permute-start.51 = (bf16[2,2,160,640]{3,2,1,0:T(8,128)(2,1)S(1)}, bf16[2,2,160,640]{3,2,1,0:T(8,128)(2,1)S(1)}, u32[]{:S(2)}, u32[]{:S(2)}) collective-permute-start(bf16[2,2,160,640]{3,2,1,0:T(8,128)(2,1)S(1)} %collective-permute-done.50.refs_3_), channel_id=1, source_target_pairs={{0,12},{4,0},{8,4},{12,8},{1,13},{5,1},{9,5},{13,9},{2,14},{6,2},{... | collective-permute-start | bytes 2457608 | tf_op jit(solution)/shard_map/ppermute | solution.py:40
  260.7 3.2 %collective-permute-start.55 = (bf16[2,2,160,640]{3,2,1,0:T(8,128)(2,1)S(1)}, bf16[2,2,160,640]{3,2,1,0:T(8,128)(2,1)S(1)}, u32[]{:S(2)}, u32[]{:S(2)}) collective-permute-start(bf16[2,2,160,640]{3,2,1,0:T(8,128)(2,1)S(1)} %collective-permute-done.54.refs_9_), channel_id=1, source_target_pairs={{0,48},{16,0},{32,16},{48,32},{1,49},{17,1},{33,17},{49,33},{2,50}... | collective-permute-start | bytes 2457608 | tf_op jit(solution)/shard_map/ppermute | solution.py:40
  263.9 12.1 %collective-permute-done.58.refs_10_ = bf16[2,2,160,640]{3,2,1,0:T(8,128)(2,1)S(1)} collective-permute-done((bf16[2,2,160,640]{3,2,1,0:T(8,128)(2,1)S(1)}, bf16[2,2,160,640]{3,2,1,0:T(8,128)(2,1)S(1)}, u32[]{:S(2)}, u32[]{:S(2)}) %collective-permute-start.58) | collective-permute-done | bytes 819232 | tf_op jit(solution)/shard_map/ppermute | solution.py:40
  276.0 4.4 %shard_map.98.refs_4_ = bf16[2,4,4,160,1280]{4,3,2,1,0:T(8,128)(2,1)} custom-call(s32[5]{0:T(128)S(1)} %stack.23.place, bf16[2,2,160,640]{3,2,1,0:T(8,128)(2,1)S(1)} %get-tuple-element.130.refs_0_, bf16[2,2,160,640]{3,2,1,0:T(8,128)(2,1)S(1)} %get-tuple-element.131.refs_1_, bf16[2,2,160,640]{3,2,1,0:T(8,128)(2,1)S(1)} %collective-permute-done.48.refs_2_, ...), custom_call_target="tpu_custom_call" | custom-call | tf_op jit(solution)/shard_map/pallas_call | solution.py:51
  280.5 5.7 %collective-permute-done.53.refs_2_ = bf16[2,2,160,640]{3,2,1,0:T(8,128)(2,1)S(1)} collective-permute-done((bf16[2,2,160,640]{3,2,1,0:T(8,128)(2,1)S(1)}, bf16[2,2,160,640]{3,2,1,0:T(8,128)(2,1)S(1)}, u32[]{:S(2)}, u32[]{:S(2)}) %collective-permute-start.53) | collective-permute-done | bytes 819232 | tf_op jit(solution)/shard_map/ppermute | solution.py:40
  286.2 2.3 shard_map.99
  (149 shorter events, 39.8 us)
Async XLA Ops:
  0.6 12.3 %collective-permute-start = (bf16[1024,1280]{1,0:T(8,128)(2,1)}, bf16[1024,1280]{1,0:T(8,128)(2,1)}, u32[]{:S(2)}, u32[]{:S(2)}) collective-permute-start(bf16[1024,1280]{1,0:T(8,128)(2,1)} %features.1), channel_id=1, source_target_pairs={{0,1},{1,0},{2,3},{3,2},{4,5},{5,4},{6,7},{7,6},{8,9},{9,8},{10,11... | collective-permute-start | bytes 7864328 | tf_op jit(solution)/shard_map/ppermute | solution.py:40
  0.7 87.2 %collective-permute-start.20 = (bf16[1024,1280]{1,0:T(8,128)(2,1)}, bf16[1024,1280]{1,0:T(8,128)(2,1)}, u32[]{:S(2)}, u32[]{:S(2)}) collective-permute-start(bf16[1024,1280]{1,0:T(8,128)(2,1)} %features.1), channel_id=1, source_target_pairs={{0,2},{2,0},{1,3},{3,1},{4,6},{6,4},{5,7},{7,5},{8,10},{10,8},{9,1... | collective-permute-start | bytes 7864328 | tf_op jit(solution)/shard_map/ppermute | solution.py:40
  27.5 13.1 %collective-permute-start.2 = (bf16[2,160,640]{2,1,0:T(8,128)(2,1)}, bf16[2,160,640]{2,1,0:T(8,128)(2,1)}, u32[]{:S(2)}, u32[]{:S(2)}) collective-permute-start(bf16[2,160,640]{2,1,0:T(8,128)(2,1)} %get-tuple-element.73), channel_id=1, source_target_pairs={{0,4},{4,8},{8,12},{12,0},{1,5},{5,9},{9,13},{13,1},{2,6},{6,10},{... | collective-permute-start | bytes 1228808 | tf_op jit(solution)/shard_map/ppermute | solution.py:40
  29.1 13.8 %collective-permute-start.3 = (bf16[2,160,640]{2,1,0:T(8,128)(2,1)}, bf16[2,160,640]{2,1,0:T(8,128)(2,1)}, u32[]{:S(2)}, u32[]{:S(2)}) collective-permute-start(bf16[2,160,640]{2,1,0:T(8,128)(2,1)} %get-tuple-element.75), channel_id=1, source_target_pairs={{0,12},{4,0},{8,4},{12,8},{1,13},{5,1},{9,5},{13,9},{2,14},{6,2},{... | collective-permute-start | bytes 1228808 | tf_op jit(solution)/shard_map/ppermute | solution.py:40
  30.7 20.7 %collective-permute-start.4 = (bf16[2,160,640]{2,1,0:T(8,128)(2,1)}, bf16[2,160,640]{2,1,0:T(8,128)(2,1)}, u32[]{:S(2)}, u32[]{:S(2)}) collective-permute-start(bf16[2,160,640]{2,1,0:T(8,128)(2,1)} %get-tuple-element.77), channel_id=1, source_target_pairs={{0,16},{16,32},{32,48},{48,0},{1,17},{17,33},{33,49},{49,1},{2,18}... | collective-permute-start | bytes 1228808 | tf_op jit(solution)/shard_map/ppermute | solution.py:40
  32.6 24.4 %collective-permute-start.5 = (bf16[2,160,640]{2,1,0:T(8,128)(2,1)}, bf16[2,160,640]{2,1,0:T(8,128)(2,1)}, u32[]{:S(2)}, u32[]{:S(2)}) collective-permute-start(bf16[2,160,640]{2,1,0:T(8,128)(2,1)} %get-tuple-element.79), channel_id=1, source_target_pairs={{0,48},{16,0},{32,16},{48,32},{1,49},{17,1},{33,17},{49,33},{2,50}... | collective-permute-start | bytes 1228808 | tf_op jit(solution)/shard_map/ppermute | solution.py:40
  34.8 51.2 %all-to-all-start = ((bf16[16,2,40,480]{3,2,1,0:T(8,128)(2,1)}), bf16[16,2,40,480]{3,2,1,0:T(8,128)(2,1)}, u32[]{:S(2)}, u32[]{:S(2)}) async-start(bf16[16,2,40,480]{3,2,1,0:T(8,128)(2,1)} %copy-done.2), calls=%async_computation | async-start | bytes 2621440 | tf_op jit(solution)/shard_map/all_to_all | solution.py:358
  40.6 23.9 %collective-permute-start.1 = (bf16[2,160,640]{2,1,0:T(8,128)(2,1)}, bf16[2,160,640]{2,1,0:T(8,128)(2,1)S(1)}, u32[]{:S(2)}, u32[]{:S(2)}) collective-permute-start(bf16[2,160,640]{2,1,0:T(8,128)(2,1)} %copy-done.24), channel_id=1, source_target_pairs={{0,12},{4,0},{8,4},{12,8},{1,13},{5,1},{9,5},{13,9},{2,14},{6,2},{... | collective-permute-start | bytes 1228808 | tf_op jit(solution)/shard_map/ppermute | solution.py:40
  42.8 22.6 %collective-permute-start.7 = (bf16[2,160,640]{2,1,0:T(8,128)(2,1)}, bf16[2,160,640]{2,1,0:T(8,128)(2,1)S(1)}, u32[]{:S(2)}, u32[]{:S(2)}) collective-permute-start(bf16[2,160,640]{2,1,0:T(8,128)(2,1)} %copy-done.23), channel_id=1, source_target_pairs={{0,4},{4,8},{8,12},{12,0},{1,5},{5,9},{9,13},{13,1},{2,6},{6,10},{... | collective-permute-start | bytes 1228808 | tf_op jit(solution)/shard_map/ppermute | solution.py:40
  51.5 16.3 %collective-permute-start.9 = (bf16[2,160,640]{2,1,0:T(8,128)(2,1)}, bf16[2,160,640]{2,1,0:T(8,128)(2,1)S(1)}, u32[]{:S(2)}, u32[]{:S(2)}) collective-permute-start(bf16[2,160,640]{2,1,0:T(8,128)(2,1)} %copy-done.22), channel_id=1, source_target_pairs={{0,48},{16,0},{32,16},{48,32},{1,49},{17,1},{33,17},{49,33},{2,50}... | collective-permute-start | bytes 1228808 | tf_op jit(solution)/shard_map/ppermute | solution.py:40
  57.1 11.6 %collective-permute-start.11 = (bf16[2,160,640]{2,1,0:T(8,128)(2,1)}, bf16[2,160,640]{2,1,0:T(8,128)(2,1)S(1)}, u32[]{:S(2)}, u32[]{:S(2)}) collective-permute-start(bf16[2,160,640]{2,1,0:T(8,128)(2,1)} %copy-done.21), channel_id=1, source_target_pairs={{0,16},{16,32},{32,48},{48,0},{1,17},{17,33},{33,49},{49,1},{2,18}... | collective-permute-start | bytes 1228808 | tf_op jit(solution)/shard_map/ppermute | solution.py:40
  64.4 10.9 %collective-permute-start.6 = (bf16[2,160,640]{2,1,0:T(8,128)(2,1)S(1)}, bf16[2,160,640]{2,1,0:T(8,128)(2,1)S(1)}, u32[]{:S(2)}, u32[]{:S(2)}) collective-permute-start(bf16[2,160,640]{2,1,0:T(8,128)(2,1)S(1)} %get-tuple-element.80), channel_id=1, source_target_pairs={{0,4},{4,8},{8,12},{12,0},{1,5},{5,9},{9,13},{13,1},{2,6},{6,10},{... | collective-permute-start | bytes 1228808 | tf_op jit(solution)/shard_map/ppermute | solution.py:40
  65.4 10.8 %collective-permute-start.8 = (bf16[2,160,640]{2,1,0:T(8,128)(2,1)S(1)}, bf16[2,160,640]{2,1,0:T(8,128)(2,1)S(1)}, u32[]{:S(2)}, u32[]{:S(2)}) collective-permute-start(bf16[2,160,640]{2,1,0:T(8,128)(2,1)S(1)} %get-tuple-element.82), channel_id=1, source_target_pairs={{0,12},{4,0},{8,4},{12,8},{1,13},{5,1},{9,5},{13,9},{2,14},{6,2},{... | collective-permute-start | bytes 1228808 | tf_op jit(solution)/shard_map/ppermute | solution.py:40
  67.8 11.0 %collective-permute-start.10 = (bf16[2,160,640]{2,1,0:T(8,128)(2,1)S(1)}, bf16[2,160,640]{2,1,0:T(8,128)(2,1)S(1)}, u32[]{:S(2)}, u32[]{:S(2)}) collective-permute-start(bf16[2,160,640]{2,1,0:T(8,128)(2,1)S(1)} %get-tuple-element.85), channel_id=1, source_target_pairs={{0,16},{16,32},{32,48},{48,0},{1,17},{17,33},{33,49},{49,1},{2,18}... | collective-permute-start | bytes 1228808 | tf_op jit(solution)/shard_map/ppermute | solution.py:40
  68.7 10.1 %collective-permute-start.12 = (bf16[2,160,640]{2,1,0:T(8,128)(2,1)S(1)}, bf16[2,160,640]{2,1,0:T(8,128)(2,1)S(1)}, u32[]{:S(2)}, u32[]{:S(2)}) collective-permute-start(bf16[2,160,640]{2,1,0:T(8,128)(2,1)S(1)} %get-tuple-element.87), channel_id=1, source_target_pairs={{0,48},{16,0},{32,16},{48,32},{1,49},{17,1},{33,17},{49,33},{2,50}... | collective-permute-start | bytes 1228808 | tf_op jit(solution)/shard_map/ppermute | solution.py:40
  87.9 5.9 %collective-permute-start.21 = (bf16[1024,1280]{1,0:T(8,128)(2,1)}, bf16[1024,1280]{1,0:T(8,128)(2,1)S(1)}, u32[]{:S(2)}, u32[]{:S(2)}) collective-permute-start(bf16[1024,1280]{1,0:T(8,128)(2,1)} %collective-permute-done.20.features), channel_id=1, source_target_pairs={{0,1},{1,0},{2,3},{3,2},{4,5},{5,4},{6,7},{7,6},{8,9},{9,8},{10,11... | collective-permute-start | bytes 7864328 | tf_op jit(solution)/shard_map/ppermute | solution.py:40
  98.9 46.3 %copy-start.28 = (bf16[160,640]{1,0:T(8,128)(2,1)S(1)}, bf16[160,640]{1,0:T(8,128)(2,1)}, u32[]{:S(2)}) copy-start(bf16[160,640]{1,0:T(8,128)(2,1)} %copy-done.27) | copy-start | bytes 614404
  98.9 13.1 %collective-permute-start.23 = (bf16[2,160,640]{2,1,0:T(8,128)(2,1)S(1)}, bf16[2,160,640]{2,1,0:T(8,128)(2,1)S(1)}, u32[]{:S(2)}, u32[]{:S(2)}) collective-permute-start(bf16[2,160,640]{2,1,0:T(8,128)(2,1)S(1)} %get-tuple-element.101), channel_id=1, source_target_pairs={{0,4},{4,8},{8,12},{12,0},{1,5},{5,9},{9,13},{13,1},{2,6},{6,10},{... | collective-permute-start | bytes 1228808 | tf_op jit(solution)/shard_map/ppermute | solution.py:40
  100.1 12.3 %collective-permute-start.24 = (bf16[2,160,640]{2,1,0:T(8,128)(2,1)S(1)}, bf16[2,160,640]{2,1,0:T(8,128)(2,1)S(1)}, u32[]{:S(2)}, u32[]{:S(2)}) collective-permute-start(bf16[2,160,640]{2,1,0:T(8,128)(2,1)S(1)} %get-tuple-element.103), channel_id=1, source_target_pairs={{0,12},{4,0},{8,4},{12,8},{1,13},{5,1},{9,5},{13,9},{2,14},{6,2},{... | collective-permute-start | bytes 1228808 | tf_op jit(solution)/shard_map/ppermute | solution.py:40
  102.2 13.2 %collective-permute-start.25 = (bf16[2,160,640]{2,1,0:T(8,128)(2,1)S(1)}, bf16[2,160,640]{2,1,0:T(8,128)(2,1)S(1)}, u32[]{:S(2)}, u32[]{:S(2)}) collective-permute-start(bf16[2,160,640]{2,1,0:T(8,128)(2,1)S(1)} %get-tuple-element.105), channel_id=1, source_target_pairs={{0,16},{16,32},{32,48},{48,0},{1,17},{17,33},{33,49},{49,1},{2,18}... | collective-permute-start | bytes 1228808 | tf_op jit(solution)/shard_map/ppermute | solution.py:40
  103.5 13.0 %collective-permute-start.26 = (bf16[2,160,640]{2,1,0:T(8,128)(2,1)S(1)}, bf16[2,160,640]{2,1,0:T(8,128)(2,1)S(1)}, u32[]{:S(2)}, u32[]{:S(2)}) collective-permute-start(bf16[2,160,640]{2,1,0:T(8,128)(2,1)S(1)} %get-tuple-element.107), channel_id=1, source_target_pairs={{0,48},{16,0},{32,16},{48,32},{1,49},{17,1},{33,17},{49,33},{2,50}... | collective-permute-start | bytes 1228808 | tf_op jit(solution)/shard_map/ppermute | solution.py:40
  105.5 20.1 %collective-permute-start.22 = (bf16[2,160,640]{2,1,0:T(8,128)(2,1)S(1)}, bf16[2,160,640]{2,1,0:T(8,128)(2,1)S(1)}, u32[]{:S(2)}, u32[]{:S(2)}) collective-permute-start(bf16[2,160,640]{2,1,0:T(8,128)(2,1)S(1)} %get-tuple-element.99), channel_id=1, source_target_pairs={{0,12},{4,0},{8,4},{12,8},{1,13},{5,1},{9,5},{13,9},{2,14},{6,2},{... | collective-permute-start | bytes 1228808 | tf_op jit(solution)/shard_map/ppermute | solution.py:40
  112.1 16.2 %collective-permute-start.28 = (bf16[2,160,640]{2,1,0:T(8,128)(2,1)S(1)}, bf16[2,160,640]{2,1,0:T(8,128)(2,1)S(1)}, u32[]{:S(2)}, u32[]{:S(2)}) collective-permute-start(bf16[2,160,640]{2,1,0:T(8,128)(2,1)S(1)} %get-tuple-element.109), channel_id=1, source_target_pairs={{0,4},{4,8},{8,12},{12,0},{1,5},{5,9},{9,13},{13,1},{2,6},{6,10},{... | collective-permute-start | bytes 1228808 | tf_op jit(solution)/shard_map/ppermute | solution.py:40
  112.4 21.1 %collective-permute-start.30 = (bf16[2,160,640]{2,1,0:T(8,128)(2,1)S(1)}, bf16[2,160,640]{2,1,0:T(8,128)(2,1)S(1)}, u32[]{:S(2)}, u32[]{:S(2)}) collective-permute-start(bf16[2,160,640]{2,1,0:T(8,128)(2,1)S(1)} %get-tuple-element.112), channel_id=1, source_target_pairs={{0,48},{16,0},{32,16},{48,32},{1,49},{17,1},{33,17},{49,33},{2,50}... | collective-permute-start | bytes 1228808 | tf_op jit(solution)/shard_map/ppermute | solution.py:40
  115.4 9.5 %collective-permute-start.14 = (bf16[160,640]{1,0:T(8,128)(2,1)S(1)}, bf16[160,640]{1,0:T(8,128)(2,1)S(1)}, u32[]{:S(2)}, u32[]{:S(2)}) collective-permute-start(bf16[160,640]{1,0:T(8,128)(2,1)S(1)} %copy-done.36), channel_id=1, source_target_pairs={{0,32},{16,48},{32,0},{48,16},{1,33},{17,49},{33,1},{49,17},{2,34}... | collective-permute-start | bytes 614408 | tf_op jit(solution)/shard_map/ppermute | solution.py:40
  116.5 17.3 %collective-permute-start.32 = (bf16[2,160,640]{2,1,0:T(8,128)(2,1)S(1)}, bf16[2,160,640]{2,1,0:T(8,128)(2,1)S(1)}, u32[]{:S(2)}, u32[]{:S(2)}) collective-permute-start(bf16[2,160,640]{2,1,0:T(8,128)(2,1)S(1)} %get-tuple-element.114), channel_id=1, source_target_pairs={{0,16},{16,32},{32,48},{48,0},{1,17},{17,33},{33,49},{49,1},{2,18}... | collective-permute-start | bytes 1228808 | tf_op jit(solution)/shard_map/ppermute | solution.py:40
  118.4 46.4 %copy-start.10 = (f32[160,640]{1,0:T(8,128)S(1)}, f32[160,640]{1,0:T(8,128)}, u32[]{:S(2)}) copy-start(f32[160,640]{1,0:T(8,128)} %copy-done.9) | copy-start | bytes 1228804
  118.4 46.4 %copy-start.12 = (f32[160,640]{1,0:T(8,128)S(1)}, f32[160,640]{1,0:T(8,128)}, u32[]{:S(2)}) copy-start(f32[160,640]{1,0:T(8,128)} %copy-done.11) | copy-start | bytes 1228804
  124.9 11.6 %collective-permute-start.27 = (bf16[2,160,640]{2,1,0:T(8,128)(2,1)S(1)}, bf16[2,160,640]{2,1,0:T(8,128)(2,1)S(1)}, u32[]{:S(2)}, u32[]{:S(2)}) collective-permute-start(bf16[2,160,640]{2,1,0:T(8,128)(2,1)S(1)} %get-tuple-element.108), channel_id=1, source_target_pairs={{0,4},{4,8},{8,12},{12,0},{1,5},{5,9},{9,13},{13,1},{2,6},{6,10},{... | collective-permute-start | bytes 1228808 | tf_op jit(solution)/shard_map/ppermute | solution.py:40
  125.6 16.0 %collective-permute-start.29 = (bf16[2,160,640]{2,1,0:T(8,128)(2,1)S(1)}, bf16[2,160,640]{2,1,0:T(8,128)(2,1)S(1)}, u32[]{:S(2)}, u32[]{:S(2)}) collective-permute-start(bf16[2,160,640]{2,1,0:T(8,128)(2,1)S(1)} %get-tuple-element.110), channel_id=1, source_target_pairs={{0,12},{4,0},{8,4},{12,8},{1,13},{5,1},{9,5},{13,9},{2,14},{6,2},{... | collective-permute-start | bytes 1228808 | tf_op jit(solution)/shard_map/ppermute | solution.py:40
  128.3 13.3 %collective-permute-start.31 = (bf16[2,160,640]{2,1,0:T(8,128)(2,1)S(1)}, bf16[2,160,640]{2,1,0:T(8,128)(2,1)S(1)}, u32[]{:S(2)}, u32[]{:S(2)}) collective-permute-start(bf16[2,160,640]{2,1,0:T(8,128)(2,1)S(1)} %get-tuple-element.113), channel_id=1, source_target_pairs={{0,16},{16,32},{32,48},{48,0},{1,17},{17,33},{33,49},{49,1},{2,18}... | collective-permute-start | bytes 1228808 | tf_op jit(solution)/shard_map/ppermute | solution.py:40
  133.5 11.7 %collective-permute-start.33 = (bf16[2,160,640]{2,1,0:T(8,128)(2,1)S(1)}, bf16[2,160,640]{2,1,0:T(8,128)(2,1)S(1)}, u32[]{:S(2)}, u32[]{:S(2)}) collective-permute-start(bf16[2,160,640]{2,1,0:T(8,128)(2,1)S(1)} %get-tuple-element.115), channel_id=1, source_target_pairs={{0,48},{16,0},{32,16},{48,32},{1,49},{17,1},{33,17},{49,33},{2,50}... | collective-permute-start | bytes 1228808 | tf_op jit(solution)/shard_map/ppermute | solution.py:40
  133.8 44.6 %collective-permute-start.41 = (bf16[2,3,160,640]{3,2,1,0:T(8,128)(2,1)S(1)}, bf16[2,3,160,640]{3,2,1,0:T(8,128)(2,1)S(1)}, u32[]{:S(2)}, u32[]{:S(2)}) collective-permute-start(bf16[2,3,160,640]{3,2,1,0:T(8,128)(2,1)S(1)} %shard_map.90.here), channel_id=1, source_target_pairs={{0,64},{64,0},{1,65},{65,1},{2,66},{66,2},{3,67},{67,3},{4,68},{68... | collective-permute-start | bytes 3686408 | tf_op jit(solution)/shard_map/ppermute | solution.py:40
  136.5 10.9 %collective-permute-start.15 = (bf16[160,640]{1,0:T(8,128)(2,1)S(1)}, bf16[160,640]{1,0:T(8,128)(2,1)S(1)}, u32[]{:S(2)}, u32[]{:S(2)}) collective-permute-start(bf16[160,640]{1,0:T(8,128)(2,1)S(1)} %copy-done.34), channel_id=1, source_target_pairs={{0,48},{16,0},{32,16},{48,32},{1,49},{17,1},{33,17},{49,33},{2,50}... | collective-permute-start | bytes 614408 | tf_op jit(solution)/shard_map/ppermute | solution.py:40
  141.6 10.0 %collective-permute-start.16 = (bf16[160,640]{1,0:T(8,128)(2,1)S(1)}, bf16[160,640]{1,0:T(8,128)(2,1)S(1)}, u32[]{:S(2)}, u32[]{:S(2)}) collective-permute-start(bf16[160,640]{1,0:T(8,128)(2,1)S(1)} %copy-done.32), channel_id=1, source_target_pairs={{0,4},{4,8},{8,12},{12,0},{1,5},{5,9},{9,13},{13,1},{2,6},{6,10},{... | collective-permute-start | bytes 614408 | tf_op jit(solution)/shard_map/ppermute | solution.py:40
  141.6 10.0 %collective-permute-start.17 = (bf16[160,640]{1,0:T(8,128)(2,1)S(1)}, bf16[160,640]{1,0:T(8,128)(2,1)S(1)}, u32[]{:S(2)}, u32[]{:S(2)}) collective-permute-start(bf16[160,640]{1,0:T(8,128)(2,1)S(1)} %copy-done.30), channel_id=1, source_target_pairs={{0,8},{4,12},{8,0},{12,4},{1,9},{5,13},{9,1},{13,5},{2,10},{6,14},... | collective-permute-start | bytes 614408 | tf_op jit(solution)/shard_map/ppermute | solution.py:40
  145.2 9.1 %collective-permute-start.18 = (bf16[160,640]{1,0:T(8,128)(2,1)S(1)}, bf16[160,640]{1,0:T(8,128)(2,1)S(1)}, u32[]{:S(2)}, u32[]{:S(2)}) collective-permute-start(bf16[160,640]{1,0:T(8,128)(2,1)S(1)} %copy-done.28), channel_id=1, source_target_pairs={{0,12},{4,0},{8,4},{12,8},{1,13},{5,1},{9,5},{13,9},{2,14},{6,2},{... | collective-permute-start | bytes 614408 | tf_op jit(solution)/shard_map/ppermute | solution.py:40
  147.4 9.5 %collective-permute-start.13 = (bf16[160,640]{1,0:T(8,128)(2,1)S(1)}, bf16[160,640]{1,0:T(8,128)(2,1)S(1)}, u32[]{:S(2)}, u32[]{:S(2)}) collective-permute-start(bf16[160,640]{1,0:T(8,128)(2,1)S(1)} %copy-done.26), channel_id=1, source_target_pairs={{0,16},{16,32},{32,48},{48,0},{1,17},{17,33},{33,49},{49,1},{2,18}... | collective-permute-start | bytes 614408 | tf_op jit(solution)/shard_map/ppermute | solution.py:40
  151.6 11.5 %collective-permute-start.34 = (bf16[160,640]{1,0:T(8,128)(2,1)S(1)}, bf16[160,640]{1,0:T(8,128)(2,1)S(1)}, u32[]{:S(2)}, u32[]{:S(2)}) collective-permute-start(bf16[160,640]{1,0:T(8,128)(2,1)S(1)} %get-tuple-element.117), channel_id=1, source_target_pairs={{0,16},{16,32},{32,48},{48,0},{1,17},{17,33},{33,49},{49,1},{2,18}... | collective-permute-start | bytes 614408 | tf_op jit(solution)/shard_map/ppermute | solution.py:40
  151.7 11.5 %collective-permute-start.35 = (bf16[160,640]{1,0:T(8,128)(2,1)S(1)}, bf16[160,640]{1,0:T(8,128)(2,1)S(1)}, u32[]{:S(2)}, u32[]{:S(2)}) collective-permute-start(bf16[160,640]{1,0:T(8,128)(2,1)S(1)} %get-tuple-element.118), channel_id=1, source_target_pairs={{0,32},{16,48},{32,0},{48,16},{1,33},{17,49},{33,1},{49,17},{2,34}... | collective-permute-start | bytes 614408 | tf_op jit(solution)/shard_map/ppermute | solution.py:40
  154.3 11.2 %collective-permute-start.36 = (bf16[160,640]{1,0:T(8,128)(2,1)S(1)}, bf16[160,640]{1,0:T(8,128)(2,1)S(1)}, u32[]{:S(2)}, u32[]{:S(2)}) collective-permute-start(bf16[160,640]{1,0:T(8,128)(2,1)S(1)} %get-tuple-element.119), channel_id=1, source_target_pairs={{0,48},{16,0},{32,16},{48,32},{1,49},{17,1},{33,17},{49,33},{2,50}... | collective-permute-start | bytes 614408 | tf_op jit(solution)/shard_map/ppermute | solution.py:40
  156.9 11.5 %collective-permute-start.37 = (bf16[160,640]{1,0:T(8,128)(2,1)S(1)}, bf16[160,640]{1,0:T(8,128)(2,1)S(1)}, u32[]{:S(2)}, u32[]{:S(2)}) collective-permute-start(bf16[160,640]{1,0:T(8,128)(2,1)S(1)} %get-tuple-element.121), channel_id=1, source_target_pairs={{0,4},{4,8},{8,12},{12,0},{1,5},{5,9},{9,13},{13,1},{2,6},{6,10},{... | collective-permute-start | bytes 614408 | tf_op jit(solution)/shard_map/ppermute | solution.py:40
  163.2 7.3 %collective-permute-start.38 = (bf16[160,640]{1,0:T(8,128)(2,1)S(1)}, bf16[160,640]{1,0:T(8,128)(2,1)S(1)}, u32[]{:S(2)}, u32[]{:S(2)}) collective-permute-start(bf16[160,640]{1,0:T(8,128)(2,1)S(1)} %get-tuple-element.122), channel_id=1, source_target_pairs={{0,8},{4,12},{8,0},{12,4},{1,9},{5,13},{9,1},{13,5},{2,10},{6,14},... | collective-permute-start | bytes 614408 | tf_op jit(solution)/shard_map/ppermute | solution.py:40
  163.2 7.3 %collective-permute-start.39 = (bf16[160,640]{1,0:T(8,128)(2,1)S(1)}, bf16[160,640]{1,0:T(8,128)(2,1)S(1)}, u32[]{:S(2)}, u32[]{:S(2)}) collective-permute-start(bf16[160,640]{1,0:T(8,128)(2,1)S(1)} %get-tuple-element.123), channel_id=1, source_target_pairs={{0,12},{4,0},{8,4},{12,8},{1,13},{5,1},{9,5},{13,9},{2,14},{6,2},{... | collective-permute-start | bytes 614408 | tf_op jit(solution)/shard_map/ppermute | solution.py:40
  165.5 12.8 %collective-permute-start.19 = (bf16[160,1280]{1,0:T(8,128)(2,1)S(1)}, bf16[160,1280]{1,0:T(8,128)(2,1)S(1)}, u32[]{:S(2)}, u32[]{:S(2)}) collective-permute-start(bf16[160,1280]{1,0:T(8,128)(2,1)S(1)} %shard_map.89.near), channel_id=1, source_target_pairs={{0,64},{64,0},{1,65},{65,1},{2,66},{66,2},{3,67},{67,3},{4,68},{68... | collective-permute-start | bytes 1228808 | tf_op jit(solution)/shard_map/ppermute | solution.py:40
  171.2 13.4 %collective-permute-start.40 = (bf16[160,1280]{1,0:T(8,128)(2,1)S(1)}, bf16[160,1280]{1,0:T(8,128)(2,1)S(1)}, u32[]{:S(2)}, u32[]{:S(2)}) collective-permute-start(bf16[160,1280]{1,0:T(8,128)(2,1)S(1)} %shard_map.95.far), channel_id=1, source_target_pairs={{0,64},{64,0},{1,65},{65,1},{2,66},{66,2},{3,67},{67,3},{4,68},{68... | collective-permute-start | bytes 1228808 | tf_op jit(solution)/shard_map/ppermute | solution.py:40
  189.2 12.3 %collective-permute-start.44 = (bf16[2,160,640]{2,1,0:T(8,128)(2,1)S(1)}, bf16[2,160,640]{2,1,0:T(8,128)(2,1)S(1)}, u32[]{:S(2)}, u32[]{:S(2)}) collective-permute-start(bf16[2,160,640]{2,1,0:T(8,128)(2,1)S(1)} %get-tuple-element.128.refs_0_), channel_id=1, source_target_pairs={{0,48},{16,0},{32,16},{48,32},{1,49},{17,1},{33,17},{49,33},{2,50}... | collective-permute-start | bytes 1228808 | tf_op jit(solution)/shard_map/ppermute | solution.py:40
  191.4 13.9 %collective-permute-start.43 = (bf16[2,160,640]{2,1,0:T(8,128)(2,1)S(1)}, bf16[2,160,640]{2,1,0:T(8,128)(2,1)S(1)}, u32[]{:S(2)}, u32[]{:S(2)}) collective-permute-start(bf16[2,160,640]{2,1,0:T(8,128)(2,1)S(1)} %get-tuple-element.128.refs_0_), channel_id=1, source_target_pairs={{0,32},{16,48},{32,0},{48,16},{1,33},{17,49},{33,1},{49,17},{2,34}... | collective-permute-start | bytes 1228808 | tf_op jit(solution)/shard_map/ppermute | solution.py:40
  193.2 17.7 %collective-permute-start.42 = (bf16[2,160,640]{2,1,0:T(8,128)(2,1)S(1)}, bf16[2,160,640]{2,1,0:T(8,128)(2,1)S(1)}, u32[]{:S(2)}, u32[]{:S(2)}) collective-permute-start(bf16[2,160,640]{2,1,0:T(8,128)(2,1)S(1)} %get-tuple-element.128.refs_0_), channel_id=1, source_target_pairs={{0,16},{16,32},{32,48},{48,0},{1,17},{17,33},{33,49},{49,1},{2,18}... | collective-permute-start | bytes 1228808 | tf_op jit(solution)/shard_map/ppermute | solution.py:40
  193.2 17.7 %collective-permute-start.47 = (bf16[2,160,640]{2,1,0:T(8,128)(2,1)S(1)}, bf16[2,160,640]{2,1,0:T(8,128)(2,1)S(1)}, u32[]{:S(2)}, u32[]{:S(2)}) collective-permute-start(bf16[2,160,640]{2,1,0:T(8,128)(2,1)S(1)} %get-tuple-element.129.refs_4_), channel_id=1, source_target_pairs={{0,12},{4,0},{8,4},{12,8},{1,13},{5,1},{9,5},{13,9},{2,14},{6,2},{... | collective-permute-start | bytes 1228808 | tf_op jit(solution)/shard_map/ppermute | solution.py:40
  193.2 17.7 %collective-permute-start.46 = (bf16[2,160,640]{2,1,0:T(8,128)(2,1)S(1)}, bf16[2,160,640]{2,1,0:T(8,128)(2,1)S(1)}, u32[]{:S(2)}, u32[]{:S(2)}) collective-permute-start(bf16[2,160,640]{2,1,0:T(8,128)(2,1)S(1)} %get-tuple-element.129.refs_4_), channel_id=1, source_target_pairs={{0,8},{4,12},{8,0},{12,4},{1,9},{5,13},{9,1},{13,5},{2,10},{6,14},... | collective-permute-start | bytes 1228808 | tf_op jit(solution)/shard_map/ppermute | solution.py:40
  201.5 11.5 %collective-permute-start.45 = (bf16[2,160,640]{2,1,0:T(8,128)(2,1)S(1)}, bf16[2,160,640]{2,1,0:T(8,128)(2,1)S(1)}, u32[]{:S(2)}, u32[]{:S(2)}) collective-permute-start(bf16[2,160,640]{2,1,0:T(8,128)(2,1)S(1)} %get-tuple-element.129.refs_4_), channel_id=1, source_target_pairs={{0,4},{4,8},{8,12},{12,0},{1,5},{5,9},{9,13},{13,1},{2,6},{6,10},{... | collective-permute-start | bytes 1228808 | tf_op jit(solution)/shard_map/ppermute | solution.py:40
  213.9 21.2 %collective-permute-start.57 = (bf16[2,2,160,640]{3,2,1,0:T(8,128)(2,1)S(1)}, bf16[2,2,160,640]{3,2,1,0:T(8,128)(2,1)S(1)}, u32[]{:S(2)}, u32[]{:S(2)}) collective-permute-start(bf16[2,2,160,640]{3,2,1,0:T(8,128)(2,1)S(1)} %get-tuple-element.130.refs_0_), channel_id=1, source_target_pairs={{0,12},{4,0},{8,4},{12,8},{1,13},{5,1},{9,5},{13,9},{2,14},{6,2},{... | collective-permute-start | bytes 2457608 | tf_op jit(solution)/shard_map/ppermute | solution.py:40
  215.2 25.5 %collective-permute-start.48 = (bf16[2,2,160,640]{3,2,1,0:T(8,128)(2,1)S(1)}, bf16[2,2,160,640]{3,2,1,0:T(8,128)(2,1)S(1)}, u32[]{:S(2)}, u32[]{:S(2)}) collective-permute-start(bf16[2,2,160,640]{3,2,1,0:T(8,128)(2,1)S(1)} %get-tuple-element.130.refs_0_), channel_id=1, source_target_pairs={{0,4},{4,8},{8,12},{12,0},{1,5},{5,9},{9,13},{13,1},{2,6},{6,10},{... | collective-permute-start | bytes 2457608 | tf_op jit(solution)/shard_map/ppermute | solution.py:40
  216.0 35.1 %collective-permute-start.56 = (bf16[2,2,160,640]{3,2,1,0:T(8,128)(2,1)S(1)}, bf16[2,2,160,640]{3,2,1,0:T(8,128)(2,1)S(1)}, u32[]{:S(2)}, u32[]{:S(2)}) collective-permute-start(bf16[2,2,160,640]{3,2,1,0:T(8,128)(2,1)S(1)} %get-tuple-element.131.refs_1_), channel_id=1, source_target_pairs={{0,4},{4,8},{8,12},{12,0},{1,5},{5,9},{9,13},{13,1},{2,6},{6,10},{... | collective-permute-start | bytes 2457608 | tf_op jit(solution)/shard_map/ppermute | solution.py:40
  216.0 41.4 %collective-permute-start.50 = (bf16[2,2,160,640]{3,2,1,0:T(8,128)(2,1)S(1)}, bf16[2,2,160,640]{3,2,1,0:T(8,128)(2,1)S(1)}, u32[]{:S(2)}, u32[]{:S(2)}) collective-permute-start(bf16[2,2,160,640]{3,2,1,0:T(8,128)(2,1)S(1)} %get-tuple-element.131.refs_1_), channel_id=1, source_target_pairs={{0,12},{4,0},{8,4},{12,8},{1,13},{5,1},{9,5},{13,9},{2,14},{6,2},{... | collective-permute-start | bytes 2457608 | tf_op jit(solution)/shard_map/ppermute | solution.py:40
  219.3 38.2 %collective-permute-start.59 = (bf16[2,2,160,640]{3,2,1,0:T(8,128)(2,1)S(1)}, bf16[2,2,160,640]{3,2,1,0:T(8,128)(2,1)S(1)}, u32[]{:S(2)}, u32[]{:S(2)}) collective-permute-start(bf16[2,2,160,640]{3,2,1,0:T(8,128)(2,1)S(1)} %get-tuple-element.132.refs_6_), channel_id=1, source_target_pairs={{0,48},{16,0},{32,16},{48,32},{1,49},{17,1},{33,17},{49,33},{2,50}... | collective-permute-start | bytes 2457608 | tf_op jit(solution)/shard_map/ppermute | solution.py:40
  235.1 25.6 %collective-permute-start.52 = (bf16[2,2,160,640]{3,2,1,0:T(8,128)(2,1)S(1)}, bf16[2,2,160,640]{3,2,1,0:T(8,128)(2,1)S(1)}, u32[]{:S(2)}, u32[]{:S(2)}) collective-permute-start(bf16[2,2,160,640]{3,2,1,0:T(8,128)(2,1)S(1)} %get-tuple-element.132.refs_6_), channel_id=1, source_target_pairs={{0,16},{16,32},{32,48},{48,0},{1,17},{17,33},{33,49},{49,1},{2,18}... | collective-permute-start | bytes 2457608 | tf_op jit(solution)/shard_map/ppermute | solution.py:40
  240.7 20.0 %collective-permute-start.54 = (bf16[2,2,160,640]{3,2,1,0:T(8,128)(2,1)S(1)}, bf16[2,2,160,640]{3,2,1,0:T(8,128)(2,1)S(1)}, u32[]{:S(2)}, u32[]{:S(2)}) collective-permute-start(bf16[2,2,160,640]{3,2,1,0:T(8,128)(2,1)S(1)} %get-tuple-element.133.refs_7_), channel_id=1, source_target_pairs={{0,48},{16,0},{32,16},{48,32},{1,49},{17,1},{33,17},{49,33},{2,50}... | collective-permute-start | bytes 2457608 | tf_op jit(solution)/shard_map/ppermute | solution.py:40
  251.1 24.9 %collective-permute-start.58 = (bf16[2,2,160,640]{3,2,1,0:T(8,128)(2,1)S(1)}, bf16[2,2,160,640]{3,2,1,0:T(8,128)(2,1)S(1)}, u32[]{:S(2)}, u32[]{:S(2)}) collective-permute-start(bf16[2,2,160,640]{3,2,1,0:T(8,128)(2,1)S(1)} %get-tuple-element.133.refs_7_), channel_id=1, source_target_pairs={{0,16},{16,32},{32,48},{48,0},{1,17},{17,33},{33,49},{49,1},{2,18}... | collective-permute-start | bytes 2457608 | tf_op jit(solution)/shard_map/ppermute | solution.py:40
  257.4 23.0 %collective-permute-start.49 = (bf16[2,2,160,640]{3,2,1,0:T(8,128)(2,1)S(1)}, bf16[2,2,160,640]{3,2,1,0:T(8,128)(2,1)S(1)}, u32[]{:S(2)}, u32[]{:S(2)}) collective-permute-start(bf16[2,2,160,640]{3,2,1,0:T(8,128)(2,1)S(1)} %collective-permute-done.48.refs_2_), channel_id=1, source_target_pairs={{0,4},{4,8},{8,12},{12,0},{1,5},{5,9},{9,13},{13,1},{2,6},{6,10},{... | collective-permute-start | bytes 2457608 | tf_op jit(solution)/shard_map/ppermute | solution.py:40
  257.4 23.0 %collective-permute-start.51 = (bf16[2,2,160,640]{3,2,1,0:T(8,128)(2,1)S(1)}, bf16[2,2,160,640]{3,2,1,0:T(8,128)(2,1)S(1)}, u32[]{:S(2)}, u32[]{:S(2)}) collective-permute-start(bf16[2,2,160,640]{3,2,1,0:T(8,128)(2,1)S(1)} %collective-permute-done.50.refs_3_), channel_id=1, source_target_pairs={{0,12},{4,0},{8,4},{12,8},{1,13},{5,1},{9,5},{13,9},{2,14},{6,2},{... | collective-permute-start | bytes 2457608 | tf_op jit(solution)/shard_map/ppermute | solution.py:40
  260.7 25.5 %collective-permute-start.53 = (bf16[2,2,160,640]{3,2,1,0:T(8,128)(2,1)S(1)}, bf16[2,2,160,640]{3,2,1,0:T(8,128)(2,1)S(1)}, u32[]{:S(2)}, u32[]{:S(2)}) collective-permute-start(bf16[2,2,160,640]{3,2,1,0:T(8,128)(2,1)S(1)} %collective-permute-done.52.refs_8_), channel_id=1, source_target_pairs={{0,16},{16,32},{32,48},{48,0},{1,17},{17,33},{33,49},{49,1},{2,18}... | collective-permute-start | bytes 2457608 | tf_op jit(solution)/shard_map/ppermute | solution.py:40
  260.7 25.5 %collective-permute-start.55 = (bf16[2,2,160,640]{3,2,1,0:T(8,128)(2,1)S(1)}, bf16[2,2,160,640]{3,2,1,0:T(8,128)(2,1)S(1)}, u32[]{:S(2)}, u32[]{:S(2)}) collective-permute-start(bf16[2,2,160,640]{3,2,1,0:T(8,128)(2,1)S(1)} %collective-permute-done.54.refs_9_), channel_id=1, source_target_pairs={{0,48},{16,0},{32,16},{48,32},{1,49},{17,1},{33,17},{49,33},{2,50}... | collective-permute-start | bytes 2457608 | tf_op jit(solution)/shard_map/ppermute | solution.py:40
  (34 other events, 249.9 us)
where the time goes:
time: 289 us
  waiting for transfers between devices  112 us (39%)
  starting transfers between devices  108 us (37%)
  Pallas kernels  45.6 us (16%)
  local copies, waits for them, and re-layouts  21.3 us (7%)
    ppermute x60, waiting for transfers between devices, shift(): lax.ppermute(value, axis, [(i, (i + step) % count) for i in range(count)])  112 us
    ppermute x60, starting transfers between devices, shift(): lax.ppermute(value, axis, [(i, (i + step) % count) for i in range(count)])  103 us
    pallas_call x16, Pallas kernels, call(): pl.pallas_call(kernel, out_shape=outs, in_specs=[pl.BlockSpec(memory_spac...  45.6 us
    unnamed x74, local copies, waits for them, and re-layouts  21.2 us
  transfers between devices with their start and end apart: 61, of which 24 were waited for; matrix products, arithmetic and copies ran while one was open for 0% of the time, Pallas kernels for 11%

commit v1 on v0

v1 whole, which is shorter than its diff:
```python
import functools

import jax
import jax.numpy as jnp
from jax import lax
from jax.experimental import pallas as pl
from jax.experimental.pallas import tpu as pltpu
from jax.sharding import Mesh, PartitionSpec as P

STEP = 20


beta_one = 0.9
beta_two = 0.95
adam_eps = 1e-08
learn_rate = 0.0003
decay_rate = 0.1

D = 5120
ROWS = 160
COLS = 1280
PART = 640
FSDP = ("xh", "z", "y")
VMEM_LIMIT = 12 * 1024 * 1024

XH, Z, Y, XL, CORE, FIRST, SECOND = range(7)


def f32(value):
    return value.astype(jnp.float32)


def bf16(value):
    return value.astype(jnp.bfloat16)


def shift(value, axis, step):
    count = lax.axis_size(axis)
    return lax.ppermute(value, axis, [(i, (i + step) % count) for i in range(count)])


def ring(value, second, step):
    pairs = []
    for z in range(4):
        for y in range(4):
            for core in range(2):
                along_y = core == second
                to = (z, (y + step) % 4) if along_y else ((z + step) % 4, y)
                pairs.append(((z * 4 + y) * 2 + core, (to[0] * 4 + to[1]) * 2 + core))
    return lax.ppermute(value, ("z", "y", "c"), pairs)


def shape(*dims, dtype=jnp.bfloat16):
    return jax.ShapeDtypeStruct(dims, dtype)


def call(kernel, place, args, outs, scratch=(), out_spaces=None, aliased=0):
    vmem = pl.BlockSpec(memory_space=pltpu.VMEM)
    there = [pl.BlockSpec(memory_space=space) for space in out_spaces or (pltpu.VMEM,) * len(outs)]
    held = len(args) - aliased
    return pl.pallas_call(
        kernel,
        out_shape=outs,
        in_specs=[pl.BlockSpec(memory_space=pltpu.SMEM)] + [vmem] * held + there[:aliased],
        out_specs=there,
        scratch_shapes=scratch,
        input_output_aliases={1 + held + i: i for i in range(aliased)},
        compiler_params=pltpu.CompilerParams(vmem_limit_bytes=VMEM_LIMIT),
    )(place, *args)


def in_rows(step):
    def run(i, carry):
        step(pl.ds(pl.multiple_of(i * 32, 32), 32))
        return carry

    lax.fori_loop(0, ROWS // 32, run, 0)


def multiply(features, cotangent, blocks):
    def one(low_z, carry):
        result = lax.dot_general(
            features[:, pl.ds(pl.multiple_of(low_z * 640, 128), 640)],
            cotangent[...],
            (((0,), (0,)), ((), ())),
            preferred_element_type=jnp.float32,
        )
        for j in range(4):
            blocks[low_z, j] = bf16(result[j * ROWS : (j + 1) * ROWS])
        return carry

    lax.fori_loop(0, 2, one, 0)


def first_product_kernel(place, features, cotangent, made):
    multiply(features, cotangent, made)


def product_kernel(place, made, features, cotangent, *refs):
    far_up, far_down, hold_up, hold_down, own, near_up, near_down, blocks, sems = refs
    multiply(features, cotangent, blocks)

    def send(value, ref, k):
        pltpu.make_async_copy(value, ref, sems.at[k]).start()

    def over_y(values, owner, low_z):
        def y_block(steps):
            return values.at[low_z, lax.rem(place[Y] + steps, 4)]

        send(y_block(0), own.at[2 * owner + low_z], 0)
        if owner == 0:
            send(y_block(3), near_down.at[low_z], 2)
            far_up[low_z] = y_block(2)[...]
            hold_up[low_z] = y_block(1)[...]
        else:
            send(y_block(1), near_up.at[low_z], 1)
            far_down[low_z] = y_block(2)[...]
            hold_down[low_z] = y_block(3)[...]

    def over_z(values, owner, low_z):
        ahead = lax.rem(2 * owner + low_z + 4 - place[Z], 4)

        @pl.when(ahead == 0)
        def _():
            send(values.at[low_z], own, 0)

        @pl.when(ahead == 1)
        def _():
            send(values.at[low_z, pl.ds(2, 2)], near_up, 1)
            hold_up[...] = values[low_z, :2]

        @pl.when(ahead == 2)
        def _():
            far_up[...] = values[low_z, :2]
            far_down[...] = values[low_z, 2:]

        @pl.when(ahead == 3)
        def _():
            send(values.at[low_z, pl.ds(0, 2)], near_down, 2)
            hold_down[...] = values[low_z, 2:]

    for core, arrange in ((0, over_y), (1, over_z)):

        @pl.when(place[CORE] == core)
        def _():
            for low_z in range(2):
                arrange(made, core, low_z)
                arrange(blocks, 1 - core, low_z)

    pltpu.make_async_copy(blocks.at[0], own, sems.at[0]).wait()
    pltpu.make_async_copy(blocks.at[0, pl.ds(0, 2)], near_up, sems.at[1]).wait()
    pltpu.make_async_copy(blocks.at[0, pl.ds(0, 2)], near_down, sems.at[2]).wait()


def products(place, cotangent, mine, other):
    made = call(first_product_kernel, place, (mine, cotangent), [shape(2, 4, ROWS, COLS)])[0]
    return call(
        product_kernel,
        place,
        (made, other, cotangent),
        [shape(n, ROWS, COLS) for n in (2, 2, 2, 2, 4, 2, 2)],
        [pltpu.VMEM((2, 4, ROWS, COLS), jnp.bfloat16), pltpu.SemaphoreType.DMA((3,))],
        (pltpu.VMEM,) * 4 + (pltpu.HBM,) * 3,
    )


def add_kernel(place, *refs):
    def step(rows):
        for k in range(2):
            for j in range(2):
                refs[4 + k][j, rows] = bf16(f32(refs[2 * k][j, rows]) + f32(refs[2 * k + 1][j, rows]))

    in_rows(step)


def pass_on(place, *blocks):
    return call(add_kernel, place, blocks, [shape(2, ROWS, COLS)] * 2)


def finish_kernel(place, own, near_down, last_up, near_up, last_down, *outs):
    def step(rows):
        for steps in range(4):
            to = lax.rem(place[SECOND] + steps, 4)
            first, second = jnp.minimum(to, 1), jnp.maximum(to - 2, 0)
            near = jnp.where(to < 2, f32(near_down[first, rows]), f32(near_up[second, rows]))
            last = jnp.where(to < 2, f32(last_up[first, rows]), f32(last_down[second, rows]))
            value = f32(own[to, rows]) + near + last
            outs[steps][rows] = value.astype(outs[steps].dtype)

    in_rows(step)


def finish(place, *blocks):
    kinds = (jnp.float32, jnp.bfloat16, jnp.bfloat16, jnp.bfloat16)
    return call(finish_kernel, place, blocks, [shape(ROWS, COLS, dtype=k) for k in kinds])


def total_kernel(place, keep, one, two, three, out):
    def step(rows):
        out[rows] = bf16(keep[rows] + f32(one[rows]) + f32(two[rows]) + f32(three[rows]))

    in_rows(step)


def reduced(place, messages):
    far_up, far_down, hold_up, hold_down, own, near_up, near_down = messages
    far_up, far_down = ring(far_up, 0, 1), ring(far_down, 0, -1)
    near_up, near_down = ring(near_up, 0, 1), ring(near_down, 0, -1)
    last_up, last_down = pass_on(place, hold_up, far_up, hold_down, far_down)
    last_up, last_down = ring(last_up, 0, 1), ring(last_down, 0, -1)
    keep, *sent = finish(place, own, near_down, last_up, near_up, last_down)
    got = [ring(block, 1, k + 1) for k, block in enumerate(sent)]
    return call(total_kernel, place, (keep, *got), [shape(ROWS, COLS)])[0], sent[0]


def adam_update(weights, first_moment, second_moment, gradient):
    first_new = beta_one * first_moment + (1.0 - beta_one) * gradient
    second_new = beta_two * second_moment + (1.0 - beta_two) * gradient * gradient
    corrected = first_new * (1.0 / (1.0 - beta_one**STEP))
    scaled = jnp.sqrt(second_new * (1.0 / (1.0 - beta_two**STEP))) + adam_eps
    weights_new = weights - learn_rate * (corrected / scaled + decay_rate * weights)
    return (weights_new, first_new, second_new)


def adam_kernel(place, near, near_got, far, far_got, here, there, weights, first, second, *both):
    def step(rows):
        for half in range(2):
            is_near = half == place[XL]
            gradient = f32(jnp.where(is_near, f32(near[rows]), f32(far[rows]))) + jnp.where(
                is_near, f32(near_got[rows]), f32(far_got[rows])
            )
            for s in range(2):
                old = [
                    jnp.where(place[XH] == s, f32(here[half, k, rows]), f32(there[half, k, rows])) for k in range(3)
                ]
                columns = slice(s * PART, (s + 1) * PART)
                new = adam_update(*old, gradient[:, columns])
                both[half][rows, columns] = bf16(new[0])

                @pl.when(half == place[XH])
                def _():
                    for ref, value in zip((weights, first, second), new):
                        ref[rows, columns] = value

    in_rows(step)


def adam(place, gradients, here, there):
    return call(
        adam_kernel,
        place,
        (*gradients, here, there),
        [shape(ROWS, COLS, dtype=jnp.float32)] * 3 + [shape(ROWS, COLS)] * 2,
    )


def line_kernel(place, *refs):
    low, high = refs[8:]
    for ahead in range(4):
        source = lax.rem(place[SECOND] + ahead, 4)

        @pl.when(source < 2)
        def _():
            for x in range(2):
                low[x, source] = refs[2 * ahead + x][...]

        @pl.when(source >= 2)
        def _():
            for x in range(2):
                high[x, source - 2] = refs[2 * ahead + x][...]


def lay_kernel(steps, place, *refs):
    out, sems = refs[-2], refs[-1]

    def copy(k, along_y):
        half, ahead = steps[k]
        other, pair = lax.rem(place[FIRST] + ahead, 4), pl.ds(2 * half, 2)
        index = (slice(None), pair, other) if along_y else (slice(None), other, pair)
        return pltpu.make_async_copy(refs[k], out.at[index], sems.at[k])

    for core in range(2):

        @pl.when(place[CORE] == core)
        def _():
            for k in range(len(steps)):
                copy(k, core == 0).start()
            for k in range(len(steps)):
                copy(k, core == 0).wait()


def lay(place, steps, pieces, *out):
    return call(
        functools.partial(lay_kernel, steps),
        place,
        [*pieces, *out],
        [shape(2, 4, 4, ROWS, COLS)],
        [pltpu.SemaphoreType.DMA((len(pieces),))],
        (pltpu.HBM,),
        len(out),
    )[0]


def gather_ring(low, high, second):
    low_up, high_down = ring(low, second, 1), ring(high, second, -1)
    high_up, low_down = ring(high, second, 1), ring(low, second, -1)
    far_up, far_down = ring(low_up, second, 1), ring(high_down, second, -1)
    return low_down, high_down, far_up, far_down, low_up, high_up


def gathered(place, both):
    blocks = (*both, *gather_ring(*both, 1))
    low, high = call(line_kernel, place, blocks, [shape(2, 2, ROWS, COLS)] * 2)
    low_down, high_down, far_up, far_down, low_up, high_up = gather_ring(low, high, 0)
    steps = ((0, 0), (1, 0), (0, 3), (1, 1), (1, 3), (0, 1))
    out = lay(place, steps, (low, high, low_up, high_down, high_up, low_down))
    return lay(place, ((0, 2), (1, 2)), (far_up, far_down), out)


def state_kernel(place, got, out, turned):
    def half(h, carry):
        for source in range(16):
            turned[source * 40 : (source + 1) * 40, :480] = f32(got[source, h])
        flat = turned[...].T
        for k in range(3):
            out[h, k] = bf16(flat[k * ROWS : (k + 1) * ROWS])
        return carry

    turned[:, 480:] = jnp.zeros((PART, 32), jnp.float32)
    lax.fori_loop(0, 2, half, 0)


def send_kernel(place, *refs):
    states, out = refs[:3], refs[3]

    def four(g, carry):
        for j in range(4):
            block = 4 * g + j
            for k, state in enumerate(states):
                rows = state[:, pl.ds(pl.multiple_of(g * 640, 128), 640)]
                out[lax.rem(block, 16), lax.div(block, 16), :, k * ROWS : (k + 1) * ROWS] = bf16(
                    rows[:, j * ROWS : (j + 1) * ROWS]
                )
        return carry

    lax.fori_loop(0, 8, four, 0)


def sent_state(place, states):
    return call(send_kernel, place, [s.T for s in states], [shape(16, 2, 40, 3 * ROWS)])[0]


def moved_state(place, flat):
    got = lax.all_to_all(flat, ("z", "y"), 0, 0, tiled=True)
    return call(
        state_kernel, place, (got,), [shape(2, 3, ROWS, PART)], [pltpu.VMEM((PART, 512), jnp.float32)]
    )[0]


def step(activations, cotangent, weights, first_moment, second_moment):
    place = [lax.axis_index(a) for a in ("xh", "z", "y", "xl", "c")]
    swapped = place[CORE] == 1
    place += [jnp.where(swapped, place[Z], place[Y]), jnp.where(swapped, place[Y], place[Z])]
    place = jnp.stack(place).astype(jnp.int32)
    across = shift(activations, "xl", 1)
    beside = shift(activations, "c", 1)
    flat = sent_state(place, (weights, first_moment, second_moment))
    here = moved_state(place, flat)
    messages = products(place, cotangent, activations, beside)
    near, sent = reduced(place, messages)

    across, here, _ = lax.optimization_barrier((across, here, sent))
    there = shift(here, "xh", 1)
    messages = products(place, cotangent, across, shift(across, "c", 1))
    near_got = shift(near, "xh", 1)
    far, _ = reduced(place, messages)
    far_got = shift(far, "xh", 1)
    weights_new, first_new, second_new, *both = adam(place, (near, near_got, far, far_got), here, there)
    out = gathered(place, both)
    return (weights_new, first_new, second_new, out.reshape(D, COLS))


def solution(mesh):
    wide = Mesh(mesh.devices.reshape(2, 4, 4, 2, 2), ("xh", "z", "y", "xl", "c"))
    tensor = ("xl", "c")
    columns = P(None, (*tensor, *FSDP))
    rows = P(FSDP, tensor)
    return jax.shard_map(
        step,
        mesh=wide,
        in_specs=(rows, rows, columns, columns, columns),
        out_specs=(rows, rows, rows, P(None, tensor)),
        check_vma=False,
    )
```

time: 289 us -> 244 us (0.84)
  starting transfers between devices: 108 us -> 69.3 us
  local copies, waits for them, and re-layouts: 21.3 us -> 11.8 us
  Pallas kernels: 45.6 us -> 50.7 us
    ppermute x60 -> x6, waiting for transfers between devices: 112 us -> 10.6 us  [shift(): lax.ppermute(value, axis, [(i, (i + step) % count) for i in range(count)])]
    ppermute x0 -> x30, waiting for transfers between devices: none -> 96.8 us  [ring(): return lax.ppermute(value, ('z', 'y', 'c'), pairs)]
    ppermute x60 -> x6, starting transfers between devices: 103 us -> 10.7 us  [shift(): lax.ppermute(value, axis, [(i, (i + step) % count) for i in range(count)])]
    ppermute x0 -> x30, starting transfers between devices: none -> 51.7 us  [ring(): return lax.ppermute(value, ('z', 'y', 'c'), pairs)]
    unnamed x74 -> x30, local copies, waits for them, and re-layouts: 21.2 us -> 11.7 us
    pallas_call x16, Pallas kernels: 45.6 us -> 50.7 us  [call(): pl.pallas_call(kernel, out_shape=outs, in_specs=[pl.BlockSpec(memory_spac...]
    all_to_all x1, waiting for transfers between devices: 0.01 us -> 3.14 us  [moved_state(): got = lax.all_to_all(flat, ('z', 'y'), 0, 0, tiled=True)]
  transfers between devices with their start and end apart: 61 -> 37, of which waited for: 24 -> 20; matrix products, arithmetic and copies ran while one was open for 0% -> 0% of each run, Pallas kernels for 11% -> 15%
where the time goes in v1:
time: 244 us; the launch traced here: 243 us
  waiting for transfers between devices  110 us (45%)
  starting transfers between devices  69.3 us (28%)
  Pallas kernels  50.7 us (21%)
  local copies, waits for them, and re-layouts  11.8 us (5%)
    ppermute x30, waiting for transfers between devices, ring(): return lax.ppermute(value, ('z', 'y', 'c'), pairs)  96.8 us
    ppermute x30, starting transfers between devices, ring(): return lax.ppermute(value, ('z', 'y', 'c'), pairs)  51.7 us
    pallas_call x16, Pallas kernels, call(): pl.pallas_call(kernel, out_shape=outs, in_specs=[pl.BlockSpec(memory_spac...  50.7 us
    unnamed x30, local copies, waits for them, and re-layouts  11.7 us
    ppermute x6, starting transfers between devices, shift(): lax.ppermute(value, axis, [(i, (i + step) % count) for i in range(count)])  10.7 us
    ppermute x6, waiting for transfers between devices, shift(): lax.ppermute(value, axis, [(i, (i + step) % count) for i in range(count)])  10.6 us
    all_to_all x1, starting transfers between devices, moved_state(): got = lax.all_to_all(flat, ('z', 'y'), 0, 0, tiled=True)  6.88 us
  transfers between devices with their start and end apart: 37, of which 20 were waited for; matrix products, arithmetic and copies ran while one was open for 0% of the time, Pallas kernels for 15%

profile of v1, /device:TPU:0, one launch (start us, length us, event | category | flops | bytes accessed | tf_op | source)
XLA Modules:
  0.0 243.3 jit_solution(10241879137230119811)
XLA Ops:
  0.7 1.7 collective-permute-start.11
  2.5 1.7 copy-done
  4.2 1.7 copy-done.3
  6.0 4.4 %shard_map.84.made = bf16[2,4,160,1280]{3,2,1,0:T(8,128)(2,1)S(1)} custom-call(s32[7]{0:T(128)S(1)} %stack.31.place, bf16[1024,1280]{1,0:T(8,128)(2,1)S(1)} %copy-done.3, bf16[1024,1280]{1,0:T(8,128)(2,1)S(1)} %copy-done), custom_call_target="tpu_custom_call" | custom-call | tf_op jit(solution)/shard_map/pallas_call | solution.py:61
  10.4 8.9 %shard_map.85 = (bf16[2,160,1280]{2,1,0:T(8,128)(2,1)}, bf16[2,160,1280]{2,1,0:T(8,128)(2,1)}, bf16[2,160,1280]{2,1,0:T(8,128)(2,1)S(1)}, bf16[2,160,1280]{2,1,0...) custom-call(s32[7]{0:T(128)S(1)} %stack.31.place, ...), custom_call_target="tpu_custom_call" | custom-call | tf_op jit(solution)/shard_map/pallas_call | solution.py:61
  19.4 1.2 copy-done.4
  20.5 1.0 copy-done.6
  21.5 1.0 copy-done.8
  24.2 1.6 collective-permute-start.2
  25.8 1.7 collective-permute-start.3
  27.5 1.5 shard_map.89
  29.0 1.1 copy-done.2
  30.1 6.9 %all-to-all-start = ((bf16[16,2,40,480]{3,2,1,0:T(8,128)(2,1)}), bf16[16,2,40,480]{3,2,1,0:T(8,128)(2,1)}, u32[]{:S(2)}, u32[]{:S(2)}) async-start(bf16[16,2,40,480]{3,2,1,0:T(8,128)(2,1)} %copy-done.2), calls=%async_computation | async-start | bytes 2621440 | tf_op jit(solution)/shard_map/all_to_all | solution.py:354
  37.0 3.1 %collective-permute-start.1 = (bf16[2,160,1280]{2,1,0:T(8,128)(2,1)}, bf16[2,160,1280]{2,1,0:T(8,128)(2,1)S(1)}, u32[]{:S(2)}, u32[]{:S(2)}) collective-permute-start(bf16[2,160,1280]{2,1,0:T(8,128)(2,1)} %copy-done.14), channel_id=1, source_target_pairs={{0,12},{1,49},{4,0},{5,53},{8,4},{9,57},{12,8},{13,61},{16,28},{17... | collective-permute-start | bytes 2457608 | tf_op jit(solution)/shard_map/ppermute | solution.py:50
  40.1 4.4 %collective-permute-done.3.refs_3_ = bf16[2,160,1280]{2,1,0:T(8,128)(2,1)} collective-permute-done((bf16[2,160,1280]{2,1,0:T(8,128)(2,1)}, bf16[2,160,1280]{2,1,0:T(8,128)(2,1)}, u32[]{:S(2)}, u32[]{:S(2)}) %collective-permute-start.3) | collective-permute-done | bytes 819232 | tf_op jit(solution)/shard_map/ppermute | solution.py:50
  44.4 1.1 copy-done.7
  45.6 1.1 copy-done.9
  46.7 3.0 %shard_map.86 = (bf16[2,160,1280]{2,1,0:T(8,128)(2,1)}, bf16[2,160,1280]{2,1,0:T(8,128)(2,1)}) custom-call(s32[7]{0:T(128)S(1)} %stack.31.place, bf16[2,160,1280]{2,1,0:T(8,128)(2,1)S(1)} %copy-done.7, bf16[2,160,1280]{2,1,0:T(8,128)(2,1)} %collective-permute-done.2.refs_1_, bf16[2,160,1280]{2,1,0:T(8,128)(2,1)S(1)} %copy-done.9, ...), custom_call_target="tpu_custom_call" | custom-call | tf_op jit(solution)/shard_map/pallas_call | solution.py:61
  49.7 4.2 %collective-permute-start.6 = (bf16[2,160,1280]{2,1,0:T(8,128)(2,1)}, bf16[2,160,1280]{2,1,0:T(8,128)(2,1)}, u32[]{:S(2)}, u32[]{:S(2)}) collective-permute-start(bf16[2,160,1280]{2,1,0:T(8,128)(2,1)} %get-tuple-element.47), channel_id=1, source_target_pairs={{0,12},{1,49},{4,0},{5,53},{8,4},{9,57},{12,8},{13,61},{16,28},{17... | collective-permute-start | bytes 2457608 | tf_op jit(solution)/shard_map/ppermute | solution.py:50
  53.9 3.1 %all-to-all-done.got = bf16[16,2,40,480]{3,2,1,0:T(8,128)(2,1)} async-done(((bf16[16,2,40,480]{3,2,1,0:T(8,128)(2,1)}), bf16[16,2,40,480]{3,2,1,0:T(8,128)(2,1)}, u32[]{:S(2)}, u32[]{:S(2)}) %all-to-all-start) | async-done | bytes 1228832 | tf_op jit(solution)/shard_map/all_to_all | solution.py:354
  57.0 2.0 shard_map.90.here
  59.0 2.2 collective-permute-done.1.near_down
  61.8 8.8 %collective-permute-done.4.last_up = bf16[2,160,1280]{2,1,0:T(8,128)(2,1)} collective-permute-done((bf16[2,160,1280]{2,1,0:T(8,128)(2,1)}, bf16[2,160,1280]{2,1,0:T(8,128)(2,1)}, u32[]{:S(2)}, u32[]{:S(2)}) %collective-permute-start.4) | collective-permute-done | bytes 819232 | tf_op jit(solution)/shard_map/ppermute | solution.py:50
  70.6 2.7 %shard_map.87 = (f32[160,1280]{1,0:T(8,128)S(1)}, bf16[160,1280]{1,0:T(8,128)(2,1)S(1)}, bf16[160,1280]{1,0:T(8,128)(2,1)S(1)}, bf16[160,1280]{1,0:T(8,128)(2,1)S(1)}) custom-call(s32[7]{0:T(128)S(1)} %stack.31.place, bf16[4,160,1280]{2,1,0:T(8,128)(2,1)S(1)} %copy-done.5, bf16[2,160,1280]{2,1,0:T(8,128)(2,1)S(1)} %collective-permute-done.1.near_down, ...), custom_call_target="tpu_custom_call" | custom-call | tf_op jit(solution)/shard_map/pallas_call | solution.py:61
  73.9 5.6 %shard_map.91.made = bf16[2,4,160,1280]{3,2,1,0:T(8,128)(2,1)S(1)} custom-call(s32[7]{0:T(128)S(1)} %stack.31.place, bf16[1024,1280]{1,0:T(8,128)(2,1)} %collective-permute-done.11.features, bf16[1024,1280]{1,0:T(8,128)(2,1)S(1)} %copy-done.1), custom_call_target="tpu_custom_call" | custom-call | tf_op jit(solution)/shard_map/pallas_call | solution.py:61
  79.5 6.6 %shard_map.92 = (bf16[2,160,1280]{2,1,0:T(8,128)(2,1)S(1)}, bf16[2,160,1280]{2,1,0:T(8,128)(2,1)S(1)}, bf16[2,160,1280]{2,1,0:T(8,128)(2,1)S(1)}, bf16[2,160,128...) custom-call(s32[7]{0:T(128)S(1)} %stack.31.place, ...), custom_call_target="tpu_custom_call" | custom-call | tf_op jit(solution)/shard_map/pallas_call | solution.py:61
  86.1 1.0 collective-permute-start.14
  87.1 2.3 collective-permute-start.15
  90.3 1.1 collective-permute-start.17
  91.4 8.3 %collective-permute-done.14.refs_1_ = bf16[2,160,1280]{2,1,0:T(8,128)(2,1)S(1)} collective-permute-done((bf16[2,160,1280]{2,1,0:T(8,128)(2,1)S(1)}, bf16[2,160,1280]{2,1,0:T(8,128)(2,1)S(1)}, u32[]{:S(2)}, u32[]{:S(2)}) %collective-permute-start.14) | collective-permute-done | bytes 819232 | tf_op jit(solution)/shard_map/ppermute | solution.py:50
  100.7 1.4 collective-permute-start.16
  102.0 2.0 collective-permute-start.18
  104.0 3.1 %collective-permute-start.8 = (bf16[160,1280]{1,0:T(8,128)(2,1)S(1)}, bf16[160,1280]{1,0:T(8,128)(2,1)S(1)}, u32[]{:S(2)}, u32[]{:S(2)}) collective-permute-start(bf16[160,1280]{1,0:T(8,128)(2,1)S(1)} %get-tuple-element.50), channel_id=1, source_target_pairs={{0,32},{1,9},{4,36},{5,13},{8,40},{9,1},{12,44},{13,5},{16,48},{17... | collective-permute-start | bytes 1228808 | tf_op jit(solution)/shard_map/ppermute | solution.py:50
  107.2 4.4 %collective-permute-done.13.near_down = bf16[2,160,1280]{2,1,0:T(8,128)(2,1)S(1)} collective-permute-done((bf16[2,160,1280]{2,1,0:T(8,128)(2,1)S(1)}, bf16[2,160,1280]{2,1,0:T(8,128)(2,1)S(1)}, u32[]{:S(2)}, u32[]{:S(2)}) %collective-permute-start.13) | collective-permute-done | bytes 819232 | tf_op jit(solution)/shard_map/ppermute | solution.py:50
  111.6 4.9 %collective-permute-start.9 = (bf16[160,1280]{1,0:T(8,128)(2,1)S(1)}, bf16[160,1280]{1,0:T(8,128)(2,1)S(1)}, u32[]{:S(2)}, u32[]{:S(2)}) collective-permute-start(bf16[160,1280]{1,0:T(8,128)(2,1)S(1)} %get-tuple-element.51), channel_id=1, source_target_pairs={{0,48},{1,13},{4,52},{5,1},{8,56},{9,5},{12,60},{13,9},{16,0},{17,... | collective-permute-start | bytes 1228808 | tf_op jit(solution)/shard_map/ppermute | solution.py:50
  116.5 2.7 %collective-permute-start.23 = (bf16[2,3,160,640]{3,2,1,0:T(8,128)(2,1)S(1)}, bf16[2,3,160,640]{3,2,1,0:T(8,128)(2,1)S(1)}, u32[]{:S(2)}, u32[]{:S(2)}) collective-permute-start(bf16[2,3,160,640]{3,2,1,0:T(8,128)(2,1)S(1)} %shard_map.90.here), channel_id=1, source_target_pairs={{0,64},{64,0},{1,65},{65,1},{2,66},{66,2},{3,67},{67,3},{4,68},{68... | collective-permute-start | bytes 3686408 | tf_op jit(solution)/shard_map/ppermute | solution.py:39
  119.2 2.5 %collective-permute-done.16.last_up = bf16[2,160,1280]{2,1,0:T(8,128)(2,1)S(1)} collective-permute-done((bf16[2,160,1280]{2,1,0:T(8,128)(2,1)S(1)}, bf16[2,160,1280]{2,1,0:T(8,128)(2,1)S(1)}, u32[]{:S(2)}, u32[]{:S(2)}) %collective-permute-start.16) | collective-permute-done | bytes 819232 | tf_op jit(solution)/shard_map/ppermute | solution.py:50
  121.6 1.0 collective-permute-start.7
  122.6 3.2 %collective-permute-done.18.last_down = bf16[2,160,1280]{2,1,0:T(8,128)(2,1)S(1)} collective-permute-done((bf16[2,160,1280]{2,1,0:T(8,128)(2,1)S(1)}, bf16[2,160,1280]{2,1,0:T(8,128)(2,1)S(1)}, u32[]{:S(2)}, u32[]{:S(2)}) %collective-permute-start.18) | collective-permute-done | bytes 819232 | tf_op jit(solution)/shard_map/ppermute | solution.py:50
  125.8 1.6 shard_map.94
  127.4 1.6 collective-permute-start.19
  129.0 3.6 %collective-permute-start.20 = (bf16[160,1280]{1,0:T(8,128)(2,1)S(1)}, bf16[160,1280]{1,0:T(8,128)(2,1)S(1)}, u32[]{:S(2)}, u32[]{:S(2)}) collective-permute-start(bf16[160,1280]{1,0:T(8,128)(2,1)S(1)} %get-tuple-element.64), channel_id=1, source_target_pairs={{0,32},{1,9},{4,36},{5,13},{8,40},{9,1},{12,44},{13,5},{16,48},{17... | collective-permute-start | bytes 1228808 | tf_op jit(solution)/shard_map/ppermute | solution.py:50
  132.6 1.0 collective-permute-start.21
  134.3 2.8 %collective-permute-start.10 = (bf16[160,1280]{1,0:T(8,128)(2,1)S(1)}, bf16[160,1280]{1,0:T(8,128)(2,1)S(1)}, u32[]{:S(2)}, u32[]{:S(2)}) collective-permute-start(bf16[160,1280]{1,0:T(8,128)(2,1)S(1)} %shard_map.88.near), channel_id=1, source_target_pairs={{0,64},{64,0},{1,65},{65,1},{2,66},{66,2},{3,67},{67,3},{4,68},{68... | collective-permute-start | bytes 1228808 | tf_op jit(solution)/shard_map/ppermute | solution.py:39
  137.1 5.7 %collective-permute-done.20.two = bf16[160,1280]{1,0:T(8,128)(2,1)S(1)} collective-permute-done((bf16[160,1280]{1,0:T(8,128)(2,1)S(1)}, bf16[160,1280]{1,0:T(8,128)(2,1)S(1)}, u32[]{:S(2)}, u32[]{:S(2)}) %collective-permute-start.20) | collective-permute-done | bytes 409632 | tf_op jit(solution)/shard_map/ppermute | solution.py:50
  143.6 2.8 %collective-permute-start.22 = (bf16[160,1280]{1,0:T(8,128)(2,1)S(1)}, bf16[160,1280]{1,0:T(8,128)(2,1)S(1)}, u32[]{:S(2)}, u32[]{:S(2)}) collective-permute-start(bf16[160,1280]{1,0:T(8,128)(2,1)S(1)} %shard_map.95.far), channel_id=1, source_target_pairs={{0,64},{64,0},{1,65},{65,1},{2,66},{66,2},{3,67},{67,3},{4,68},{68... | collective-permute-start | bytes 1228808 | tf_op jit(solution)/shard_map/ppermute | solution.py:39
  146.4 6.2 %collective-permute-done.10.near_got = bf16[160,1280]{1,0:T(8,128)(2,1)S(1)} collective-permute-done((bf16[160,1280]{1,0:T(8,128)(2,1)S(1)}, bf16[160,1280]{1,0:T(8,128)(2,1)S(1)}, u32[]{:S(2)}, u32[]{:S(2)}) %collective-permute-start.10) | collective-permute-done | bytes 409632 | tf_op jit(solution)/shard_map/ppermute | solution.py:39
  152.6 4.4 %collective-permute-done.22.far_got = bf16[160,1280]{1,0:T(8,128)(2,1)S(1)} collective-permute-done((bf16[160,1280]{1,0:T(8,128)(2,1)S(1)}, bf16[160,1280]{1,0:T(8,128)(2,1)S(1)}, u32[]{:S(2)}, u32[]{:S(2)}) %collective-permute-start.22) | collective-permute-done | bytes 409632 | tf_op jit(solution)/shard_map/ppermute | solution.py:39
  157.0 4.6 %shard_map.96 = (f32[160,1280]{1,0:T(8,128)}, f32[160,1280]{1,0:T(8,128)}, f32[160,1280]{1,0:T(8,128)}, bf16[160,1280]{1,0:T(8,128)(2,1)S(1)}, bf16[160,1280]{1,0:T(8,128)(2,1)S(1)}) custom-call(s32[7]{0:T(128)S(1)} %stack.31.place, bf16[160,1280]{1,0:T(8,128)(2,1)S(1)} %shard_map.88.near, bf16[160,1280]{1,0:T(8,128)(2,1)S(1)} %collective-permute-done.10.near_got, ...), custom_call_target="tpu_custom_call" | custom-call | tf_op jit(solution)/shard_map/pallas_call | solution.py:61
  161.6 1.7 collective-permute-start.26
  163.4 1.8 collective-permute-start.25
  165.1 2.0 collective-permute-start.24
  167.2 3.9 %collective-permute-done.26.refs_6_ = bf16[160,1280]{1,0:T(8,128)(2,1)S(1)} collective-permute-done((bf16[160,1280]{1,0:T(8,128)(2,1)S(1)}, bf16[160,1280]{1,0:T(8,128)(2,1)S(1)}, u32[]{:S(2)}, u32[]{:S(2)}) %collective-permute-start.26) | collective-permute-done | bytes 409632 | tf_op jit(solution)/shard_map/ppermute | solution.py:50
  171.3 3.0 %collective-permute-start.28 = (bf16[160,1280]{1,0:T(8,128)(2,1)S(1)}, bf16[160,1280]{1,0:T(8,128)(2,1)S(1)}, u32[]{:S(2)}, u32[]{:S(2)}) collective-permute-start(bf16[160,1280]{1,0:T(8,128)(2,1)S(1)} %collective-permute-done.25.refs_3_), channel_id=1, source_target_pairs={{0,48},{1,13},{4,52},{5,1},{8,56},{9,5},{12,60},{13,9},{16,0},{17,... | collective-permute-start | bytes 1228808 | tf_op jit(solution)/shard_map/ppermute | solution.py:50
  174.3 1.4 collective-permute-done.24.refs_2_
  176.3 6.2 %collective-permute-done.27.refs_4_ = bf16[160,1280]{1,0:T(8,128)(2,1)S(1)} collective-permute-done((bf16[160,1280]{1,0:T(8,128)(2,1)S(1)}, bf16[160,1280]{1,0:T(8,128)(2,1)S(1)}, u32[]{:S(2)}, u32[]{:S(2)}) %collective-permute-start.27) | collective-permute-done | bytes 409632 | tf_op jit(solution)/shard_map/ppermute | solution.py:50
  183.5 3.2 %collective-permute-start.32 = (bf16[2,2,160,1280]{3,2,1,0:T(8,128)(2,1)S(1)}, bf16[2,2,160,1280]{3,2,1,0:T(8,128)(2,1)S(1)}, u32[]{:S(2)}, u32[]{:S(2)}) collective-permute-start(bf16[2,2,160,1280]{3,2,1,0:T(8,128)(2,1)S(1)} %get-tuple-element.73.refs_1_), channel_id=1, source_target_pairs={{0,12},{1,49},{4,0},{5,53},{8,4},{9,57},{12,8},{13,61},{16,28},{17... | collective-permute-start | bytes 4915208 | tf_op jit(solution)/shard_map/ppermute | solution.py:50
  186.7 2.0 collective-permute-start.34
  188.7 17.1 %collective-permute-done.30.refs_2_ = bf16[2,2,160,1280]{3,2,1,0:T(8,128)(2,1)S(1)} collective-permute-done((bf16[2,2,160,1280]{3,2,1,0:T(8,128)(2,1)S(1)}, bf16[2,2,160,1280]{3,2,1,0:T(8,128)(2,1)S(1)}, u32[]{:S(2)}, u32[]{:S(2)}) %collective-permute-start.30) | collective-permute-done | bytes 1638432 | tf_op jit(solution)/shard_map/ppermute | solution.py:50
  205.8 3.2 %collective-permute-start.33 = (bf16[2,2,160,1280]{3,2,1,0:T(8,128)(2,1)S(1)}, bf16[2,2,160,1280]{3,2,1,0:T(8,128)(2,1)S(1)}, u32[]{:S(2)}, u32[]{:S(2)}) collective-permute-start(bf16[2,2,160,1280]{3,2,1,0:T(8,128)(2,1)S(1)} %collective-permute-done.32.refs_3_), channel_id=1, source_target_pairs={{0,12},{1,49},{4,0},{5,53},{8,4},{9,57},{12,8},{13,61},{16,28},{17... | collective-permute-start | bytes 4915208 | tf_op jit(solution)/shard_map/ppermute | solution.py:50
  209.0 13.9 %collective-permute-done.35.refs_5_ = bf16[2,2,160,1280]{3,2,1,0:T(8,128)(2,1)S(1)} collective-permute-done((bf16[2,2,160,1280]{3,2,1,0:T(8,128)(2,1)S(1)}, bf16[2,2,160,1280]{3,2,1,0:T(8,128)(2,1)S(1)}, u32[]{:S(2)}, u32[]{:S(2)}) %collective-permute-start.35) | collective-permute-done | bytes 1638432 | tf_op jit(solution)/shard_map/ppermute | solution.py:50
  223.3 4.4 %shard_map.98.refs_2_ = bf16[2,4,4,160,1280]{4,3,2,1,0:T(8,128)(2,1)} custom-call(s32[7]{0:T(128)S(1)} %stack.31.place, bf16[2,2,160,1280]{3,2,1,0:T(8,128)(2,1)S(1)} %get-tuple-element.72.refs_0_, bf16[2,2,160,1280]{3,2,1,0:T(8,128)(2,1)S(1)} %get-tuple-element.73.refs_1_, bf16[2,2,160,1280]{3,2,1,0:T(8,128)(2,1)S(1)} %collective-permute-done.30.refs_2_, ...), custom_call_target="tpu_custom_call" | custom-call | tf_op jit(solution)/shard_map/pallas_call | solution.py:61
  227.7 13.2 %collective-permute-done.31.refs_0_ = bf16[2,2,160,1280]{3,2,1,0:T(8,128)(2,1)S(1)} collective-permute-done((bf16[2,2,160,1280]{3,2,1,0:T(8,128)(2,1)S(1)}, bf16[2,2,160,1280]{3,2,1,0:T(8,128)(2,1)S(1)}, u32[]{:S(2)}, u32[]{:S(2)}) %collective-permute-start.31) | collective-permute-done | bytes 1638432 | tf_op jit(solution)/shard_map/ppermute | solution.py:50
  240.9 2.3 shard_map.99
  (57 shorter events, 8.8 us)
Async XLA Ops:
  0.6 9.8 %collective-permute-start = (bf16[1024,1280]{1,0:T(8,128)(2,1)}, bf16[1024,1280]{1,0:T(8,128)(2,1)}, u32[]{:S(2)}, u32[]{:S(2)}) collective-permute-start(bf16[1024,1280]{1,0:T(8,128)(2,1)} %features.1), channel_id=1, source_target_pairs={{0,1},{1,0},{2,3},{3,2},{4,5},{5,4},{6,7},{7,6},{8,9},{9,8},{10,11... | collective-permute-start | bytes 7864328 | tf_op jit(solution)/shard_map/ppermute | solution.py:39
  0.7 72.6 %collective-permute-start.11 = (bf16[1024,1280]{1,0:T(8,128)(2,1)}, bf16[1024,1280]{1,0:T(8,128)(2,1)}, u32[]{:S(2)}, u32[]{:S(2)}) collective-permute-start(bf16[1024,1280]{1,0:T(8,128)(2,1)} %features.1), channel_id=1, source_target_pairs={{0,2},{2,0},{1,3},{3,1},{4,6},{6,4},{5,7},{7,5},{8,10},{10,8},{9,1... | collective-permute-start | bytes 7864328 | tf_op jit(solution)/shard_map/ppermute | solution.py:39
  2.5 1.7 copy-start
  4.2 1.7 copy-start.3
  6.0 4.5 %copy-start.1 = (bf16[1024,1280]{1,0:T(8,128)(2,1)S(1)}, bf16[1024,1280]{1,0:T(8,128)(2,1)}, u32[]{:S(2)}) copy-start(bf16[1024,1280]{1,0:T(8,128)(2,1)} %cotangent.7) | copy-start | bytes 7864324
  10.4 17.1 %copy-start.10 = (f32[5120,40]{0,1:T(8,128)S(1)}, f32[5120,40]{0,1:T(8,128)}, u32[]{:S(2)}) copy-start(f32[5120,40]{0,1:T(8,128)} %param.7) | copy-start | bytes 2457604
  10.4 17.1 %copy-start.11 = (f32[5120,40]{0,1:T(8,128)S(1)}, f32[5120,40]{0,1:T(8,128)}, u32[]{:S(2)}) copy-start(f32[5120,40]{0,1:T(8,128)} %param.8) | copy-start | bytes 2457604
  10.4 17.1 %copy-start.12 = (f32[5120,40]{0,1:T(8,128)S(1)}, f32[5120,40]{0,1:T(8,128)}, u32[]{:S(2)}) copy-start(f32[5120,40]{0,1:T(8,128)} %param.9) | copy-start | bytes 2457604
  19.3 1.2 copy-start.4
  20.5 1.0 copy-start.6
  21.5 1.0 copy-start.8
  22.4 0.9 copy-start.13
  23.3 0.9 copy-start.14
  24.2 15.8 %collective-permute-start.2 = (bf16[2,160,1280]{2,1,0:T(8,128)(2,1)}, bf16[2,160,1280]{2,1,0:T(8,128)(2,1)}, u32[]{:S(2)}, u32[]{:S(2)}) collective-permute-start(bf16[2,160,1280]{2,1,0:T(8,128)(2,1)} %get-tuple-element.42), channel_id=1, source_target_pairs={{0,4},{1,17},{4,8},{5,21},{8,12},{9,25},{12,0},{13,29},{16,20},{17... | collective-permute-start | bytes 2457608 | tf_op jit(solution)/shard_map/ppermute | solution.py:50
  25.8 18.6 %collective-permute-start.3 = (bf16[2,160,1280]{2,1,0:T(8,128)(2,1)}, bf16[2,160,1280]{2,1,0:T(8,128)(2,1)}, u32[]{:S(2)}, u32[]{:S(2)}) collective-permute-start(bf16[2,160,1280]{2,1,0:T(8,128)(2,1)} %get-tuple-element.44), channel_id=1, source_target_pairs={{0,12},{1,49},{4,0},{5,53},{8,4},{9,57},{12,8},{13,61},{16,28},{17... | collective-permute-start | bytes 2457608 | tf_op jit(solution)/shard_map/ppermute | solution.py:50
  29.0 1.1 copy-start.2
  30.1 26.9 %all-to-all-start = ((bf16[16,2,40,480]{3,2,1,0:T(8,128)(2,1)}), bf16[16,2,40,480]{3,2,1,0:T(8,128)(2,1)}, u32[]{:S(2)}, u32[]{:S(2)}) async-start(bf16[16,2,40,480]{3,2,1,0:T(8,128)(2,1)} %copy-done.2), calls=%async_computation | async-start | bytes 2621440 | tf_op jit(solution)/shard_map/all_to_all | solution.py:354
  37.0 24.3 %collective-permute-start.1 = (bf16[2,160,1280]{2,1,0:T(8,128)(2,1)}, bf16[2,160,1280]{2,1,0:T(8,128)(2,1)S(1)}, u32[]{:S(2)}, u32[]{:S(2)}) collective-permute-start(bf16[2,160,1280]{2,1,0:T(8,128)(2,1)} %copy-done.14), channel_id=1, source_target_pairs={{0,12},{1,49},{4,0},{5,53},{8,4},{9,57},{12,8},{13,61},{16,28},{17... | collective-permute-start | bytes 2457608 | tf_op jit(solution)/shard_map/ppermute | solution.py:50
  40.0 21.7 %collective-permute-start.5 = (bf16[2,160,1280]{2,1,0:T(8,128)(2,1)}, bf16[2,160,1280]{2,1,0:T(8,128)(2,1)}, u32[]{:S(2)}, u32[]{:S(2)}) collective-permute-start(bf16[2,160,1280]{2,1,0:T(8,128)(2,1)} %copy-done.13), channel_id=1, source_target_pairs={{0,4},{1,17},{4,8},{5,21},{8,12},{9,25},{12,0},{13,29},{16,20},{17... | collective-permute-start | bytes 2457608 | tf_op jit(solution)/shard_map/ppermute | solution.py:50
  44.4 1.1 copy-start.7
  45.6 1.1 copy-start.9
  49.7 20.9 %collective-permute-start.4 = (bf16[2,160,1280]{2,1,0:T(8,128)(2,1)}, bf16[2,160,1280]{2,1,0:T(8,128)(2,1)}, u32[]{:S(2)}, u32[]{:S(2)}) collective-permute-start(bf16[2,160,1280]{2,1,0:T(8,128)(2,1)} %get-tuple-element.45), channel_id=1, source_target_pairs={{0,4},{1,17},{4,8},{5,21},{8,12},{9,25},{12,0},{13,29},{16,20},{17... | collective-permute-start | bytes 2457608 | tf_op jit(solution)/shard_map/ppermute | solution.py:50
  49.7 20.9 %collective-permute-start.6 = (bf16[2,160,1280]{2,1,0:T(8,128)(2,1)}, bf16[2,160,1280]{2,1,0:T(8,128)(2,1)}, u32[]{:S(2)}, u32[]{:S(2)}) collective-permute-start(bf16[2,160,1280]{2,1,0:T(8,128)(2,1)} %get-tuple-element.47), channel_id=1, source_target_pairs={{0,12},{1,49},{4,0},{5,53},{8,4},{9,57},{12,8},{13,61},{16,28},{17... | collective-permute-start | bytes 2457608 | tf_op jit(solution)/shard_map/ppermute | solution.py:50
  57.0 13.6 %copy-start.5 = (bf16[4,160,1280]{2,1,0:T(8,128)(2,1)S(1)}, bf16[4,160,1280]{2,1,0:T(8,128)(2,1)}, u32[]{:S(2)}) copy-start(bf16[4,160,1280]{2,1,0:T(8,128)(2,1)} %copy-done.4) | copy-start | bytes 4915204
  73.3 6.2 %collective-permute-start.12 = (bf16[1024,1280]{1,0:T(8,128)(2,1)}, bf16[1024,1280]{1,0:T(8,128)(2,1)S(1)}, u32[]{:S(2)}, u32[]{:S(2)}) collective-permute-start(bf16[1024,1280]{1,0:T(8,128)(2,1)} %collective-permute-done.11.features), channel_id=1, source_target_pairs={{0,1},{1,0},{2,3},{3,2},{4,5},{5,4},{6,7},{7,6},{8,9},{9,8},{10,11... | collective-permute-start | bytes 7864328 | tf_op jit(solution)/shard_map/ppermute | solution.py:39
  86.1 13.6 %collective-permute-start.14 = (bf16[2,160,1280]{2,1,0:T(8,128)(2,1)S(1)}, bf16[2,160,1280]{2,1,0:T(8,128)(2,1)S(1)}, u32[]{:S(2)}, u32[]{:S(2)}) collective-permute-start(bf16[2,160,1280]{2,1,0:T(8,128)(2,1)S(1)} %get-tuple-element.56), channel_id=1, source_target_pairs={{0,4},{1,17},{4,8},{5,21},{8,12},{9,25},{12,0},{13,29},{16,20},{17... | collective-permute-start | bytes 2457608 | tf_op jit(solution)/shard_map/ppermute | solution.py:50
  87.1 12.6 %collective-permute-start.15 = (bf16[2,160,1280]{2,1,0:T(8,128)(2,1)S(1)}, bf16[2,160,1280]{2,1,0:T(8,128)(2,1)S(1)}, u32[]{:S(2)}, u32[]{:S(2)}) collective-permute-start(bf16[2,160,1280]{2,1,0:T(8,128)(2,1)S(1)} %get-tuple-element.58), channel_id=1, source_target_pairs={{0,12},{1,49},{4,0},{5,53},{8,4},{9,57},{12,8},{13,61},{16,28},{17... | collective-permute-start | bytes 2457608 | tf_op jit(solution)/shard_map/ppermute | solution.py:50
  89.4 22.2 %collective-permute-start.13 = (bf16[2,160,1280]{2,1,0:T(8,128)(2,1)S(1)}, bf16[2,160,1280]{2,1,0:T(8,128)(2,1)S(1)}, u32[]{:S(2)}, u32[]{:S(2)}) collective-permute-start(bf16[2,160,1280]{2,1,0:T(8,128)(2,1)S(1)} %get-tuple-element.54), channel_id=1, source_target_pairs={{0,12},{1,49},{4,0},{5,53},{8,4},{9,57},{12,8},{13,61},{16,28},{17... | collective-permute-start | bytes 2457608 | tf_op jit(solution)/shard_map/ppermute | solution.py:50
  90.3 26.2 %collective-permute-start.17 = (bf16[2,160,1280]{2,1,0:T(8,128)(2,1)S(1)}, bf16[2,160,1280]{2,1,0:T(8,128)(2,1)S(1)}, u32[]{:S(2)}, u32[]{:S(2)}) collective-permute-start(bf16[2,160,1280]{2,1,0:T(8,128)(2,1)S(1)} %get-tuple-element.60), channel_id=1, source_target_pairs={{0,4},{1,17},{4,8},{5,21},{8,12},{9,25},{12,0},{13,29},{16,20},{17... | collective-permute-start | bytes 2457608 | tf_op jit(solution)/shard_map/ppermute | solution.py:50
  100.7 21.0 %collective-permute-start.16 = (bf16[2,160,1280]{2,1,0:T(8,128)(2,1)S(1)}, bf16[2,160,1280]{2,1,0:T(8,128)(2,1)S(1)}, u32[]{:S(2)}, u32[]{:S(2)}) collective-permute-start(bf16[2,160,1280]{2,1,0:T(8,128)(2,1)S(1)} %get-tuple-element.59), channel_id=1, source_target_pairs={{0,4},{1,17},{4,8},{5,21},{8,12},{9,25},{12,0},{13,29},{16,20},{17... | collective-permute-start | bytes 2457608 | tf_op jit(solution)/shard_map/ppermute | solution.py:50
  102.0 23.8 %collective-permute-start.18 = (bf16[2,160,1280]{2,1,0:T(8,128)(2,1)S(1)}, bf16[2,160,1280]{2,1,0:T(8,128)(2,1)S(1)}, u32[]{:S(2)}, u32[]{:S(2)}) collective-permute-start(bf16[2,160,1280]{2,1,0:T(8,128)(2,1)S(1)} %get-tuple-element.61), channel_id=1, source_target_pairs={{0,12},{1,49},{4,0},{5,53},{8,4},{9,57},{12,8},{13,61},{16,28},{17... | collective-permute-start | bytes 2457608 | tf_op jit(solution)/shard_map/ppermute | solution.py:50
  104.0 24.9 %collective-permute-start.8 = (bf16[160,1280]{1,0:T(8,128)(2,1)S(1)}, bf16[160,1280]{1,0:T(8,128)(2,1)S(1)}, u32[]{:S(2)}, u32[]{:S(2)}) collective-permute-start(bf16[160,1280]{1,0:T(8,128)(2,1)S(1)} %get-tuple-element.50), channel_id=1, source_target_pairs={{0,32},{1,9},{4,36},{5,13},{8,40},{9,1},{12,44},{13,5},{16,48},{17... | collective-permute-start | bytes 1228808 | tf_op jit(solution)/shard_map/ppermute | solution.py:50
  111.6 20.9 %collective-permute-start.9 = (bf16[160,1280]{1,0:T(8,128)(2,1)S(1)}, bf16[160,1280]{1,0:T(8,128)(2,1)S(1)}, u32[]{:S(2)}, u32[]{:S(2)}) collective-permute-start(bf16[160,1280]{1,0:T(8,128)(2,1)S(1)} %get-tuple-element.51), channel_id=1, source_target_pairs={{0,48},{1,13},{4,52},{5,1},{8,56},{9,5},{12,60},{13,9},{16,0},{17,... | collective-permute-start | bytes 1228808 | tf_op jit(solution)/shard_map/ppermute | solution.py:50
  116.5 36.2 %collective-permute-start.23 = (bf16[2,3,160,640]{3,2,1,0:T(8,128)(2,1)S(1)}, bf16[2,3,160,640]{3,2,1,0:T(8,128)(2,1)S(1)}, u32[]{:S(2)}, u32[]{:S(2)}) collective-permute-start(bf16[2,3,160,640]{3,2,1,0:T(8,128)(2,1)S(1)} %shard_map.90.here), channel_id=1, source_target_pairs={{0,64},{64,0},{1,65},{65,1},{2,66},{66,2},{3,67},{67,3},{4,68},{68... | collective-permute-start | bytes 3686408 | tf_op jit(solution)/shard_map/ppermute | solution.py:39
  121.6 11.9 %collective-permute-start.7 = (bf16[160,1280]{1,0:T(8,128)(2,1)S(1)}, bf16[160,1280]{1,0:T(8,128)(2,1)S(1)}, u32[]{:S(2)}, u32[]{:S(2)}) collective-permute-start(bf16[160,1280]{1,0:T(8,128)(2,1)S(1)} %get-tuple-element.49), channel_id=1, source_target_pairs={{0,16},{1,5},{4,20},{5,9},{8,24},{9,13},{12,28},{13,1},{16,32},{17... | collective-permute-start | bytes 1228808 | tf_op jit(solution)/shard_map/ppermute | solution.py:50
  127.4 9.7 %collective-permute-start.19 = (bf16[160,1280]{1,0:T(8,128)(2,1)S(1)}, bf16[160,1280]{1,0:T(8,128)(2,1)S(1)}, u32[]{:S(2)}, u32[]{:S(2)}) collective-permute-start(bf16[160,1280]{1,0:T(8,128)(2,1)S(1)} %get-tuple-element.63), channel_id=1, source_target_pairs={{0,16},{1,5},{4,20},{5,9},{8,24},{9,13},{12,28},{13,1},{16,32},{17... | collective-permute-start | bytes 1228808 | tf_op jit(solution)/shard_map/ppermute | solution.py:50
  129.0 13.9 %collective-permute-start.20 = (bf16[160,1280]{1,0:T(8,128)(2,1)S(1)}, bf16[160,1280]{1,0:T(8,128)(2,1)S(1)}, u32[]{:S(2)}, u32[]{:S(2)}) collective-permute-start(bf16[160,1280]{1,0:T(8,128)(2,1)S(1)} %get-tuple-element.64), channel_id=1, source_target_pairs={{0,32},{1,9},{4,36},{5,13},{8,40},{9,1},{12,44},{13,5},{16,48},{17... | collective-permute-start | bytes 1228808 | tf_op jit(solution)/shard_map/ppermute | solution.py:50
  132.6 10.3 %collective-permute-start.21 = (bf16[160,1280]{1,0:T(8,128)(2,1)S(1)}, bf16[160,1280]{1,0:T(8,128)(2,1)S(1)}, u32[]{:S(2)}, u32[]{:S(2)}) collective-permute-start(bf16[160,1280]{1,0:T(8,128)(2,1)S(1)} %get-tuple-element.65), channel_id=1, source_target_pairs={{0,48},{1,13},{4,52},{5,1},{8,56},{9,5},{12,60},{13,9},{16,0},{17,... | collective-permute-start | bytes 1228808 | tf_op jit(solution)/shard_map/ppermute | solution.py:50
  134.3 18.3 %collective-permute-start.10 = (bf16[160,1280]{1,0:T(8,128)(2,1)S(1)}, bf16[160,1280]{1,0:T(8,128)(2,1)S(1)}, u32[]{:S(2)}, u32[]{:S(2)}) collective-permute-start(bf16[160,1280]{1,0:T(8,128)(2,1)S(1)} %shard_map.88.near), channel_id=1, source_target_pairs={{0,64},{64,0},{1,65},{65,1},{2,66},{66,2},{3,67},{67,3},{4,68},{68... | collective-permute-start | bytes 1228808 | tf_op jit(solution)/shard_map/ppermute | solution.py:39
  143.6 13.4 %collective-permute-start.22 = (bf16[160,1280]{1,0:T(8,128)(2,1)S(1)}, bf16[160,1280]{1,0:T(8,128)(2,1)S(1)}, u32[]{:S(2)}, u32[]{:S(2)}) collective-permute-start(bf16[160,1280]{1,0:T(8,128)(2,1)S(1)} %shard_map.95.far), channel_id=1, source_target_pairs={{0,64},{64,0},{1,65},{65,1},{2,66},{66,2},{3,67},{67,3},{4,68},{68... | collective-permute-start | bytes 1228808 | tf_op jit(solution)/shard_map/ppermute | solution.py:39
  161.6 9.4 %collective-permute-start.26 = (bf16[160,1280]{1,0:T(8,128)(2,1)S(1)}, bf16[160,1280]{1,0:T(8,128)(2,1)S(1)}, u32[]{:S(2)}, u32[]{:S(2)}) collective-permute-start(bf16[160,1280]{1,0:T(8,128)(2,1)S(1)} %get-tuple-element.70.refs_0_), channel_id=1, source_target_pairs={{0,16},{1,5},{4,20},{5,9},{8,24},{9,13},{12,28},{13,1},{16,32},{17... | collective-permute-start | bytes 1228808 | tf_op jit(solution)/shard_map/ppermute | solution.py:50
  163.4 8.0 %collective-permute-start.25 = (bf16[160,1280]{1,0:T(8,128)(2,1)S(1)}, bf16[160,1280]{1,0:T(8,128)(2,1)S(1)}, u32[]{:S(2)}, u32[]{:S(2)}) collective-permute-start(bf16[160,1280]{1,0:T(8,128)(2,1)S(1)} %get-tuple-element.71.refs_1_), channel_id=1, source_target_pairs={{0,48},{1,13},{4,52},{5,1},{8,56},{9,5},{12,60},{13,9},{16,0},{17,... | collective-permute-start | bytes 1228808 | tf_op jit(solution)/shard_map/ppermute | solution.py:50
  165.1 10.6 %collective-permute-start.24 = (bf16[160,1280]{1,0:T(8,128)(2,1)S(1)}, bf16[160,1280]{1,0:T(8,128)(2,1)S(1)}, u32[]{:S(2)}, u32[]{:S(2)}) collective-permute-start(bf16[160,1280]{1,0:T(8,128)(2,1)S(1)} %get-tuple-element.70.refs_0_), channel_id=1, source_target_pairs={{0,48},{1,13},{4,52},{5,1},{8,56},{9,5},{12,60},{13,9},{16,0},{17,... | collective-permute-start | bytes 1228808 | tf_op jit(solution)/shard_map/ppermute | solution.py:50
  167.2 9.2 %collective-permute-start.29 = (bf16[160,1280]{1,0:T(8,128)(2,1)S(1)}, bf16[160,1280]{1,0:T(8,128)(2,1)S(1)}, u32[]{:S(2)}, u32[]{:S(2)}) collective-permute-start(bf16[160,1280]{1,0:T(8,128)(2,1)S(1)} %get-tuple-element.71.refs_1_), channel_id=1, source_target_pairs={{0,16},{1,5},{4,20},{5,9},{8,24},{9,13},{12,28},{13,1},{16,32},{17... | collective-permute-start | bytes 1228808 | tf_op jit(solution)/shard_map/ppermute | solution.py:50
  171.1 11.5 %collective-permute-start.27 = (bf16[160,1280]{1,0:T(8,128)(2,1)S(1)}, bf16[160,1280]{1,0:T(8,128)(2,1)S(1)}, u32[]{:S(2)}, u32[]{:S(2)}) collective-permute-start(bf16[160,1280]{1,0:T(8,128)(2,1)S(1)} %collective-permute-done.26.refs_6_), channel_id=1, source_target_pairs={{0,16},{1,5},{4,20},{5,9},{8,24},{9,13},{12,28},{13,1},{16,32},{17... | collective-permute-start | bytes 1228808 | tf_op jit(solution)/shard_map/ppermute | solution.py:50
  171.3 11.3 %collective-permute-start.28 = (bf16[160,1280]{1,0:T(8,128)(2,1)S(1)}, bf16[160,1280]{1,0:T(8,128)(2,1)S(1)}, u32[]{:S(2)}, u32[]{:S(2)}) collective-permute-start(bf16[160,1280]{1,0:T(8,128)(2,1)S(1)} %collective-permute-done.25.refs_3_), channel_id=1, source_target_pairs={{0,48},{1,13},{4,52},{5,1},{8,56},{9,5},{12,60},{13,9},{16,0},{17,... | collective-permute-start | bytes 1228808 | tf_op jit(solution)/shard_map/ppermute | solution.py:50
  183.4 22.4 %collective-permute-start.30 = (bf16[2,2,160,1280]{3,2,1,0:T(8,128)(2,1)S(1)}, bf16[2,2,160,1280]{3,2,1,0:T(8,128)(2,1)S(1)}, u32[]{:S(2)}, u32[]{:S(2)}) collective-permute-start(bf16[2,2,160,1280]{3,2,1,0:T(8,128)(2,1)S(1)} %get-tuple-element.72.refs_0_), channel_id=1, source_target_pairs={{0,4},{1,17},{4,8},{5,21},{8,12},{9,25},{12,0},{13,29},{16,20},{17... | collective-permute-start | bytes 4915208 | tf_op jit(solution)/shard_map/ppermute | solution.py:50
  183.5 22.3 %collective-permute-start.32 = (bf16[2,2,160,1280]{3,2,1,0:T(8,128)(2,1)S(1)}, bf16[2,2,160,1280]{3,2,1,0:T(8,128)(2,1)S(1)}, u32[]{:S(2)}, u32[]{:S(2)}) collective-permute-start(bf16[2,2,160,1280]{3,2,1,0:T(8,128)(2,1)S(1)} %get-tuple-element.73.refs_1_), channel_id=1, source_target_pairs={{0,12},{1,49},{4,0},{5,53},{8,4},{9,57},{12,8},{13,61},{16,28},{17... | collective-permute-start | bytes 4915208 | tf_op jit(solution)/shard_map/ppermute | solution.py:50
  186.7 36.2 %collective-permute-start.35 = (bf16[2,2,160,1280]{3,2,1,0:T(8,128)(2,1)S(1)}, bf16[2,2,160,1280]{3,2,1,0:T(8,128)(2,1)S(1)}, u32[]{:S(2)}, u32[]{:S(2)}) collective-permute-start(bf16[2,2,160,1280]{3,2,1,0:T(8,128)(2,1)S(1)} %get-tuple-element.72.refs_0_), channel_id=1, source_target_pairs={{0,12},{1,49},{4,0},{5,53},{8,4},{9,57},{12,8},{13,61},{16,28},{17... | collective-permute-start | bytes 4915208 | tf_op jit(solution)/shard_map/ppermute | solution.py:50
  186.7 36.6 %collective-permute-start.34 = (bf16[2,2,160,1280]{3,2,1,0:T(8,128)(2,1)S(1)}, bf16[2,2,160,1280]{3,2,1,0:T(8,128)(2,1)S(1)}, u32[]{:S(2)}, u32[]{:S(2)}) collective-permute-start(bf16[2,2,160,1280]{3,2,1,0:T(8,128)(2,1)S(1)} %get-tuple-element.73.refs_1_), channel_id=1, source_target_pairs={{0,4},{1,17},{4,8},{5,21},{8,12},{9,25},{12,0},{13,29},{16,20},{17... | collective-permute-start | bytes 4915208 | tf_op jit(solution)/shard_map/ppermute | solution.py:50
  205.8 35.1 %collective-permute-start.31 = (bf16[2,2,160,1280]{3,2,1,0:T(8,128)(2,1)S(1)}, bf16[2,2,160,1280]{3,2,1,0:T(8,128)(2,1)S(1)}, u32[]{:S(2)}, u32[]{:S(2)}) collective-permute-start(bf16[2,2,160,1280]{3,2,1,0:T(8,128)(2,1)S(1)} %collective-permute-done.30.refs_2_), channel_id=1, source_target_pairs={{0,4},{1,17},{4,8},{5,21},{8,12},{9,25},{12,0},{13,29},{16,20},{17... | collective-permute-start | bytes 4915208 | tf_op jit(solution)/shard_map/ppermute | solution.py:50
  205.8 35.1 %collective-permute-start.33 = (bf16[2,2,160,1280]{3,2,1,0:T(8,128)(2,1)S(1)}, bf16[2,2,160,1280]{3,2,1,0:T(8,128)(2,1)S(1)}, u32[]{:S(2)}, u32[]{:S(2)}) collective-permute-start(bf16[2,2,160,1280]{3,2,1,0:T(8,128)(2,1)S(1)} %collective-permute-done.32.refs_3_), channel_id=1, source_target_pairs={{0,12},{1,49},{4,0},{5,53},{8,4},{9,57},{12,8},{13,61},{16,28},{17... | collective-permute-start | bytes 4915208 | tf_op jit(solution)/shard_map/ppermute | solution.py:50

commit v2 on v1

--- a/solution.py
+++ b/solution.py
@@ -222,61 +222,67 @@
     return (weights_new, first_new, second_new)
 
 
-def adam_kernel(place, near, near_got, far, far_got, here, there, weights, first, second, *both):
+def gradient_and_state(place, pair, half, states, rows, s):
+    here, there = states
+    columns = slice(s * PART, (s + 1) * PART)
+    gradient = f32(pair[0][rows, columns]) + f32(pair[1][rows, columns])
+    return gradient, [
+        jnp.where(place[XH] == s, f32(here[half, k, rows]), f32(there[half, k, rows])) for k in range(3)
+    ]
+
+
+def adam_kernel(is_near, place, one, two, here, there, out):
+    half = place[XL] if is_near else 1 - place[XL]
+
     def step(rows):
-        for half in range(2):
-            is_near = half == place[XL]
-            gradient = f32(jnp.where(is_near, f32(near[rows]), f32(far[rows]))) + jnp.where(
-                is_near, f32(near_got[rows]), f32(far_got[rows])
+        for s in range(2):
+            gradient, old = gradient_and_state(place, (one, two), half, (here, there), rows, s)
+            out[rows, s * PART : (s + 1) * PART] = bf16(adam_update(*old, gradient)[0])
+
+    in_rows(step)
+
+
+def adam(place, is_near, pair, states):
+    return call(functools.partial(adam_kernel, is_near), place, (*pair, *states), [shape(ROWS, COLS)])[0]
+
+
+def adam_own_kernel(place, near, near_got, far, far_got, here, there, weights, first, second):
+    def step(rows):
+        is_near = place[XH] == place[XL]
+        for s in range(2):
+            columns = slice(s * PART, (s + 1) * PART)
+            _, old = gradient_and_state(place, (near, near_got), place[XH], (here, there), rows, s)
+            gradient = jnp.where(is_near, f32(near[rows, columns]), f32(far[rows, columns])) + jnp.where(
+                is_near, f32(near_got[rows, columns]), f32(far_got[rows, columns])
             )
-            for s in range(2):
-                old = [
-                    jnp.where(place[XH] == s, f32(here[half, k, rows]), f32(there[half, k, rows])) for k in range(3)
-                ]
-                columns = slice(s * PART, (s + 1) * PART)
-                new = adam_update(*old, gradient[:, columns])
-                both[half][rows, columns] = bf16(new[0])
-
-                @pl.when(half == place[XH])
-                def _():
-                    for ref, value in zip((weights, first, second), new):
-                        ref[rows, columns] = value
+            for ref, value in zip((weights, first, second), adam_update(*old, gradient)):
+                ref[rows, columns] = value
 
     in_rows(step)
 
 
-def adam(place, gradients, here, there):
-    return call(
-        adam_kernel,
-        place,
-        (*gradients, here, there),
-        [shape(ROWS, COLS, dtype=jnp.float32)] * 3 + [shape(ROWS, COLS)] * 2,
-    )
-
-
 def line_kernel(place, *refs):
-    low, high = refs[8:]
-    for ahead in range(4):
-        source = lax.rem(place[SECOND] + ahead, 4)
+    low, high = refs[4:]
+    for behind in range(4):
+        source = lax.rem(place[SECOND] + 4 - behind, 4)
 
         @pl.when(source < 2)
         def _():
-            for x in range(2):
-                low[x, source] = refs[2 * ahead + x][...]
+            low[source] = refs[behind][...]
 
         @pl.when(source >= 2)
         def _():
-            for x in range(2):
-                high[x, source - 2] = refs[2 * ahead + x][...]
-
-
-def lay_kernel(steps, place, *refs):
+            high[source - 2] = refs[behind][...]
+
+
+def lay_kernel(is_near, steps, place, *refs):
     out, sems = refs[-2], refs[-1]
+    x = place[XL] if is_near else 1 - place[XL]
 
     def copy(k, along_y):
         half, ahead = steps[k]
         other, pair = lax.rem(place[FIRST] + ahead, 4), pl.ds(2 * half, 2)
-        index = (slice(None), pair, other) if along_y else (slice(None), other, pair)
+        index = (x, pair, other) if along_y else (x, other, pair)
         return pltpu.make_async_copy(refs[k], out.at[index], sems.at[k])
 
     for core in range(2):
@@ -289,9 +295,9 @@
                 copy(k, core == 0).wait()
 
 
-def lay(place, steps, pieces, *out):
+def lay(place, is_near, steps, pieces, *out):
     return call(
-        functools.partial(lay_kernel, steps),
+        functools.partial(lay_kernel, is_near, steps),
         place,
         [*pieces, *out],
         [shape(2, 4, 4, ROWS, COLS)],
@@ -301,20 +307,19 @@
     )[0]
 
 
-def gather_ring(low, high, second):
-    low_up, high_down = ring(low, second, 1), ring(high, second, -1)
-    high_up, low_down = ring(high, second, 1), ring(low, second, -1)
-    far_up, far_down = ring(low_up, second, 1), ring(high_down, second, -1)
-    return low_down, high_down, far_up, far_down, low_up, high_up
-
-
-def gathered(place, both):
-    blocks = (*both, *gather_ring(*both, 1))
-    low, high = call(line_kernel, place, blocks, [shape(2, 2, ROWS, COLS)] * 2)
-    low_down, high_down, far_up, far_down, low_up, high_up = gather_ring(low, high, 0)
+def lines(place, block):
+    blocks = (block, *(ring(block, 1, k) for k in (1, 2, 3)))
+    return call(line_kernel, place, blocks, [shape(2, ROWS, COLS)] * 2)
+
+
+def gathered(place, line, is_near, *out):
+    low, high = line
+    low_up, high_down = ring(low, 0, 1), ring(high, 0, -1)
+    high_up, low_down = ring(high, 0, 1), ring(low, 0, -1)
+    far_up, far_down = ring(low_up, 0, 1), ring(high_down, 0, -1)
     steps = ((0, 0), (1, 0), (0, 3), (1, 1), (1, 3), (0, 1))
-    out = lay(place, steps, (low, high, low_up, high_down, high_up, low_down))
-    return lay(place, ((0, 2), (1, 2)), (far_up, far_down), out)
+    out = lay(place, is_near, steps, (low, high, low_up, high_down, high_up, low_down), *out)
+    return lay(place, is_near, ((0, 2), (1, 2)), (far_up, far_down), out)
 
 
 def state_kernel(place, got, out, turned):
@@ -373,10 +378,21 @@
     there = shift(here, "xh", 1)
     messages = products(place, cotangent, across, shift(across, "c", 1))
     near_got = shift(near, "xh", 1)
-    far, _ = reduced(place, messages)
+    near_line = lines(place, adam(place, True, (near, near_got), (here, there)))
+    far, sent = reduced(place, messages)
+
+    *near_line, _ = lax.optimization_barrier((*near_line, sent))
+    out = gathered(place, near_line, True)
     far_got = shift(far, "xh", 1)
-    weights_new, first_new, second_new, *both = adam(place, (near, near_got, far, far_got), here, there)
-    out = gathered(place, both)
+    block = adam(place, False, (far, far_got), (here, there))
+    far_line = lines(place, block)
+    out = gathered(place, far_line, False, out)
+    weights_new, first_new, second_new = call(
+        adam_own_kernel,
+        place,
+        (near, near_got, far, far_got, here, there),
+        [shape(ROWS, COLS, dtype=jnp.float32)] * 3,
+    )
     return (weights_new, first_new, second_new, out.reshape(D, COLS))
 
 

time: 244 us -> 257 us (1.053)
  starting transfers between devices: 69.3 us -> 88.2 us
  waiting for transfers between devices: 110 us -> 101 us
  Pallas kernels: 50.7 us -> 55.3 us
    ppermute x30 -> x36, waiting for transfers between devices: 96.8 us -> 76.8 us  [ring(): return lax.ppermute(value, ('z', 'y', 'c'), pairs)]
    ppermute x30 -> x36, starting transfers between devices: 51.7 us -> 70.6 us  [ring(): return lax.ppermute(value, ('z', 'y', 'c'), pairs)]
    ppermute x6, waiting for transfers between devices: 10.6 us -> 21.1 us  [shift(): lax.ppermute(value, axis, [(i, (i + step) % count) for i in range(count)])]
    pallas_call x16 -> x21, Pallas kernels: 50.7 us -> 55.3 us  [call(): pl.pallas_call(kernel, out_shape=outs, in_specs=[pl.BlockSpec(memory_spac...]
  transfers between devices with their start and end apart: 37 -> 43, of which waited for: 20 -> 18; matrix products, arithmetic and copies ran while one was open for 0% -> 0% of each run, Pallas kernels for 15% -> 21%
where the time goes in v2:
time: 257 us; the launch traced here: 256 us
  waiting for transfers between devices  101 us (39%)
  starting transfers between devices  88.2 us (34%)
  Pallas kernels  55.3 us (22%)
  local copies, waits for them, and re-layouts  10.1 us (4%)
    ppermute x36, waiting for transfers between devices, ring(): return lax.ppermute(value, ('z', 'y', 'c'), pairs)  76.8 us
    ppermute x36, starting transfers between devices, ring(): return lax.ppermute(value, ('z', 'y', 'c'), pairs)  70.6 us
    pallas_call x21, Pallas kernels, call(): pl.pallas_call(kernel, out_shape=outs, in_specs=[pl.BlockSpec(memory_spac...  55.3 us
    ppermute x6, waiting for transfers between devices, shift(): lax.ppermute(value, axis, [(i, (i + step) % count) for i in range(count)])  21.1 us
    ppermute x6, starting transfers between devices, shift(): lax.ppermute(value, axis, [(i, (i + step) % count) for i in range(count)])  10.8 us
    unnamed x30, local copies, waits for them, and re-layouts  10 us
    all_to_all x1, starting transfers between devices, moved_state(): got = lax.all_to_all(flat, ('z', 'y'), 0, 0, tiled=True)  6.88 us
  transfers between devices with their start and end apart: 43, of which 18 were waited for; matrix products, arithmetic and copies ran while one was open for 0% of the time, Pallas kernels for 21%

profile of v2, /device:TPU:0, one launch (start us, length us, event | category | flops | bytes accessed | tf_op | source)
XLA Modules:
  0.0 255.8 jit_solution(6826859315530622555)
XLA Ops:
  0.7 1.7 collective-permute-start.11
  2.5 1.7 copy-done
  4.2 1.7 copy-done.3
  6.0 4.4 %shard_map.84.made = bf16[2,4,160,1280]{3,2,1,0:T(8,128)(2,1)S(1)} custom-call(s32[7]{0:T(128)S(1)} %stack.31.place, bf16[1024,1280]{1,0:T(8,128)(2,1)S(1)} %copy-done.3, bf16[1024,1280]{1,0:T(8,128)(2,1)S(1)} %copy-done), custom_call_target="tpu_custom_call" | custom-call | tf_op jit(solution)/shard_map/pallas_call | solution.py:61
  10.4 8.9 %shard_map.85 = (bf16[2,160,1280]{2,1,0:T(8,128)(2,1)}, bf16[2,160,1280]{2,1,0:T(8,128)(2,1)}, bf16[2,160,1280]{2,1,0:T(8,128)(2,1)S(1)}, bf16[2,160,1280]{2,1,0...) custom-call(s32[7]{0:T(128)S(1)} %stack.31.place, ...), custom_call_target="tpu_custom_call" | custom-call | tf_op jit(solution)/shard_map/pallas_call | solution.py:61
  19.3 1.2 copy-done.4
  22.5 1.6 collective-permute-start.2
  24.0 1.7 collective-permute-start.3
  25.7 1.5 shard_map.89
  28.3 6.9 %all-to-all-start = ((bf16[16,2,40,480]{3,2,1,0:T(8,128)(2,1)}), bf16[16,2,40,480]{3,2,1,0:T(8,128)(2,1)}, u32[]{:S(2)}, u32[]{:S(2)}) async-start(bf16[16,2,40,480]{3,2,1,0:T(8,128)(2,1)} %copy-done.2), calls=%async_computation | async-start | bytes 2621440 | tf_op jit(solution)/shard_map/all_to_all | solution.py:359
  35.2 3.1 %collective-permute-start.1 = (bf16[2,160,1280]{2,1,0:T(8,128)(2,1)}, bf16[2,160,1280]{2,1,0:T(8,128)(2,1)S(1)}, u32[]{:S(2)}, u32[]{:S(2)}) collective-permute-start(bf16[2,160,1280]{2,1,0:T(8,128)(2,1)} %copy-done.14), channel_id=1, source_target_pairs={{0,12},{1,49},{4,0},{5,53},{8,4},{9,57},{12,8},{13,61},{16,28},{17... | collective-permute-start | bytes 2457608 | tf_op jit(solution)/shard_map/ppermute | solution.py:50
  38.3 4.4 %collective-permute-done.3.refs_3_ = bf16[2,160,1280]{2,1,0:T(8,128)(2,1)} collective-permute-done((bf16[2,160,1280]{2,1,0:T(8,128)(2,1)}, bf16[2,160,1280]{2,1,0:T(8,128)(2,1)}, u32[]{:S(2)}, u32[]{:S(2)}) %collective-permute-start.3) | collective-permute-done | bytes 819232 | tf_op jit(solution)/shard_map/ppermute | solution.py:50
  45.0 3.0 %shard_map.86 = (bf16[2,160,1280]{2,1,0:T(8,128)(2,1)}, bf16[2,160,1280]{2,1,0:T(8,128)(2,1)}) custom-call(s32[7]{0:T(128)S(1)} %stack.31.place, bf16[2,160,1280]{2,1,0:T(8,128)(2,1)S(1)} %copy-done.7, bf16[2,160,1280]{2,1,0:T(8,128)(2,1)} %collective-permute-done.2.refs_1_, bf16[2,160,1280]{2,1,0:T(8,128)(2,1)S(1)} %copy-done.9, ...), custom_call_target="tpu_custom_call" | custom-call | tf_op jit(solution)/shard_map/pallas_call | solution.py:61
  47.9 4.2 %collective-permute-start.6 = (bf16[2,160,1280]{2,1,0:T(8,128)(2,1)}, bf16[2,160,1280]{2,1,0:T(8,128)(2,1)}, u32[]{:S(2)}, u32[]{:S(2)}) collective-permute-start(bf16[2,160,1280]{2,1,0:T(8,128)(2,1)} %get-tuple-element.49), channel_id=1, source_target_pairs={{0,12},{1,49},{4,0},{5,53},{8,4},{9,57},{12,8},{13,61},{16,28},{17... | collective-permute-start | bytes 2457608 | tf_op jit(solution)/shard_map/ppermute | solution.py:50
  52.1 3.1 %all-to-all-done.got = bf16[16,2,40,480]{3,2,1,0:T(8,128)(2,1)} async-done(((bf16[16,2,40,480]{3,2,1,0:T(8,128)(2,1)}), bf16[16,2,40,480]{3,2,1,0:T(8,128)(2,1)}, u32[]{:S(2)}, u32[]{:S(2)}) %all-to-all-start) | async-done | bytes 1228832 | tf_op jit(solution)/shard_map/all_to_all | solution.py:359
  55.2 2.0 shard_map.90.here
  57.3 2.2 collective-permute-done.1.near_down
  60.0 8.8 %collective-permute-done.4.last_up = bf16[2,160,1280]{2,1,0:T(8,128)(2,1)} collective-permute-done((bf16[2,160,1280]{2,1,0:T(8,128)(2,1)}, bf16[2,160,1280]{2,1,0:T(8,128)(2,1)}, u32[]{:S(2)}, u32[]{:S(2)}) %collective-permute-start.4) | collective-permute-done | bytes 819232 | tf_op jit(solution)/shard_map/ppermute | solution.py:50
  68.8 2.8 %shard_map.87 = (f32[160,1280]{1,0:T(8,128)S(1)}, bf16[160,1280]{1,0:T(8,128)(2,1)S(1)}, bf16[160,1280]{1,0:T(8,128)(2,1)S(1)}, bf16[160,1280]{1,0:T(8,128)(2,1)S(1)}) custom-call(s32[7]{0:T(128)S(1)} %stack.31.place, bf16[4,160,1280]{2,1,0:T(8,128)(2,1)S(1)} %copy-done.5, bf16[2,160,1280]{2,1,0:T(8,128)(2,1)S(1)} %collective-permute-done.1.near_down, ...), custom_call_target="tpu_custom_call" | custom-call | tf_op jit(solution)/shard_map/pallas_call | solution.py:61
  72.2 1.2 collective-permute-start.7
  73.4 5.6 %shard_map.91.made = bf16[2,4,160,1280]{3,2,1,0:T(8,128)(2,1)S(1)} custom-call(s32[7]{0:T(128)S(1)} %stack.31.place, bf16[1024,1280]{1,0:T(8,128)(2,1)} %collective-permute-done.11.features, bf16[1024,1280]{1,0:T(8,128)(2,1)S(1)} %copy-done.1), custom_call_target="tpu_custom_call" | custom-call | tf_op jit(solution)/shard_map/pallas_call | solution.py:61
  79.0 6.4 %shard_map.92 = (bf16[2,160,1280]{2,1,0:T(8,128)(2,1)S(1)}, bf16[2,160,1280]{2,1,0:T(8,128)(2,1)S(1)}, bf16[2,160,1280]{2,1,0:T(8,128)(2,1)S(1)}, bf16[2,160,128...) custom-call(s32[7]{0:T(128)S(1)} %stack.31.place, ...), custom_call_target="tpu_custom_call" | custom-call | tf_op jit(solution)/shard_map/pallas_call | solution.py:61
  85.4 1.6 collective-permute-start.14
  87.0 1.7 collective-permute-start.15
  88.7 3.6 %collective-permute-start.8 = (bf16[160,1280]{1,0:T(8,128)(2,1)S(1)}, bf16[160,1280]{1,0:T(8,128)(2,1)S(1)}, u32[]{:S(2)}, u32[]{:S(2)}) collective-permute-start(bf16[160,1280]{1,0:T(8,128)(2,1)S(1)} %get-tuple-element.52), channel_id=1, source_target_pairs={{0,32},{1,9},{4,36},{5,13},{8,40},{9,1},{12,44},{13,5},{16,48},{17... | collective-permute-start | bytes 1228808 | tf_op jit(solution)/shard_map/ppermute | solution.py:50
  93.3 2.7 %collective-permute-start.23 = (bf16[2,3,160,640]{3,2,1,0:T(8,128)(2,1)S(1)}, bf16[2,3,160,640]{3,2,1,0:T(8,128)(2,1)S(1)}, u32[]{:S(2)}, u32[]{:S(2)}) collective-permute-start(bf16[2,3,160,640]{3,2,1,0:T(8,128)(2,1)S(1)} %shard_map.90.here), channel_id=1, source_target_pairs={{0,64},{64,0},{1,65},{65,1},{2,66},{66,2},{3,67},{67,3},{4,68},{68... | collective-permute-start | bytes 3686408 | tf_op jit(solution)/shard_map/ppermute | solution.py:39
  96.0 6.6 %collective-permute-done.8.two = bf16[160,1280]{1,0:T(8,128)(2,1)S(1)} collective-permute-done((bf16[160,1280]{1,0:T(8,128)(2,1)S(1)}, bf16[160,1280]{1,0:T(8,128)(2,1)S(1)}, u32[]{:S(2)}, u32[]{:S(2)}) %collective-permute-start.8) | collective-permute-done | bytes 409632 | tf_op jit(solution)/shard_map/ppermute | solution.py:50
  102.6 3.2 %collective-permute-done.9.three = bf16[160,1280]{1,0:T(8,128)(2,1)S(1)} collective-permute-done((bf16[160,1280]{1,0:T(8,128)(2,1)S(1)}, bf16[160,1280]{1,0:T(8,128)(2,1)S(1)}, u32[]{:S(2)}, u32[]{:S(2)}) %collective-permute-start.9) | collective-permute-done | bytes 409632 | tf_op jit(solution)/shard_map/ppermute | solution.py:50
  106.5 2.8 %collective-permute-start.10 = (bf16[160,1280]{1,0:T(8,128)(2,1)S(1)}, bf16[160,1280]{1,0:T(8,128)(2,1)S(1)}, u32[]{:S(2)}, u32[]{:S(2)}) collective-permute-start(bf16[160,1280]{1,0:T(8,128)(2,1)S(1)} %shard_map.88.near.one), channel_id=1, source_target_pairs={{0,64},{64,0},{1,65},{65,1},{2,66},{66,2},{3,67},{67,3},{4,68},{68... | collective-permute-start | bytes 1228808 | tf_op jit(solution)/shard_map/ppermute | solution.py:39
  109.3 1.7 collective-permute-start.13
  112.3 1.4 collective-permute-start.16
  113.7 16.6 %collective-permute-done.10.near_got.two = bf16[160,1280]{1,0:T(8,128)(2,1)S(1)} collective-permute-done((bf16[160,1280]{1,0:T(8,128)(2,1)S(1)}, bf16[160,1280]{1,0:T(8,128)(2,1)S(1)}, u32[]{:S(2)}, u32[]{:S(2)}) %collective-permute-start.10) | collective-permute-done | bytes 409632 | tf_op jit(solution)/shard_map/ppermute | solution.py:39
  130.5 1.6 shard_map.99.refs_0_
  132.2 3.1 %collective-permute-start.34 = (bf16[160,1280]{1,0:T(8,128)(2,1)S(1)}, bf16[160,1280]{1,0:T(8,128)(2,1)S(1)}, u32[]{:S(2)}, u32[]{:S(2)}) collective-permute-start(bf16[160,1280]{1,0:T(8,128)(2,1)S(1)} %shard_map.99.refs_0_), channel_id=1, source_target_pairs={{0,32},{1,9},{4,36},{5,13},{8,40},{9,1},{12,44},{13,5},{16,48},{17... | collective-permute-start | bytes 1228808 | tf_op jit(solution)/shard_map/ppermute | solution.py:50
  136.4 12.8 %collective-permute-done.18.last_down = bf16[2,160,1280]{2,1,0:T(8,128)(2,1)S(1)} collective-permute-done((bf16[2,160,1280]{2,1,0:T(8,128)(2,1)S(1)}, bf16[2,160,1280]{2,1,0:T(8,128)(2,1)S(1)}, u32[]{:S(2)}, u32[]{:S(2)}) %collective-permute-start.18) | collective-permute-done | bytes 819232 | tf_op jit(solution)/shard_map/ppermute | solution.py:50
  149.2 1.6 shard_map.94
  150.8 1.3 collective-permute-start.19
  152.1 6.3 %collective-permute-start.20 = (bf16[160,1280]{1,0:T(8,128)(2,1)S(1)}, bf16[160,1280]{1,0:T(8,128)(2,1)S(1)}, u32[]{:S(2)}, u32[]{:S(2)}) collective-permute-start(bf16[160,1280]{1,0:T(8,128)(2,1)S(1)} %get-tuple-element.66), channel_id=1, source_target_pairs={{0,32},{1,9},{4,36},{5,13},{8,40},{9,1},{12,44},{13,5},{16,48},{17... | collective-permute-start | bytes 1228808 | tf_op jit(solution)/shard_map/ppermute | solution.py:50
  158.4 2.5 collective-permute-start.21
  161.7 3.5 %collective-permute-start.36 = (bf16[2,160,1280]{2,1,0:T(8,128)(2,1)S(1)}, bf16[2,160,1280]{2,1,0:T(8,128)(2,1)S(1)}, u32[]{:S(2)}, u32[]{:S(2)}) collective-permute-start(bf16[2,160,1280]{2,1,0:T(8,128)(2,1)S(1)} %get-tuple-element.76.refs_0_), channel_id=1, source_target_pairs={{0,4},{1,17},{4,8},{5,21},{8,12},{9,25},{12,0},{13,29},{16,20},{17... | collective-permute-start | bytes 2457608 | tf_op jit(solution)/shard_map/ppermute | solution.py:50
  165.2 9.7 %collective-permute-done.20.two = bf16[160,1280]{1,0:T(8,128)(2,1)S(1)} collective-permute-done((bf16[160,1280]{1,0:T(8,128)(2,1)S(1)}, bf16[160,1280]{1,0:T(8,128)(2,1)S(1)}, u32[]{:S(2)}, u32[]{:S(2)}) %collective-permute-start.20) | collective-permute-done | bytes 409632 | tf_op jit(solution)/shard_map/ppermute | solution.py:50
  175.6 2.9 %collective-permute-start.22 = (bf16[160,1280]{1,0:T(8,128)(2,1)S(1)}, bf16[160,1280]{1,0:T(8,128)(2,1)S(1)}, u32[]{:S(2)}, u32[]{:S(2)}) collective-permute-start(bf16[160,1280]{1,0:T(8,128)(2,1)S(1)} %shard_map.95.far.one), channel_id=1, source_target_pairs={{0,64},{64,0},{1,65},{65,1},{2,66},{66,2},{3,67},{67,3},{4,68},{68... | collective-permute-start | bytes 1228808 | tf_op jit(solution)/shard_map/ppermute | solution.py:39
  178.5 2.2 collective-permute-start.38
  180.7 4.5 %collective-permute-done.22.far_got.two = bf16[160,1280]{1,0:T(8,128)(2,1)S(1)} collective-permute-done((bf16[160,1280]{1,0:T(8,128)(2,1)S(1)}, bf16[160,1280]{1,0:T(8,128)(2,1)S(1)}, u32[]{:S(2)}, u32[]{:S(2)}) %collective-permute-start.22) | collective-permute-done | bytes 409632 | tf_op jit(solution)/shard_map/ppermute | solution.py:39
  185.2 1.6 shard_map.97.refs_0_
  186.8 1.4 collective-permute-start.25
  188.2 2.5 collective-permute-start.26
  190.8 6.4 %collective-permute-start.40 = (bf16[2,160,1280]{2,1,0:T(8,128)(2,1)S(1)}, bf16[2,160,1280]{2,1,0:T(8,128)(2,1)S(1)}, u32[]{:S(2)}, u32[]{:S(2)}) collective-permute-start(bf16[2,160,1280]{2,1,0:T(8,128)(2,1)S(1)} %get-tuple-element.77.refs_1_), channel_id=1, source_target_pairs={{0,4},{1,17},{4,8},{5,21},{8,12},{9,25},{12,0},{13,29},{16,20},{17... | collective-permute-start | bytes 2457608 | tf_op jit(solution)/shard_map/ppermute | solution.py:50
  197.2 5.8 %collective-permute-done.24.refs_1_ = bf16[160,1280]{1,0:T(8,128)(2,1)S(1)} collective-permute-done((bf16[160,1280]{1,0:T(8,128)(2,1)S(1)}, bf16[160,1280]{1,0:T(8,128)(2,1)S(1)}, u32[]{:S(2)}, u32[]{:S(2)}) %collective-permute-start.24) | collective-permute-done | bytes 409632 | tf_op jit(solution)/shard_map/ppermute | solution.py:50
  203.0 3.6 %collective-permute-done.25.refs_2_ = bf16[160,1280]{1,0:T(8,128)(2,1)S(1)} collective-permute-done((bf16[160,1280]{1,0:T(8,128)(2,1)S(1)}, bf16[160,1280]{1,0:T(8,128)(2,1)S(1)}, u32[]{:S(2)}, u32[]{:S(2)}) %collective-permute-start.25) | collective-permute-done | bytes 409632 | tf_op jit(solution)/shard_map/ppermute | solution.py:50
  206.5 7.1 %collective-permute-start.37 = (bf16[2,160,1280]{2,1,0:T(8,128)(2,1)S(1)}, bf16[2,160,1280]{2,1,0:T(8,128)(2,1)S(1)}, u32[]{:S(2)}, u32[]{:S(2)}) collective-permute-start(bf16[2,160,1280]{2,1,0:T(8,128)(2,1)S(1)} %collective-permute-done.36.refs_2_), channel_id=1, source_target_pairs={{0,4},{1,17},{4,8},{5,21},{8,12},{9,25},{12,0},{13,29},{16,20},{17... | collective-permute-start | bytes 2457608 | tf_op jit(solution)/shard_map/ppermute | solution.py:50
  214.5 3.2 %collective-permute-start.29 = (bf16[2,160,1280]{2,1,0:T(8,128)(2,1)S(1)}, bf16[2,160,1280]{2,1,0:T(8,128)(2,1)S(1)}, u32[]{:S(2)}, u32[]{:S(2)}) collective-permute-start(bf16[2,160,1280]{2,1,0:T(8,128)(2,1)S(1)} %get-tuple-element.73.refs_1_), channel_id=1, source_target_pairs={{0,12},{1,49},{4,0},{5,53},{8,4},{9,57},{12,8},{13,61},{16,28},{17... | collective-permute-start | bytes 2457608 | tf_op jit(solution)/shard_map/ppermute | solution.py:50
  217.8 2.0 collective-permute-start.31
  219.7 3.8 %collective-permute-done.37.refs_0_ = bf16[2,160,1280]{2,1,0:T(8,128)(2,1)S(1)} collective-permute-done((bf16[2,160,1280]{2,1,0:T(8,128)(2,1)S(1)}, bf16[2,160,1280]{2,1,0:T(8,128)(2,1)S(1)}, u32[]{:S(2)}, u32[]{:S(2)}) %collective-permute-start.37) | collective-permute-done | bytes 819232 | tf_op jit(solution)/shard_map/ppermute | solution.py:50
  224.6 7.7 %collective-permute-done.27.refs_2_ = bf16[2,160,1280]{2,1,0:T(8,128)(2,1)S(1)} collective-permute-done((bf16[2,160,1280]{2,1,0:T(8,128)(2,1)S(1)}, bf16[2,160,1280]{2,1,0:T(8,128)(2,1)S(1)}, u32[]{:S(2)}, u32[]{:S(2)}) %collective-permute-start.27) | collective-permute-done | bytes 819232 | tf_op jit(solution)/shard_map/ppermute | solution.py:50
  232.3 2.5 collective-permute-start.28
  235.5 3.1 %shard_map.96 = (f32[160,1280]{1,0:T(8,128)}, f32[160,1280]{1,0:T(8,128)}, f32[160,1280]{1,0:T(8,128)}) custom-call(s32[7]{0:T(128)S(1)} %stack.31.place, bf16[160,1280]{1,0:T(8,128)(2,1)S(1)} %shard_map.88.near.one, bf16[160,1280]{1,0:T(8,128)(2,1)S(1)} %collective-permute-done.10.near_got.two, bf16[160,1280]{1,0:T(8,128)(2,1)S(1)} %shard_map.95.far.one, ...), custom_call_target="tpu_custom_call" | custom-call | tf_op jit(solution)/shard_map/pallas_call | solution.py:61
  238.6 2.8 %shard_map.101.refs_2_ = bf16[2,4,4,160,1280]{4,3,2,1,0:T(8,128)(2,1)} custom-call(s32[7]{0:T(128)S(1)} %stack.31.place, bf16[2,160,1280]{2,1,0:T(8,128)(2,1)S(1)} %get-tuple-element.76.refs_0_, bf16[2,160,1280]{2,1,0:T(8,128)(2,1)S(1)} %get-tuple-element.77.refs_1_, bf16[2,160,1280]{2,1,0:T(8,128)(2,1)S(1)} %collective-permute-done.36.refs_2_, ...), custom_call_target="tpu_custom_call" | custom-call | tf_op jit(solution)/shard_map/pallas_call | solution.py:61
  241.5 1.7 shard_map.102.refs_6_
  243.2 1.9 collective-permute-done.32.refs_5_
  245.1 2.8 %shard_map.103.refs_2_ = bf16[2,4,4,160,1280]{4,3,2,1,0:T(8,128)(2,1)} custom-call(s32[7]{0:T(128)S(1)} %stack.31.place, bf16[2,160,1280]{2,1,0:T(8,128)(2,1)S(1)} %get-tuple-element.72.refs_0_, bf16[2,160,1280]{2,1,0:T(8,128)(2,1)S(1)} %get-tuple-element.73.refs_1_, ...), custom_call_target="tpu_custom_call", output_to_operand_aliasing={{}: (7, {})} | custom-call | tf_op jit(solution)/shard_map/pallas_call | solution.py:61
  247.9 1.9 collective-permute-done.28.refs_0_
  249.9 4.0 %collective-permute-done.30.refs_1_ = bf16[2,160,1280]{2,1,0:T(8,128)(2,1)S(1)} collective-permute-done((bf16[2,160,1280]{2,1,0:T(8,128)(2,1)S(1)}, bf16[2,160,1280]{2,1,0:T(8,128)(2,1)S(1)}, u32[]{:S(2)}, u32[]{:S(2)}) %collective-permute-start.30) | collective-permute-done | bytes 819232 | tf_op jit(solution)/shard_map/ppermute | solution.py:50
  253.9 1.7 shard_map.104
  (74 shorter events, 15.4 us)
Async XLA Ops:
  0.6 9.8 %collective-permute-start = (bf16[1024,1280]{1,0:T(8,128)(2,1)}, bf16[1024,1280]{1,0:T(8,128)(2,1)}, u32[]{:S(2)}, u32[]{:S(2)}) collective-permute-start(bf16[1024,1280]{1,0:T(8,128)(2,1)} %features.1), channel_id=1, source_target_pairs={{0,1},{1,0},{2,3},{3,2},{4,5},{5,4},{6,7},{7,6},{8,9},{9,8},{10,11... | collective-permute-start | bytes 7864328 | tf_op jit(solution)/shard_map/ppermute | solution.py:39
  0.7 70.9 %collective-permute-start.11 = (bf16[1024,1280]{1,0:T(8,128)(2,1)}, bf16[1024,1280]{1,0:T(8,128)(2,1)}, u32[]{:S(2)}, u32[]{:S(2)}) collective-permute-start(bf16[1024,1280]{1,0:T(8,128)(2,1)} %features.1), channel_id=1, source_target_pairs={{0,2},{2,0},{1,3},{3,1},{4,6},{6,4},{5,7},{7,5},{8,10},{10,8},{9,1... | collective-permute-start | bytes 7864328 | tf_op jit(solution)/shard_map/ppermute | solution.py:39
  2.5 1.7 copy-start
  4.2 1.7 copy-start.3
  6.0 4.5 %copy-start.1 = (bf16[1024,1280]{1,0:T(8,128)(2,1)S(1)}, bf16[1024,1280]{1,0:T(8,128)(2,1)}, u32[]{:S(2)}) copy-start(bf16[1024,1280]{1,0:T(8,128)(2,1)} %cotangent.7) | copy-start | bytes 7864324
  10.4 15.3 %copy-start.10 = (f32[5120,40]{0,1:T(8,128)S(1)}, f32[5120,40]{0,1:T(8,128)}, u32[]{:S(2)}) copy-start(f32[5120,40]{0,1:T(8,128)} %param.7) | copy-start | bytes 2457604
  10.4 15.3 %copy-start.11 = (f32[5120,40]{0,1:T(8,128)S(1)}, f32[5120,40]{0,1:T(8,128)}, u32[]{:S(2)}) copy-start(f32[5120,40]{0,1:T(8,128)} %param.8) | copy-start | bytes 2457604
  10.4 15.3 %copy-start.12 = (f32[5120,40]{0,1:T(8,128)S(1)}, f32[5120,40]{0,1:T(8,128)}, u32[]{:S(2)}) copy-start(f32[5120,40]{0,1:T(8,128)} %param.9) | copy-start | bytes 2457604
  19.3 1.2 copy-start.4
  20.5 1.0 copy-start.6
  21.5 1.0 copy-start.8
  22.5 3.2 %copy-start.13 = (bf16[2,160,1280]{2,1,0:T(8,128)(2,1)}, bf16[2,160,1280]{2,1,0:T(8,128)(2,1)S(1)}, u32[]{:S(2)}) copy-start(bf16[2,160,1280]{2,1,0:T(8,128)(2,1)S(1)} %get-tuple-element.48) | copy-start | bytes 2457604
  22.5 3.2 %copy-start.14 = (bf16[2,160,1280]{2,1,0:T(8,128)(2,1)}, bf16[2,160,1280]{2,1,0:T(8,128)(2,1)S(1)}, u32[]{:S(2)}) copy-start(bf16[2,160,1280]{2,1,0:T(8,128)(2,1)S(1)} %get-tuple-element.42) | copy-start | bytes 2457604
  22.5 15.8 %collective-permute-start.2 = (bf16[2,160,1280]{2,1,0:T(8,128)(2,1)}, bf16[2,160,1280]{2,1,0:T(8,128)(2,1)}, u32[]{:S(2)}, u32[]{:S(2)}) collective-permute-start(bf16[2,160,1280]{2,1,0:T(8,128)(2,1)} %get-tuple-element.44), channel_id=1, source_target_pairs={{0,4},{1,17},{4,8},{5,21},{8,12},{9,25},{12,0},{13,29},{16,20},{17... | collective-permute-start | bytes 2457608 | tf_op jit(solution)/shard_map/ppermute | solution.py:50
  24.0 18.6 %collective-permute-start.3 = (bf16[2,160,1280]{2,1,0:T(8,128)(2,1)}, bf16[2,160,1280]{2,1,0:T(8,128)(2,1)}, u32[]{:S(2)}, u32[]{:S(2)}) collective-permute-start(bf16[2,160,1280]{2,1,0:T(8,128)(2,1)} %get-tuple-element.46), channel_id=1, source_target_pairs={{0,12},{1,49},{4,0},{5,53},{8,4},{9,57},{12,8},{13,61},{16,28},{17... | collective-permute-start | bytes 2457608 | tf_op jit(solution)/shard_map/ppermute | solution.py:50
  27.2 1.1 copy-start.2
  28.3 26.9 %all-to-all-start = ((bf16[16,2,40,480]{3,2,1,0:T(8,128)(2,1)}), bf16[16,2,40,480]{3,2,1,0:T(8,128)(2,1)}, u32[]{:S(2)}, u32[]{:S(2)}) async-start(bf16[16,2,40,480]{3,2,1,0:T(8,128)(2,1)} %copy-done.2), calls=%async_computation | async-start | bytes 2621440 | tf_op jit(solution)/shard_map/all_to_all | solution.py:359
  35.2 24.3 %collective-permute-start.1 = (bf16[2,160,1280]{2,1,0:T(8,128)(2,1)}, bf16[2,160,1280]{2,1,0:T(8,128)(2,1)S(1)}, u32[]{:S(2)}, u32[]{:S(2)}) collective-permute-start(bf16[2,160,1280]{2,1,0:T(8,128)(2,1)} %copy-done.14), channel_id=1, source_target_pairs={{0,12},{1,49},{4,0},{5,53},{8,4},{9,57},{12,8},{13,61},{16,28},{17... | collective-permute-start | bytes 2457608 | tf_op jit(solution)/shard_map/ppermute | solution.py:50
  38.3 21.7 %collective-permute-start.5 = (bf16[2,160,1280]{2,1,0:T(8,128)(2,1)}, bf16[2,160,1280]{2,1,0:T(8,128)(2,1)}, u32[]{:S(2)}, u32[]{:S(2)}) collective-permute-start(bf16[2,160,1280]{2,1,0:T(8,128)(2,1)} %copy-done.13), channel_id=1, source_target_pairs={{0,4},{1,17},{4,8},{5,21},{8,12},{9,25},{12,0},{13,29},{16,20},{17... | collective-permute-start | bytes 2457608 | tf_op jit(solution)/shard_map/ppermute | solution.py:50
  42.7 1.1 copy-start.7
  43.8 1.1 copy-start.9
  47.9 20.9 %collective-permute-start.4 = (bf16[2,160,1280]{2,1,0:T(8,128)(2,1)}, bf16[2,160,1280]{2,1,0:T(8,128)(2,1)}, u32[]{:S(2)}, u32[]{:S(2)}) collective-permute-start(bf16[2,160,1280]{2,1,0:T(8,128)(2,1)} %get-tuple-element.47), channel_id=1, source_target_pairs={{0,4},{1,17},{4,8},{5,21},{8,12},{9,25},{12,0},{13,29},{16,20},{17... | collective-permute-start | bytes 2457608 | tf_op jit(solution)/shard_map/ppermute | solution.py:50
  47.9 20.9 %collective-permute-start.6 = (bf16[2,160,1280]{2,1,0:T(8,128)(2,1)}, bf16[2,160,1280]{2,1,0:T(8,128)(2,1)}, u32[]{:S(2)}, u32[]{:S(2)}) collective-permute-start(bf16[2,160,1280]{2,1,0:T(8,128)(2,1)} %get-tuple-element.49), channel_id=1, source_target_pairs={{0,12},{1,49},{4,0},{5,53},{8,4},{9,57},{12,8},{13,61},{16,28},{17... | collective-permute-start | bytes 2457608 | tf_op jit(solution)/shard_map/ppermute | solution.py:50
  55.2 13.6 %copy-start.5 = (bf16[4,160,1280]{2,1,0:T(8,128)(2,1)S(1)}, bf16[4,160,1280]{2,1,0:T(8,128)(2,1)}, u32[]{:S(2)}) copy-start(bf16[4,160,1280]{2,1,0:T(8,128)(2,1)} %copy-done.4) | copy-start | bytes 4915204
  71.6 7.4 %collective-permute-start.12 = (bf16[1024,1280]{1,0:T(8,128)(2,1)}, bf16[1024,1280]{1,0:T(8,128)(2,1)S(1)}, u32[]{:S(2)}, u32[]{:S(2)}) collective-permute-start(bf16[1024,1280]{1,0:T(8,128)(2,1)} %collective-permute-done.11.features), channel_id=1, source_target_pairs={{0,1},{1,0},{2,3},{3,2},{4,5},{5,4},{6,7},{7,6},{8,9},{9,8},{10,11... | collective-permute-start | bytes 7864328 | tf_op jit(solution)/shard_map/ppermute | solution.py:39
  72.2 21.0 %collective-permute-start.7 = (bf16[160,1280]{1,0:T(8,128)(2,1)S(1)}, bf16[160,1280]{1,0:T(8,128)(2,1)S(1)}, u32[]{:S(2)}, u32[]{:S(2)}) collective-permute-start(bf16[160,1280]{1,0:T(8,128)(2,1)S(1)} %get-tuple-element.51), channel_id=1, source_target_pairs={{0,16},{1,5},{4,20},{5,9},{8,24},{9,13},{12,28},{13,1},{16,32},{17... | collective-permute-start | bytes 1228808 | tf_op jit(solution)/shard_map/ppermute | solution.py:50
  85.4 25.6 %collective-permute-start.14 = (bf16[2,160,1280]{2,1,0:T(8,128)(2,1)S(1)}, bf16[2,160,1280]{2,1,0:T(8,128)(2,1)S(1)}, u32[]{:S(2)}, u32[]{:S(2)}) collective-permute-start(bf16[2,160,1280]{2,1,0:T(8,128)(2,1)S(1)} %get-tuple-element.58), channel_id=1, source_target_pairs={{0,4},{1,17},{4,8},{5,21},{8,12},{9,25},{12,0},{13,29},{16,20},{17... | collective-permute-start | bytes 2457608 | tf_op jit(solution)/shard_map/ppermute | solution.py:50
  87.0 24.4 %collective-permute-start.15 = (bf16[2,160,1280]{2,1,0:T(8,128)(2,1)S(1)}, bf16[2,160,1280]{2,1,0:T(8,128)(2,1)S(1)}, u32[]{:S(2)}, u32[]{:S(2)}) collective-permute-start(bf16[2,160,1280]{2,1,0:T(8,128)(2,1)S(1)} %get-tuple-element.60), channel_id=1, source_target_pairs={{0,12},{1,49},{4,0},{5,53},{8,4},{9,57},{12,8},{13,61},{16,28},{17... | collective-permute-start | bytes 2457608 | tf_op jit(solution)/shard_map/ppermute | solution.py:50
  88.7 13.9 %collective-permute-start.8 = (bf16[160,1280]{1,0:T(8,128)(2,1)S(1)}, bf16[160,1280]{1,0:T(8,128)(2,1)S(1)}, u32[]{:S(2)}, u32[]{:S(2)}) collective-permute-start(bf16[160,1280]{1,0:T(8,128)(2,1)S(1)} %get-tuple-element.52), channel_id=1, source_target_pairs={{0,32},{1,9},{4,36},{5,13},{8,40},{9,1},{12,44},{13,5},{16,48},{17... | collective-permute-start | bytes 1228808 | tf_op jit(solution)/shard_map/ppermute | solution.py:50
  92.3 13.5 %collective-permute-start.9 = (bf16[160,1280]{1,0:T(8,128)(2,1)S(1)}, bf16[160,1280]{1,0:T(8,128)(2,1)S(1)}, u32[]{:S(2)}, u32[]{:S(2)}) collective-permute-start(bf16[160,1280]{1,0:T(8,128)(2,1)S(1)} %get-tuple-element.53), channel_id=1, source_target_pairs={{0,48},{1,13},{4,52},{5,1},{8,56},{9,5},{12,60},{13,9},{16,0},{17,... | collective-permute-start | bytes 1228808 | tf_op jit(solution)/shard_map/ppermute | solution.py:50
  93.3 37.2 %collective-permute-start.23 = (bf16[2,3,160,640]{3,2,1,0:T(8,128)(2,1)S(1)}, bf16[2,3,160,640]{3,2,1,0:T(8,128)(2,1)S(1)}, u32[]{:S(2)}, u32[]{:S(2)}) collective-permute-start(bf16[2,3,160,640]{3,2,1,0:T(8,128)(2,1)S(1)} %shard_map.90.here), channel_id=1, source_target_pairs={{0,64},{64,0},{1,65},{65,1},{2,66},{66,2},{3,67},{67,3},{4,68},{68... | collective-permute-start | bytes 3686408 | tf_op jit(solution)/shard_map/ppermute | solution.py:39
  106.5 23.7 %collective-permute-start.10 = (bf16[160,1280]{1,0:T(8,128)(2,1)S(1)}, bf16[160,1280]{1,0:T(8,128)(2,1)S(1)}, u32[]{:S(2)}, u32[]{:S(2)}) collective-permute-start(bf16[160,1280]{1,0:T(8,128)(2,1)S(1)} %shard_map.88.near.one), channel_id=1, source_target_pairs={{0,64},{64,0},{1,65},{65,1},{2,66},{66,2},{3,67},{67,3},{4,68},{68... | collective-permute-start | bytes 1228808 | tf_op jit(solution)/shard_map/ppermute | solution.py:39
  109.3 22.9 %collective-permute-start.13 = (bf16[2,160,1280]{2,1,0:T(8,128)(2,1)S(1)}, bf16[2,160,1280]{2,1,0:T(8,128)(2,1)S(1)}, u32[]{:S(2)}, u32[]{:S(2)}) collective-permute-start(bf16[2,160,1280]{2,1,0:T(8,128)(2,1)S(1)} %get-tuple-element.56), channel_id=1, source_target_pairs={{0,12},{1,49},{4,0},{5,53},{8,4},{9,57},{12,8},{13,61},{16,28},{17... | collective-permute-start | bytes 2457608 | tf_op jit(solution)/shard_map/ppermute | solution.py:50
  111.0 24.3 %collective-permute-start.17 = (bf16[2,160,1280]{2,1,0:T(8,128)(2,1)S(1)}, bf16[2,160,1280]{2,1,0:T(8,128)(2,1)S(1)}, u32[]{:S(2)}, u32[]{:S(2)}) collective-permute-start(bf16[2,160,1280]{2,1,0:T(8,128)(2,1)S(1)} %get-tuple-element.62), channel_id=1, source_target_pairs={{0,4},{1,17},{4,8},{5,21},{8,12},{9,25},{12,0},{13,29},{16,20},{17... | collective-permute-start | bytes 2457608 | tf_op jit(solution)/shard_map/ppermute | solution.py:50
  112.3 24.1 %collective-permute-start.16 = (bf16[2,160,1280]{2,1,0:T(8,128)(2,1)S(1)}, bf16[2,160,1280]{2,1,0:T(8,128)(2,1)S(1)}, u32[]{:S(2)}, u32[]{:S(2)}) collective-permute-start(bf16[2,160,1280]{2,1,0:T(8,128)(2,1)S(1)} %get-tuple-element.61), channel_id=1, source_target_pairs={{0,4},{1,17},{4,8},{5,21},{8,12},{9,25},{12,0},{13,29},{16,20},{17... | collective-permute-start | bytes 2457608 | tf_op jit(solution)/shard_map/ppermute | solution.py:50
  130.3 18.9 %collective-permute-start.18 = (bf16[2,160,1280]{2,1,0:T(8,128)(2,1)S(1)}, bf16[2,160,1280]{2,1,0:T(8,128)(2,1)S(1)}, u32[]{:S(2)}, u32[]{:S(2)}) collective-permute-start(bf16[2,160,1280]{2,1,0:T(8,128)(2,1)S(1)} %get-tuple-element.63), channel_id=1, source_target_pairs={{0,12},{1,49},{4,0},{5,53},{8,4},{9,57},{12,8},{13,61},{16,28},{17... | collective-permute-start | bytes 2457608 | tf_op jit(solution)/shard_map/ppermute | solution.py:50
  132.1 26.3 %collective-permute-start.33 = (bf16[160,1280]{1,0:T(8,128)(2,1)S(1)}, bf16[160,1280]{1,0:T(8,128)(2,1)S(1)}, u32[]{:S(2)}, u32[]{:S(2)}) collective-permute-start(bf16[160,1280]{1,0:T(8,128)(2,1)S(1)} %shard_map.99.refs_0_), channel_id=1, source_target_pairs={{0,16},{1,5},{4,20},{5,9},{8,24},{9,13},{12,28},{13,1},{16,32},{17... | collective-permute-start | bytes 1228808 | tf_op jit(solution)/shard_map/ppermute | solution.py:50
  132.2 28.8 %collective-permute-start.34 = (bf16[160,1280]{1,0:T(8,128)(2,1)S(1)}, bf16[160,1280]{1,0:T(8,128)(2,1)S(1)}, u32[]{:S(2)}, u32[]{:S(2)}) collective-permute-start(bf16[160,1280]{1,0:T(8,128)(2,1)S(1)} %shard_map.99.refs_0_), channel_id=1, source_target_pairs={{0,32},{1,9},{4,36},{5,13},{8,40},{9,1},{12,44},{13,5},{16,48},{17... | collective-permute-start | bytes 1228808 | tf_op jit(solution)/shard_map/ppermute | solution.py:50
  135.3 25.7 %collective-permute-start.35 = (bf16[160,1280]{1,0:T(8,128)(2,1)S(1)}, bf16[160,1280]{1,0:T(8,128)(2,1)S(1)}, u32[]{:S(2)}, u32[]{:S(2)}) collective-permute-start(bf16[160,1280]{1,0:T(8,128)(2,1)S(1)} %shard_map.99.refs_0_), channel_id=1, source_target_pairs={{0,48},{1,13},{4,52},{5,1},{8,56},{9,5},{12,60},{13,9},{16,0},{17,... | collective-permute-start | bytes 1228808 | tf_op jit(solution)/shard_map/ppermute | solution.py:50
  150.8 14.4 %collective-permute-start.19 = (bf16[160,1280]{1,0:T(8,128)(2,1)S(1)}, bf16[160,1280]{1,0:T(8,128)(2,1)S(1)}, u32[]{:S(2)}, u32[]{:S(2)}) collective-permute-start(bf16[160,1280]{1,0:T(8,128)(2,1)S(1)} %get-tuple-element.65), channel_id=1, source_target_pairs={{0,16},{1,5},{4,20},{5,9},{8,24},{9,13},{12,28},{13,1},{16,32},{17... | collective-permute-start | bytes 1228808 | tf_op jit(solution)/shard_map/ppermute | solution.py:50
  152.1 22.8 %collective-permute-start.20 = (bf16[160,1280]{1,0:T(8,128)(2,1)S(1)}, bf16[160,1280]{1,0:T(8,128)(2,1)S(1)}, u32[]{:S(2)}, u32[]{:S(2)}) collective-permute-start(bf16[160,1280]{1,0:T(8,128)(2,1)S(1)} %get-tuple-element.66), channel_id=1, source_target_pairs={{0,32},{1,9},{4,36},{5,13},{8,40},{9,1},{12,44},{13,5},{16,48},{17... | collective-permute-start | bytes 1228808 | tf_op jit(solution)/shard_map/ppermute | solution.py:50
  158.4 16.5 %collective-permute-start.21 = (bf16[160,1280]{1,0:T(8,128)(2,1)S(1)}, bf16[160,1280]{1,0:T(8,128)(2,1)S(1)}, u32[]{:S(2)}, u32[]{:S(2)}) collective-permute-start(bf16[160,1280]{1,0:T(8,128)(2,1)S(1)} %get-tuple-element.67), channel_id=1, source_target_pairs={{0,48},{1,13},{4,52},{5,1},{8,56},{9,5},{12,60},{13,9},{16,0},{17,... | collective-permute-start | bytes 1228808 | tf_op jit(solution)/shard_map/ppermute | solution.py:50
  161.7 29.1 %collective-permute-start.36 = (bf16[2,160,1280]{2,1,0:T(8,128)(2,1)S(1)}, bf16[2,160,1280]{2,1,0:T(8,128)(2,1)S(1)}, u32[]{:S(2)}, u32[]{:S(2)}) collective-permute-start(bf16[2,160,1280]{2,1,0:T(8,128)(2,1)S(1)} %get-tuple-element.76.refs_0_), channel_id=1, source_target_pairs={{0,4},{1,17},{4,8},{5,21},{8,12},{9,25},{12,0},{13,29},{16,20},{17... | collective-permute-start | bytes 2457608 | tf_op jit(solution)/shard_map/ppermute | solution.py:50
  175.6 9.5 %collective-permute-start.22 = (bf16[160,1280]{1,0:T(8,128)(2,1)S(1)}, bf16[160,1280]{1,0:T(8,128)(2,1)S(1)}, u32[]{:S(2)}, u32[]{:S(2)}) collective-permute-start(bf16[160,1280]{1,0:T(8,128)(2,1)S(1)} %shard_map.95.far.one), channel_id=1, source_target_pairs={{0,64},{64,0},{1,65},{65,1},{2,66},{66,2},{3,67},{67,3},{4,68},{68... | collective-permute-start | bytes 1228808 | tf_op jit(solution)/shard_map/ppermute | solution.py:39
  178.5 36.0 %collective-permute-start.38 = (bf16[2,160,1280]{2,1,0:T(8,128)(2,1)S(1)}, bf16[2,160,1280]{2,1,0:T(8,128)(2,1)S(1)}, u32[]{:S(2)}, u32[]{:S(2)}) collective-permute-start(bf16[2,160,1280]{2,1,0:T(8,128)(2,1)S(1)} %get-tuple-element.77.refs_1_), channel_id=1, source_target_pairs={{0,12},{1,49},{4,0},{5,53},{8,4},{9,57},{12,8},{13,61},{16,28},{17... | collective-permute-start | bytes 2457608 | tf_op jit(solution)/shard_map/ppermute | solution.py:50
  186.8 16.2 %collective-permute-start.24 = (bf16[160,1280]{1,0:T(8,128)(2,1)S(1)}, bf16[160,1280]{1,0:T(8,128)(2,1)S(1)}, u32[]{:S(2)}, u32[]{:S(2)}) collective-permute-start(bf16[160,1280]{1,0:T(8,128)(2,1)S(1)} %shard_map.97.refs_0_), channel_id=1, source_target_pairs={{0,16},{1,5},{4,20},{5,9},{8,24},{9,13},{12,28},{13,1},{16,32},{17... | collective-permute-start | bytes 1228808 | tf_op jit(solution)/shard_map/ppermute | solution.py:50
  186.8 19.7 %collective-permute-start.25 = (bf16[160,1280]{1,0:T(8,128)(2,1)S(1)}, bf16[160,1280]{1,0:T(8,128)(2,1)S(1)}, u32[]{:S(2)}, u32[]{:S(2)}) collective-permute-start(bf16[160,1280]{1,0:T(8,128)(2,1)S(1)} %shard_map.97.refs_0_), channel_id=1, source_target_pairs={{0,32},{1,9},{4,36},{5,13},{8,40},{9,1},{12,44},{13,5},{16,48},{17... | collective-permute-start | bytes 1228808 | tf_op jit(solution)/shard_map/ppermute | solution.py:50
  188.2 25.4 %collective-permute-start.26 = (bf16[160,1280]{1,0:T(8,128)(2,1)S(1)}, bf16[160,1280]{1,0:T(8,128)(2,1)S(1)}, u32[]{:S(2)}, u32[]{:S(2)}) collective-permute-start(bf16[160,1280]{1,0:T(8,128)(2,1)S(1)} %shard_map.97.refs_0_), channel_id=1, source_target_pairs={{0,48},{1,13},{4,52},{5,1},{8,56},{9,5},{12,60},{13,9},{16,0},{17,... | collective-permute-start | bytes 1228808 | tf_op jit(solution)/shard_map/ppermute | solution.py:50
  190.8 26.9 %collective-permute-start.40 = (bf16[2,160,1280]{2,1,0:T(8,128)(2,1)S(1)}, bf16[2,160,1280]{2,1,0:T(8,128)(2,1)S(1)}, u32[]{:S(2)}, u32[]{:S(2)}) collective-permute-start(bf16[2,160,1280]{2,1,0:T(8,128)(2,1)S(1)} %get-tuple-element.77.refs_1_), channel_id=1, source_target_pairs={{0,4},{1,17},{4,8},{5,21},{8,12},{9,25},{12,0},{13,29},{16,20},{17... | collective-permute-start | bytes 2457608 | tf_op jit(solution)/shard_map/ppermute | solution.py:50
  203.0 14.8 %collective-permute-start.41 = (bf16[2,160,1280]{2,1,0:T(8,128)(2,1)S(1)}, bf16[2,160,1280]{2,1,0:T(8,128)(2,1)S(1)}, u32[]{:S(2)}, u32[]{:S(2)}) collective-permute-start(bf16[2,160,1280]{2,1,0:T(8,128)(2,1)S(1)} %get-tuple-element.76.refs_0_), channel_id=1, source_target_pairs={{0,12},{1,49},{4,0},{5,53},{8,4},{9,57},{12,8},{13,61},{16,28},{17... | collective-permute-start | bytes 2457608 | tf_op jit(solution)/shard_map/ppermute | solution.py:50
  206.5 17.0 %collective-permute-start.37 = (bf16[2,160,1280]{2,1,0:T(8,128)(2,1)S(1)}, bf16[2,160,1280]{2,1,0:T(8,128)(2,1)S(1)}, u32[]{:S(2)}, u32[]{:S(2)}) collective-permute-start(bf16[2,160,1280]{2,1,0:T(8,128)(2,1)S(1)} %collective-permute-done.36.refs_2_), channel_id=1, source_target_pairs={{0,4},{1,17},{4,8},{5,21},{8,12},{9,25},{12,0},{13,29},{16,20},{17... | collective-permute-start | bytes 2457608 | tf_op jit(solution)/shard_map/ppermute | solution.py:50
  214.4 17.9 %collective-permute-start.27 = (bf16[2,160,1280]{2,1,0:T(8,128)(2,1)S(1)}, bf16[2,160,1280]{2,1,0:T(8,128)(2,1)S(1)}, u32[]{:S(2)}, u32[]{:S(2)}) collective-permute-start(bf16[2,160,1280]{2,1,0:T(8,128)(2,1)S(1)} %get-tuple-element.72.refs_0_), channel_id=1, source_target_pairs={{0,4},{1,17},{4,8},{5,21},{8,12},{9,25},{12,0},{13,29},{16,20},{17... | collective-permute-start | bytes 2457608 | tf_op jit(solution)/shard_map/ppermute | solution.py:50
  214.5 20.3 %collective-permute-start.29 = (bf16[2,160,1280]{2,1,0:T(8,128)(2,1)S(1)}, bf16[2,160,1280]{2,1,0:T(8,128)(2,1)S(1)}, u32[]{:S(2)}, u32[]{:S(2)}) collective-permute-start(bf16[2,160,1280]{2,1,0:T(8,128)(2,1)S(1)} %get-tuple-element.73.refs_1_), channel_id=1, source_target_pairs={{0,12},{1,49},{4,0},{5,53},{8,4},{9,57},{12,8},{13,61},{16,28},{17... | collective-permute-start | bytes 2457608 | tf_op jit(solution)/shard_map/ppermute | solution.py:50
  217.7 23.8 %collective-permute-start.39 = (bf16[2,160,1280]{2,1,0:T(8,128)(2,1)S(1)}, bf16[2,160,1280]{2,1,0:T(8,128)(2,1)S(1)}, u32[]{:S(2)}, u32[]{:S(2)}) collective-permute-start(bf16[2,160,1280]{2,1,0:T(8,128)(2,1)S(1)} %collective-permute-done.38.refs_3_), channel_id=1, source_target_pairs={{0,12},{1,49},{4,0},{5,53},{8,4},{9,57},{12,8},{13,61},{16,28},{17... | collective-permute-start | bytes 2457608 | tf_op jit(solution)/shard_map/ppermute | solution.py:50
  217.8 25.5 %collective-permute-start.31 = (bf16[2,160,1280]{2,1,0:T(8,128)(2,1)S(1)}, bf16[2,160,1280]{2,1,0:T(8,128)(2,1)S(1)}, u32[]{:S(2)}, u32[]{:S(2)}) collective-permute-start(bf16[2,160,1280]{2,1,0:T(8,128)(2,1)S(1)} %get-tuple-element.73.refs_1_), channel_id=1, source_target_pairs={{0,4},{1,17},{4,8},{5,21},{8,12},{9,25},{12,0},{13,29},{16,20},{17... | collective-permute-start | bytes 2457608 | tf_op jit(solution)/shard_map/ppermute | solution.py:50
  223.5 21.6 %collective-permute-start.32 = (bf16[2,160,1280]{2,1,0:T(8,128)(2,1)S(1)}, bf16[2,160,1280]{2,1,0:T(8,128)(2,1)S(1)}, u32[]{:S(2)}, u32[]{:S(2)}) collective-permute-start(bf16[2,160,1280]{2,1,0:T(8,128)(2,1)S(1)} %get-tuple-element.72.refs_0_), channel_id=1, source_target_pairs={{0,12},{1,49},{4,0},{5,53},{8,4},{9,57},{12,8},{13,61},{16,28},{17... | collective-permute-start | bytes 2457608 | tf_op jit(solution)/shard_map/ppermute | solution.py:50
  232.3 17.6 %collective-permute-start.28 = (bf16[2,160,1280]{2,1,0:T(8,128)(2,1)S(1)}, bf16[2,160,1280]{2,1,0:T(8,128)(2,1)S(1)}, u32[]{:S(2)}, u32[]{:S(2)}) collective-permute-start(bf16[2,160,1280]{2,1,0:T(8,128)(2,1)S(1)} %collective-permute-done.27.refs_2_), channel_id=1, source_target_pairs={{0,4},{1,17},{4,8},{5,21},{8,12},{9,25},{12,0},{13,29},{16,20},{17... | collective-permute-start | bytes 2457608 | tf_op jit(solution)/shard_map/ppermute | solution.py:50
  234.8 19.1 %collective-permute-start.30 = (bf16[2,160,1280]{2,1,0:T(8,128)(2,1)S(1)}, bf16[2,160,1280]{2,1,0:T(8,128)(2,1)S(1)}, u32[]{:S(2)}, u32[]{:S(2)}) collective-permute-start(bf16[2,160,1280]{2,1,0:T(8,128)(2,1)S(1)} %collective-permute-done.29.refs_3_), channel_id=1, source_target_pairs={{0,12},{1,49},{4,0},{5,53},{8,4},{9,57},{12,8},{13,61},{16,28},{17... | collective-permute-start | bytes 2457608 | tf_op jit(solution)/shard_map/ppermute | solution.py:50

commit v3 on v2

--- a/solution.py
+++ b/solution.py
@@ -206,11 +206,11 @@
     far_up, far_down, hold_up, hold_down, own, near_up, near_down = messages
     far_up, far_down = ring(far_up, 0, 1), ring(far_down, 0, -1)
     near_up, near_down = ring(near_up, 0, 1), ring(near_down, 0, -1)
-    last_up, last_down = pass_on(place, hold_up, far_up, hold_down, far_down)
+    last_up, last_down = passed = pass_on(place, hold_up, far_up, hold_down, far_down)
     last_up, last_down = ring(last_up, 0, 1), ring(last_down, 0, -1)
     keep, *sent = finish(place, own, near_down, last_up, near_up, last_down)
     got = [ring(block, 1, k + 1) for k, block in enumerate(sent)]
-    return call(total_kernel, place, (keep, *got), [shape(ROWS, COLS)])[0], sent[0]
+    return call(total_kernel, place, (keep, *got), [shape(ROWS, COLS)])[0], passed[0], sent[0]
 
 
 def adam_update(weights, first_moment, second_moment, gradient):
@@ -372,14 +372,14 @@
     flat = sent_state(place, (weights, first_moment, second_moment))
     here = moved_state(place, flat)
     messages = products(place, cotangent, activations, beside)
-    near, sent = reduced(place, messages)
-
-    across, here, _ = lax.optimization_barrier((across, here, sent))
+    near, passed, _ = reduced(place, messages)
+
+    across, here, _ = lax.optimization_barrier((across, here, passed))
     there = shift(here, "xh", 1)
     messages = products(place, cotangent, across, shift(across, "c", 1))
     near_got = shift(near, "xh", 1)
     near_line = lines(place, adam(place, True, (near, near_got), (here, there)))
-    far, sent = reduced(place, messages)
+    far, _, sent = reduced(place, messages)
 
     *near_line, _ = lax.optimization_barrier((*near_line, sent))
     out = gathered(place, near_line, True)

time: 257 us -> 249 us (0.969)
  waiting for transfers between devices: 101 us -> 91.8 us
  starting transfers between devices: 88.2 us -> 91.4 us
    ppermute x36, waiting for transfers between devices: 76.8 us -> 67.1 us  [ring(): return lax.ppermute(value, ('z', 'y', 'c'), pairs)]
    ppermute x36, starting transfers between devices: 70.6 us -> 75.3 us  [ring(): return lax.ppermute(value, ('z', 'y', 'c'), pairs)]
    ppermute x6, waiting for transfers between devices: 21.1 us -> 24.7 us  [shift(): lax.ppermute(value, axis, [(i, (i + step) % count) for i in range(count)])]
    all_to_all x1, waiting for transfers between devices: 3.14 us -> 0.01 us  [moved_state(): got = lax.all_to_all(flat, ('z', 'y'), 0, 0, tiled=True)]
    ppermute x6, starting transfers between devices: 10.8 us -> 8.05 us  [shift(): lax.ppermute(value, axis, [(i, (i + step) % count) for i in range(count)])]
    unnamed x30 -> x28, local copies, waits for them, and re-layouts: 10 us -> 10.2 us
  transfers between devices with their start and end apart: 43 -> 43, of which waited for: 18 -> 16; matrix products, arithmetic and copies ran while one was open for 0% -> 0% of each run, Pallas kernels for 21% -> 21%
where the time goes in v3:
time: 249 us; the launch traced here: 248 us
  waiting for transfers between devices  91.8 us (37%)
  starting transfers between devices  91.4 us (37%)
  Pallas kernels  53 us (21%)
  local copies, waits for them, and re-layouts  10.3 us (4%)
    ppermute x36, starting transfers between devices, ring(): return lax.ppermute(value, ('z', 'y', 'c'), pairs)  75.3 us
    ppermute x36, waiting for transfers between devices, ring(): return lax.ppermute(value, ('z', 'y', 'c'), pairs)  67.1 us
    pallas_call x21, Pallas kernels, call(): pl.pallas_call(kernel, out_shape=outs, in_specs=[pl.BlockSpec(memory_spac...  53 us
    ppermute x6, waiting for transfers between devices, shift(): lax.ppermute(value, axis, [(i, (i + step) % count) for i in range(count)])  24.7 us
    unnamed x28, local copies, waits for them, and re-layouts  10.2 us
    all_to_all x1, starting transfers between devices, moved_state(): got = lax.all_to_all(flat, ('z', 'y'), 0, 0, tiled=True)  8.09 us
    ppermute x6, starting transfers between devices, shift(): lax.ppermute(value, axis, [(i, (i + step) % count) for i in range(count)])  8.05 us
  transfers between devices with their start and end apart: 43, of which 16 were waited for; matrix products, arithmetic and copies ran while one was open for 0% of the time, Pallas kernels for 21%

profile of v3, /device:TPU:0, one launch (start us, length us, event | category | flops | bytes accessed | tf_op | source)
XLA Modules:
  0.0 247.7 jit_solution(10070028058405622533)
XLA Ops:
  0.7 1.7 collective-permute-start.11
  2.5 1.1 copy-done.7
  3.6 1.1 copy-done.8
  4.8 1.1 copy-done.9
  5.9 1.5 shard_map.89
  7.4 1.2 copy-done.1
  8.6 8.1 %all-to-all-start = ((bf16[16,2,40,480]{3,2,1,0:T(8,128)(2,1)}), bf16[16,2,40,480]{3,2,1,0:T(8,128)(2,1)}, u32[]{:S(2)}, u32[]{:S(2)}) async-start(bf16[16,2,40,480]{3,2,1,0:T(8,128)(2,1)} %copy-done.1), calls=%async_computation | async-start | bytes 2621440 | tf_op jit(solution)/shard_map/all_to_all | solution.py:359
  16.7 1.7 copy-done.2
  18.4 4.4 %shard_map.84.made = bf16[2,4,160,1280]{3,2,1,0:T(8,128)(2,1)S(1)} custom-call(s32[7]{0:T(128)S(1)} %stack.31.place, bf16[1024,1280]{1,0:T(8,128)(2,1)S(1)} %copy-done.2, bf16[1024,1280]{1,0:T(8,128)(2,1)S(1)} %copy-done), custom_call_target="tpu_custom_call" | custom-call | tf_op jit(solution)/shard_map/pallas_call | solution.py:61
  22.8 8.7 %shard_map.85 = (bf16[2,160,1280]{2,1,0:T(8,128)(2,1)}, bf16[2,160,1280]{2,1,0:T(8,128)(2,1)}, bf16[2,160,1280]{2,1,0:T(8,128)(2,1)S(1)}, bf16[2,160,1280]{2,1,0...) custom-call(s32[7]{0:T(128)S(1)} %stack.31.place, ...), custom_call_target="tpu_custom_call" | custom-call | tf_op jit(solution)/shard_map/pallas_call | solution.py:61
  31.6 1.2 copy-done.3
  32.7 0.9 copy-done.5
  33.6 0.9 copy-done.10
  34.5 0.9 copy-done.12
  35.4 1.9 collective-permute-start.2
  37.3 1.4 collective-permute-start.3
  38.7 2.1 shard_map.90.here
  40.7 8.5 %collective-permute-done.2.refs_1_ = bf16[2,160,1280]{2,1,0:T(8,128)(2,1)} collective-permute-done((bf16[2,160,1280]{2,1,0:T(8,128)(2,1)}, bf16[2,160,1280]{2,1,0:T(8,128)(2,1)}, u32[]{:S(2)}, u32[]{:S(2)}) %collective-permute-start.2) | collective-permute-done | bytes 819232 | tf_op jit(solution)/shard_map/ppermute | solution.py:50
  50.0 1.8 shard_map.86
  51.8 8.5 %collective-permute-done.11.features = bf16[1024,1280]{1,0:T(8,128)(2,1)} collective-permute-done((bf16[1024,1280]{1,0:T(8,128)(2,1)}, bf16[1024,1280]{1,0:T(8,128)(2,1)}, u32[]{:S(2)}, u32[]{:S(2)}) %collective-permute-start.11) | collective-permute-done | bytes 2621472 | tf_op jit(solution)/shard_map/ppermute | solution.py:39
  60.3 3.1 %collective-permute-start.1 = (bf16[2,160,1280]{2,1,0:T(8,128)(2,1)S(1)}, bf16[2,160,1280]{2,1,0:T(8,128)(2,1)S(1)}, u32[]{:S(2)}, u32[]{:S(2)}) collective-permute-start(bf16[2,160,1280]{2,1,0:T(8,128)(2,1)S(1)} %copy-done.13), channel_id=1, source_target_pairs={{0,12},{1,49},{4,0},{5,53},{8,4},{9,57},{12,8},{13,61},{16,28},{17... | collective-permute-start | bytes 2457608 | tf_op jit(solution)/shard_map/ppermute | solution.py:50
  64.0 2.7 %collective-permute-start.6 = (bf16[2,160,1280]{2,1,0:T(8,128)(2,1)S(1)}, bf16[2,160,1280]{2,1,0:T(8,128)(2,1)S(1)}, u32[]{:S(2)}, u32[]{:S(2)}) collective-permute-start(bf16[2,160,1280]{2,1,0:T(8,128)(2,1)S(1)} %get-tuple-element.49), channel_id=1, source_target_pairs={{0,12},{1,49},{4,0},{5,53},{8,4},{9,57},{12,8},{13,61},{16,28},{17... | collective-permute-start | bytes 2457608 | tf_op jit(solution)/shard_map/ppermute | solution.py:50
  66.7 5.6 %shard_map.91.made = bf16[2,4,160,1280]{3,2,1,0:T(8,128)(2,1)S(1)} custom-call(s32[7]{0:T(128)S(1)} %stack.31.place, bf16[1024,1280]{1,0:T(8,128)(2,1)} %collective-permute-done.11.features, bf16[1024,1280]{1,0:T(8,128)(2,1)S(1)} %copy-done), custom_call_target="tpu_custom_call" | custom-call | tf_op jit(solution)/shard_map/pallas_call | solution.py:61
  72.3 6.5 %shard_map.92 = (bf16[2,160,1280]{2,1,0:T(8,128)(2,1)S(1)}, bf16[2,160,1280]{2,1,0:T(8,128)(2,1)S(1)}, bf16[2,160,1280]{2,1,0:T(8,128)(2,1)S(1)}, bf16[2,160,128...) custom-call(s32[7]{0:T(128)S(1)} %stack.31.place, ...), custom_call_target="tpu_custom_call" | custom-call | tf_op jit(solution)/shard_map/pallas_call | solution.py:61
  79.0 3.1 %collective-permute-start.23 = (bf16[2,3,160,640]{3,2,1,0:T(8,128)(2,1)S(1)}, bf16[2,3,160,640]{3,2,1,0:T(8,128)(2,1)S(1)}, u32[]{:S(2)}, u32[]{:S(2)}) collective-permute-start(bf16[2,3,160,640]{3,2,1,0:T(8,128)(2,1)S(1)} %shard_map.90.here), channel_id=1, source_target_pairs={{0,64},{64,0},{1,65},{65,1},{2,66},{66,2},{3,67},{67,3},{4,68},{68... | collective-permute-start | bytes 3686408 | tf_op jit(solution)/shard_map/ppermute | solution.py:39
  82.1 3.1 %collective-permute-start.15 = (bf16[2,160,1280]{2,1,0:T(8,128)(2,1)S(1)}, bf16[2,160,1280]{2,1,0:T(8,128)(2,1)S(1)}, u32[]{:S(2)}, u32[]{:S(2)}) collective-permute-start(bf16[2,160,1280]{2,1,0:T(8,128)(2,1)S(1)} %get-tuple-element.60), channel_id=1, source_target_pairs={{0,12},{1,49},{4,0},{5,53},{8,4},{9,57},{12,8},{13,61},{16,28},{17... | collective-permute-start | bytes 2457608 | tf_op jit(solution)/shard_map/ppermute | solution.py:50
  85.8 1.6 shard_map.87
  87.4 2.0 collective-permute-start.7
  89.4 3.6 %collective-permute-start.8 = (bf16[160,1280]{1,0:T(8,128)(2,1)S(1)}, bf16[160,1280]{1,0:T(8,128)(2,1)S(1)}, u32[]{:S(2)}, u32[]{:S(2)}) collective-permute-start(bf16[160,1280]{1,0:T(8,128)(2,1)S(1)} %get-tuple-element.52), channel_id=1, source_target_pairs={{0,32},{1,9},{4,36},{5,13},{8,40},{9,1},{12,44},{13,5},{16,48},{17... | collective-permute-start | bytes 1228808 | tf_op jit(solution)/shard_map/ppermute | solution.py:50
  93.0 4.4 %collective-permute-done.14.refs_1_ = bf16[2,160,1280]{2,1,0:T(8,128)(2,1)S(1)} collective-permute-done((bf16[2,160,1280]{2,1,0:T(8,128)(2,1)S(1)}, bf16[2,160,1280]{2,1,0:T(8,128)(2,1)S(1)}, u32[]{:S(2)}, u32[]{:S(2)}) %collective-permute-start.14) | collective-permute-done | bytes 819232 | tf_op jit(solution)/shard_map/ppermute | solution.py:50
  97.4 10.0 %collective-permute-start.9 = (bf16[160,1280]{1,0:T(8,128)(2,1)S(1)}, bf16[160,1280]{1,0:T(8,128)(2,1)S(1)}, u32[]{:S(2)}, u32[]{:S(2)}) collective-permute-start(bf16[160,1280]{1,0:T(8,128)(2,1)S(1)} %get-tuple-element.53), channel_id=1, source_target_pairs={{0,48},{1,13},{4,52},{5,1},{8,56},{9,5},{12,60},{13,9},{16,0},{17,... | collective-permute-start | bytes 1228808 | tf_op jit(solution)/shard_map/ppermute | solution.py:50
  107.4 0.9 shard_map.93
  108.3 2.1 collective-permute-start.17
  110.5 6.7 %collective-permute-done.9.three = bf16[160,1280]{1,0:T(8,128)(2,1)S(1)} collective-permute-done((bf16[160,1280]{1,0:T(8,128)(2,1)S(1)}, bf16[160,1280]{1,0:T(8,128)(2,1)S(1)}, u32[]{:S(2)}, u32[]{:S(2)}) %collective-permute-start.9) | collective-permute-done | bytes 409632 | tf_op jit(solution)/shard_map/ppermute | solution.py:50
  117.2 0.8 shard_map.88.near.one
  118.0 3.1 %collective-permute-start.10 = (bf16[160,1280]{1,0:T(8,128)(2,1)S(1)}, bf16[160,1280]{1,0:T(8,128)(2,1)S(1)}, u32[]{:S(2)}, u32[]{:S(2)}) collective-permute-start(bf16[160,1280]{1,0:T(8,128)(2,1)S(1)} %shard_map.88.near.one), channel_id=1, source_target_pairs={{0,64},{64,0},{1,65},{65,1},{2,66},{66,2},{3,67},{67,3},{4,68},{68... | collective-permute-start | bytes 1228808 | tf_op jit(solution)/shard_map/ppermute | solution.py:39
  121.1 6.8 %collective-permute-done.10.near_got.two = bf16[160,1280]{1,0:T(8,128)(2,1)S(1)} collective-permute-done((bf16[160,1280]{1,0:T(8,128)(2,1)S(1)}, bf16[160,1280]{1,0:T(8,128)(2,1)S(1)}, u32[]{:S(2)}, u32[]{:S(2)}) %collective-permute-start.10) | collective-permute-done | bytes 409632 | tf_op jit(solution)/shard_map/ppermute | solution.py:39
  127.9 1.6 shard_map.99.refs_0_
  129.5 1.8 collective-permute-start.33
  131.3 3.1 %collective-permute-start.34 = (bf16[160,1280]{1,0:T(8,128)(2,1)S(1)}, bf16[160,1280]{1,0:T(8,128)(2,1)S(1)}, u32[]{:S(2)}, u32[]{:S(2)}) collective-permute-start(bf16[160,1280]{1,0:T(8,128)(2,1)S(1)} %shard_map.99.refs_0_), channel_id=1, source_target_pairs={{0,32},{1,9},{4,36},{5,13},{8,40},{9,1},{12,44},{13,5},{16,48},{17... | collective-permute-start | bytes 1228808 | tf_op jit(solution)/shard_map/ppermute | solution.py:50
  134.4 1.6 shard_map.94
  136.0 2.1 collective-permute-start.19
  138.1 15.8 %collective-permute-start.20 = (bf16[160,1280]{1,0:T(8,128)(2,1)S(1)}, bf16[160,1280]{1,0:T(8,128)(2,1)S(1)}, u32[]{:S(2)}, u32[]{:S(2)}) collective-permute-start(bf16[160,1280]{1,0:T(8,128)(2,1)S(1)} %get-tuple-element.66), channel_id=1, source_target_pairs={{0,32},{1,9},{4,36},{5,13},{8,40},{9,1},{12,44},{13,5},{16,48},{17... | collective-permute-start | bytes 1228808 | tf_op jit(solution)/shard_map/ppermute | solution.py:50
  153.9 2.5 %collective-permute-start.21 = (bf16[160,1280]{1,0:T(8,128)(2,1)S(1)}, bf16[160,1280]{1,0:T(8,128)(2,1)S(1)}, u32[]{:S(2)}, u32[]{:S(2)}) collective-permute-start(bf16[160,1280]{1,0:T(8,128)(2,1)S(1)} %get-tuple-element.67), channel_id=1, source_target_pairs={{0,48},{1,13},{4,52},{5,1},{8,56},{9,5},{12,60},{13,9},{16,0},{17,... | collective-permute-start | bytes 1228808 | tf_op jit(solution)/shard_map/ppermute | solution.py:50
  157.2 6.9 %collective-permute-done.20.two = bf16[160,1280]{1,0:T(8,128)(2,1)S(1)} collective-permute-done((bf16[160,1280]{1,0:T(8,128)(2,1)S(1)}, bf16[160,1280]{1,0:T(8,128)(2,1)S(1)}, u32[]{:S(2)}, u32[]{:S(2)}) %collective-permute-start.20) | collective-permute-done | bytes 409632 | tf_op jit(solution)/shard_map/ppermute | solution.py:50
  164.1 4.1 %collective-permute-done.21.three = bf16[160,1280]{1,0:T(8,128)(2,1)S(1)} collective-permute-done((bf16[160,1280]{1,0:T(8,128)(2,1)S(1)}, bf16[160,1280]{1,0:T(8,128)(2,1)S(1)}, u32[]{:S(2)}, u32[]{:S(2)}) %collective-permute-start.21) | collective-permute-done | bytes 409632 | tf_op jit(solution)/shard_map/ppermute | solution.py:50
  169.1 9.4 %collective-permute-done.22.far_got.two = bf16[160,1280]{1,0:T(8,128)(2,1)S(1)} collective-permute-done((bf16[160,1280]{1,0:T(8,128)(2,1)S(1)}, bf16[160,1280]{1,0:T(8,128)(2,1)S(1)}, u32[]{:S(2)}, u32[]{:S(2)}) %collective-permute-start.22) | collective-permute-done | bytes 409632 | tf_op jit(solution)/shard_map/ppermute | solution.py:39
  178.4 1.6 shard_map.97.refs_0_
  180.4 6.0 %collective-permute-start.25 = (bf16[160,1280]{1,0:T(8,128)(2,1)S(1)}, bf16[160,1280]{1,0:T(8,128)(2,1)S(1)}, u32[]{:S(2)}, u32[]{:S(2)}) collective-permute-start(bf16[160,1280]{1,0:T(8,128)(2,1)S(1)} %shard_map.97.refs_0_), channel_id=1, source_target_pairs={{0,32},{1,9},{4,36},{5,13},{8,40},{9,1},{12,44},{13,5},{16,48},{17... | collective-permute-start | bytes 1228808 | tf_op jit(solution)/shard_map/ppermute | solution.py:50
  186.5 2.5 %collective-permute-start.26 = (bf16[160,1280]{1,0:T(8,128)(2,1)S(1)}, bf16[160,1280]{1,0:T(8,128)(2,1)S(1)}, u32[]{:S(2)}, u32[]{:S(2)}) collective-permute-start(bf16[160,1280]{1,0:T(8,128)(2,1)S(1)} %shard_map.97.refs_0_), channel_id=1, source_target_pairs={{0,48},{1,13},{4,52},{5,1},{8,56},{9,5},{12,60},{13,9},{16,0},{17,... | collective-permute-start | bytes 1228808 | tf_op jit(solution)/shard_map/ppermute | solution.py:50
  189.0 5.8 %collective-permute-done.24.refs_1_ = bf16[160,1280]{1,0:T(8,128)(2,1)S(1)} collective-permute-done((bf16[160,1280]{1,0:T(8,128)(2,1)S(1)}, bf16[160,1280]{1,0:T(8,128)(2,1)S(1)}, u32[]{:S(2)}, u32[]{:S(2)}) %collective-permute-start.24) | collective-permute-done | bytes 409632 | tf_op jit(solution)/shard_map/ppermute | solution.py:50
  194.8 1.4 collective-permute-start.41
  196.2 9.3 %collective-permute-done.25.refs_2_ = bf16[160,1280]{1,0:T(8,128)(2,1)S(1)} collective-permute-done((bf16[160,1280]{1,0:T(8,128)(2,1)S(1)}, bf16[160,1280]{1,0:T(8,128)(2,1)S(1)}, u32[]{:S(2)}, u32[]{:S(2)}) %collective-permute-start.25) | collective-permute-done | bytes 409632 | tf_op jit(solution)/shard_map/ppermute | solution.py:50
  206.3 3.3 %collective-permute-start.29 = (bf16[2,160,1280]{2,1,0:T(8,128)(2,1)S(1)}, bf16[2,160,1280]{2,1,0:T(8,128)(2,1)S(1)}, u32[]{:S(2)}, u32[]{:S(2)}) collective-permute-start(bf16[2,160,1280]{2,1,0:T(8,128)(2,1)S(1)} %get-tuple-element.73.refs_1_), channel_id=1, source_target_pairs={{0,12},{1,49},{4,0},{5,53},{8,4},{9,57},{12,8},{13,61},{16,28},{17... | collective-permute-start | bytes 2457608 | tf_op jit(solution)/shard_map/ppermute | solution.py:50
  209.6 1.9 collective-permute-start.39
  211.6 7.4 %collective-permute-done.37.refs_0_ = bf16[2,160,1280]{2,1,0:T(8,128)(2,1)S(1)} collective-permute-done((bf16[2,160,1280]{2,1,0:T(8,128)(2,1)S(1)}, bf16[2,160,1280]{2,1,0:T(8,128)(2,1)S(1)}, u32[]{:S(2)}, u32[]{:S(2)}) %collective-permute-start.37) | collective-permute-done | bytes 819232 | tf_op jit(solution)/shard_map/ppermute | solution.py:50
  219.2 8.6 %collective-permute-done.27.refs_2_ = bf16[2,160,1280]{2,1,0:T(8,128)(2,1)S(1)} collective-permute-done((bf16[2,160,1280]{2,1,0:T(8,128)(2,1)S(1)}, bf16[2,160,1280]{2,1,0:T(8,128)(2,1)S(1)}, u32[]{:S(2)}, u32[]{:S(2)}) %collective-permute-start.27) | collective-permute-done | bytes 819232 | tf_op jit(solution)/shard_map/ppermute | solution.py:50
  227.8 3.2 %collective-permute-start.30 = (bf16[2,160,1280]{2,1,0:T(8,128)(2,1)S(1)}, bf16[2,160,1280]{2,1,0:T(8,128)(2,1)S(1)}, u32[]{:S(2)}, u32[]{:S(2)}) collective-permute-start(bf16[2,160,1280]{2,1,0:T(8,128)(2,1)S(1)} %collective-permute-done.29.refs_3_), channel_id=1, source_target_pairs={{0,12},{1,49},{4,0},{5,53},{8,4},{9,57},{12,8},{13,61},{16,28},{17... | collective-permute-start | bytes 2457608 | tf_op jit(solution)/shard_map/ppermute | solution.py:50
  231.1 3.1 %shard_map.96 = (f32[160,1280]{1,0:T(8,128)}, f32[160,1280]{1,0:T(8,128)}, f32[160,1280]{1,0:T(8,128)}) custom-call(s32[7]{0:T(128)S(1)} %stack.31.place, bf16[160,1280]{1,0:T(8,128)(2,1)S(1)} %shard_map.88.near.one, bf16[160,1280]{1,0:T(8,128)(2,1)S(1)} %collective-permute-done.10.near_got.two, bf16[160,1280]{1,0:T(8,128)(2,1)S(1)} %shard_map.95.far.one, ...), custom_call_target="tpu_custom_call" | custom-call | tf_op jit(solution)/shard_map/pallas_call | solution.py:61
  234.2 2.8 %shard_map.101.refs_2_ = bf16[2,4,4,160,1280]{4,3,2,1,0:T(8,128)(2,1)} custom-call(s32[7]{0:T(128)S(1)} %stack.31.place, bf16[2,160,1280]{2,1,0:T(8,128)(2,1)S(1)} %get-tuple-element.76.refs_0_, bf16[2,160,1280]{2,1,0:T(8,128)(2,1)S(1)} %get-tuple-element.77.refs_1_, bf16[2,160,1280]{2,1,0:T(8,128)(2,1)S(1)} %collective-permute-done.36.refs_2_, ...), custom_call_target="tpu_custom_call" | custom-call | tf_op jit(solution)/shard_map/pallas_call | solution.py:61
  237.0 1.7 shard_map.102.refs_6_
  238.8 2.8 %shard_map.103.refs_2_ = bf16[2,4,4,160,1280]{4,3,2,1,0:T(8,128)(2,1)} custom-call(s32[7]{0:T(128)S(1)} %stack.31.place, bf16[2,160,1280]{2,1,0:T(8,128)(2,1)S(1)} %get-tuple-element.72.refs_0_, bf16[2,160,1280]{2,1,0:T(8,128)(2,1)S(1)} %get-tuple-element.73.refs_1_, ...), custom_call_target="tpu_custom_call", output_to_operand_aliasing={{}: (7, {})} | custom-call | tf_op jit(solution)/shard_map/pallas_call | solution.py:61
  241.6 3.8 %collective-permute-done.28.refs_0_ = bf16[2,160,1280]{2,1,0:T(8,128)(2,1)S(1)} collective-permute-done((bf16[2,160,1280]{2,1,0:T(8,128)(2,1)S(1)}, bf16[2,160,1280]{2,1,0:T(8,128)(2,1)S(1)}, u32[]{:S(2)}, u32[]{:S(2)}) %collective-permute-start.28) | collective-permute-done | bytes 819232 | tf_op jit(solution)/shard_map/ppermute | solution.py:50
  245.8 1.7 shard_map.104
  (72 shorter events, 5.9 us)
Async XLA Ops:
  0.6 22.2 %collective-permute-start = (bf16[1024,1280]{1,0:T(8,128)(2,1)}, bf16[1024,1280]{1,0:T(8,128)(2,1)}, u32[]{:S(2)}, u32[]{:S(2)}) collective-permute-start(bf16[1024,1280]{1,0:T(8,128)(2,1)} %features.1), channel_id=1, source_target_pairs={{0,1},{1,0},{2,3},{3,2},{4,5},{5,4},{6,7},{7,6},{8,9},{9,8},{10,11... | collective-permute-start | bytes 7864328 | tf_op jit(solution)/shard_map/ppermute | solution.py:39
  0.7 59.6 %collective-permute-start.11 = (bf16[1024,1280]{1,0:T(8,128)(2,1)}, bf16[1024,1280]{1,0:T(8,128)(2,1)}, u32[]{:S(2)}, u32[]{:S(2)}) collective-permute-start(bf16[1024,1280]{1,0:T(8,128)(2,1)} %features.1), channel_id=1, source_target_pairs={{0,2},{2,0},{1,3},{3,1},{4,6},{6,4},{5,7},{7,5},{8,10},{10,8},{9,1... | collective-permute-start | bytes 7864328 | tf_op jit(solution)/shard_map/ppermute | solution.py:39
  2.5 1.1 copy-start.7
  3.6 1.1 copy-start.8
  4.8 1.1 copy-start.9
  5.9 10.8 %copy-start = (bf16[1024,1280]{1,0:T(8,128)(2,1)S(1)}, bf16[1024,1280]{1,0:T(8,128)(2,1)}, u32[]{:S(2)}) copy-start(bf16[1024,1280]{1,0:T(8,128)(2,1)} %cotangent.7) | copy-start | bytes 7864324
  7.4 1.2 copy-start.1
  8.6 30.1 %all-to-all-start = ((bf16[16,2,40,480]{3,2,1,0:T(8,128)(2,1)}), bf16[16,2,40,480]{3,2,1,0:T(8,128)(2,1)}, u32[]{:S(2)}, u32[]{:S(2)}) async-start(bf16[16,2,40,480]{3,2,1,0:T(8,128)(2,1)} %copy-done.1), calls=%async_computation | async-start | bytes 2621440 | tf_op jit(solution)/shard_map/all_to_all | solution.py:359
  16.7 1.7 copy-start.2
  31.6 1.2 copy-start.3
  32.7 0.9 copy-start.5
  33.6 0.9 copy-start.10
  34.5 0.9 copy-start.12
  35.4 13.9 %collective-permute-start.2 = (bf16[2,160,1280]{2,1,0:T(8,128)(2,1)}, bf16[2,160,1280]{2,1,0:T(8,128)(2,1)}, u32[]{:S(2)}, u32[]{:S(2)}) collective-permute-start(bf16[2,160,1280]{2,1,0:T(8,128)(2,1)} %get-tuple-element.44), channel_id=1, source_target_pairs={{0,4},{1,17},{4,8},{5,21},{8,12},{9,25},{12,0},{13,29},{16,20},{17... | collective-permute-start | bytes 2457608 | tf_op jit(solution)/shard_map/ppermute | solution.py:50
  37.3 12.7 %collective-permute-start.3 = (bf16[2,160,1280]{2,1,0:T(8,128)(2,1)}, bf16[2,160,1280]{2,1,0:T(8,128)(2,1)}, u32[]{:S(2)}, u32[]{:S(2)}) collective-permute-start(bf16[2,160,1280]{2,1,0:T(8,128)(2,1)} %get-tuple-element.46), channel_id=1, source_target_pairs={{0,12},{1,49},{4,0},{5,53},{8,4},{9,57},{12,8},{13,61},{16,28},{17... | collective-permute-start | bytes 2457608 | tf_op jit(solution)/shard_map/ppermute | solution.py:50
  38.7 11.3 %copy-start.6 = (bf16[2,160,1280]{2,1,0:T(8,128)(2,1)S(1)}, bf16[2,160,1280]{2,1,0:T(8,128)(2,1)}, u32[]{:S(2)}) copy-start(bf16[2,160,1280]{2,1,0:T(8,128)(2,1)} %copy-done.5) | copy-start | bytes 2457604
  38.7 21.7 %copy-start.13 = (bf16[2,160,1280]{2,1,0:T(8,128)(2,1)S(1)}, bf16[2,160,1280]{2,1,0:T(8,128)(2,1)}, u32[]{:S(2)}) copy-start(bf16[2,160,1280]{2,1,0:T(8,128)(2,1)} %copy-done.12) | copy-start | bytes 2457604
  38.7 24.8 %copy-start.11 = (bf16[2,160,1280]{2,1,0:T(8,128)(2,1)S(1)}, bf16[2,160,1280]{2,1,0:T(8,128)(2,1)}, u32[]{:S(2)}) copy-start(bf16[2,160,1280]{2,1,0:T(8,128)(2,1)} %copy-done.10) | copy-start | bytes 2457604
  60.3 12.0 %collective-permute-start.12 = (bf16[1024,1280]{1,0:T(8,128)(2,1)}, bf16[1024,1280]{1,0:T(8,128)(2,1)S(1)}, u32[]{:S(2)}, u32[]{:S(2)}) collective-permute-start(bf16[1024,1280]{1,0:T(8,128)(2,1)} %collective-permute-done.11.features), channel_id=1, source_target_pairs={{0,1},{1,0},{2,3},{3,2},{4,5},{5,4},{6,7},{7,6},{8,9},{9,8},{10,11... | collective-permute-start | bytes 7864328 | tf_op jit(solution)/shard_map/ppermute | solution.py:39
  60.3 18.6 %collective-permute-start.1 = (bf16[2,160,1280]{2,1,0:T(8,128)(2,1)S(1)}, bf16[2,160,1280]{2,1,0:T(8,128)(2,1)S(1)}, u32[]{:S(2)}, u32[]{:S(2)}) collective-permute-start(bf16[2,160,1280]{2,1,0:T(8,128)(2,1)S(1)} %copy-done.13), channel_id=1, source_target_pairs={{0,12},{1,49},{4,0},{5,53},{8,4},{9,57},{12,8},{13,61},{16,28},{17... | collective-permute-start | bytes 2457608 | tf_op jit(solution)/shard_map/ppermute | solution.py:50
  63.4 18.6 %collective-permute-start.5 = (bf16[2,160,1280]{2,1,0:T(8,128)(2,1)S(1)}, bf16[2,160,1280]{2,1,0:T(8,128)(2,1)S(1)}, u32[]{:S(2)}, u32[]{:S(2)}) collective-permute-start(bf16[2,160,1280]{2,1,0:T(8,128)(2,1)S(1)} %copy-done.11), channel_id=1, source_target_pairs={{0,4},{1,17},{4,8},{5,21},{8,12},{9,25},{12,0},{13,29},{16,20},{17... | collective-permute-start | bytes 2457608 | tf_op jit(solution)/shard_map/ppermute | solution.py:50
  63.4 22.3 %collective-permute-start.4 = (bf16[2,160,1280]{2,1,0:T(8,128)(2,1)S(1)}, bf16[2,160,1280]{2,1,0:T(8,128)(2,1)S(1)}, u32[]{:S(2)}, u32[]{:S(2)}) collective-permute-start(bf16[2,160,1280]{2,1,0:T(8,128)(2,1)S(1)} %get-tuple-element.47), channel_id=1, source_target_pairs={{0,4},{1,17},{4,8},{5,21},{8,12},{9,25},{12,0},{13,29},{16,20},{17... | collective-permute-start | bytes 2457608 | tf_op jit(solution)/shard_map/ppermute | solution.py:50
  64.0 21.7 %collective-permute-start.6 = (bf16[2,160,1280]{2,1,0:T(8,128)(2,1)S(1)}, bf16[2,160,1280]{2,1,0:T(8,128)(2,1)S(1)}, u32[]{:S(2)}, u32[]{:S(2)}) collective-permute-start(bf16[2,160,1280]{2,1,0:T(8,128)(2,1)S(1)} %get-tuple-element.49), channel_id=1, source_target_pairs={{0,12},{1,49},{4,0},{5,53},{8,4},{9,57},{12,8},{13,61},{16,28},{17... | collective-permute-start | bytes 2457608 | tf_op jit(solution)/shard_map/ppermute | solution.py:50
  72.3 13.5 %copy-start.4 = (bf16[4,160,1280]{2,1,0:T(8,128)(2,1)S(1)}, bf16[4,160,1280]{2,1,0:T(8,128)(2,1)}, u32[]{:S(2)}) copy-start(bf16[4,160,1280]{2,1,0:T(8,128)(2,1)} %copy-done.3) | copy-start | bytes 4915204
  78.9 18.5 %collective-permute-start.14 = (bf16[2,160,1280]{2,1,0:T(8,128)(2,1)S(1)}, bf16[2,160,1280]{2,1,0:T(8,128)(2,1)S(1)}, u32[]{:S(2)}, u32[]{:S(2)}) collective-permute-start(bf16[2,160,1280]{2,1,0:T(8,128)(2,1)S(1)} %get-tuple-element.58), channel_id=1, source_target_pairs={{0,4},{1,17},{4,8},{5,21},{8,12},{9,25},{12,0},{13,29},{16,20},{17... | collective-permute-start | bytes 2457608 | tf_op jit(solution)/shard_map/ppermute | solution.py:50
  79.0 39.0 %collective-permute-start.23 = (bf16[2,3,160,640]{3,2,1,0:T(8,128)(2,1)S(1)}, bf16[2,3,160,640]{3,2,1,0:T(8,128)(2,1)S(1)}, u32[]{:S(2)}, u32[]{:S(2)}) collective-permute-start(bf16[2,3,160,640]{3,2,1,0:T(8,128)(2,1)S(1)} %shard_map.90.here), channel_id=1, source_target_pairs={{0,64},{64,0},{1,65},{65,1},{2,66},{66,2},{3,67},{67,3},{4,68},{68... | collective-permute-start | bytes 3686408 | tf_op jit(solution)/shard_map/ppermute | solution.py:39
  82.1 25.3 %collective-permute-start.15 = (bf16[2,160,1280]{2,1,0:T(8,128)(2,1)S(1)}, bf16[2,160,1280]{2,1,0:T(8,128)(2,1)S(1)}, u32[]{:S(2)}, u32[]{:S(2)}) collective-permute-start(bf16[2,160,1280]{2,1,0:T(8,128)(2,1)S(1)} %get-tuple-element.60), channel_id=1, source_target_pairs={{0,12},{1,49},{4,0},{5,53},{8,4},{9,57},{12,8},{13,61},{16,28},{17... | collective-permute-start | bytes 2457608 | tf_op jit(solution)/shard_map/ppermute | solution.py:50
  87.4 20.9 %collective-permute-start.7 = (bf16[160,1280]{1,0:T(8,128)(2,1)S(1)}, bf16[160,1280]{1,0:T(8,128)(2,1)S(1)}, u32[]{:S(2)}, u32[]{:S(2)}) collective-permute-start(bf16[160,1280]{1,0:T(8,128)(2,1)S(1)} %get-tuple-element.51), channel_id=1, source_target_pairs={{0,16},{1,5},{4,20},{5,9},{8,24},{9,13},{12,28},{13,1},{16,32},{17... | collective-permute-start | bytes 1228808 | tf_op jit(solution)/shard_map/ppermute | solution.py:50
  89.4 21.0 %collective-permute-start.8 = (bf16[160,1280]{1,0:T(8,128)(2,1)S(1)}, bf16[160,1280]{1,0:T(8,128)(2,1)S(1)}, u32[]{:S(2)}, u32[]{:S(2)}) collective-permute-start(bf16[160,1280]{1,0:T(8,128)(2,1)S(1)} %get-tuple-element.52), channel_id=1, source_target_pairs={{0,32},{1,9},{4,36},{5,13},{8,40},{9,1},{12,44},{13,5},{16,48},{17... | collective-permute-start | bytes 1228808 | tf_op jit(solution)/shard_map/ppermute | solution.py:50
  97.4 19.9 %collective-permute-start.9 = (bf16[160,1280]{1,0:T(8,128)(2,1)S(1)}, bf16[160,1280]{1,0:T(8,128)(2,1)S(1)}, u32[]{:S(2)}, u32[]{:S(2)}) collective-permute-start(bf16[160,1280]{1,0:T(8,128)(2,1)S(1)} %get-tuple-element.53), channel_id=1, source_target_pairs={{0,48},{1,13},{4,52},{5,1},{8,56},{9,5},{12,60},{13,9},{16,0},{17,... | collective-permute-start | bytes 1228808 | tf_op jit(solution)/shard_map/ppermute | solution.py:50
  107.4 23.9 %collective-permute-start.13 = (bf16[2,160,1280]{2,1,0:T(8,128)(2,1)S(1)}, bf16[2,160,1280]{2,1,0:T(8,128)(2,1)S(1)}, u32[]{:S(2)}, u32[]{:S(2)}) collective-permute-start(bf16[2,160,1280]{2,1,0:T(8,128)(2,1)S(1)} %get-tuple-element.56), channel_id=1, source_target_pairs={{0,12},{1,49},{4,0},{5,53},{8,4},{9,57},{12,8},{13,61},{16,28},{17... | collective-permute-start | bytes 2457608 | tf_op jit(solution)/shard_map/ppermute | solution.py:50
  108.3 26.0 %collective-permute-start.17 = (bf16[2,160,1280]{2,1,0:T(8,128)(2,1)S(1)}, bf16[2,160,1280]{2,1,0:T(8,128)(2,1)S(1)}, u32[]{:S(2)}, u32[]{:S(2)}) collective-permute-start(bf16[2,160,1280]{2,1,0:T(8,128)(2,1)S(1)} %get-tuple-element.62), channel_id=1, source_target_pairs={{0,4},{1,17},{4,8},{5,21},{8,12},{9,25},{12,0},{13,29},{16,20},{17... | collective-permute-start | bytes 2457608 | tf_op jit(solution)/shard_map/ppermute | solution.py:50
  110.4 23.9 %collective-permute-start.16 = (bf16[2,160,1280]{2,1,0:T(8,128)(2,1)S(1)}, bf16[2,160,1280]{2,1,0:T(8,128)(2,1)S(1)}, u32[]{:S(2)}, u32[]{:S(2)}) collective-permute-start(bf16[2,160,1280]{2,1,0:T(8,128)(2,1)S(1)} %get-tuple-element.61), channel_id=1, source_target_pairs={{0,4},{1,17},{4,8},{5,21},{8,12},{9,25},{12,0},{13,29},{16,20},{17... | collective-permute-start | bytes 2457608 | tf_op jit(solution)/shard_map/ppermute | solution.py:50
  117.2 17.1 %collective-permute-start.18 = (bf16[2,160,1280]{2,1,0:T(8,128)(2,1)S(1)}, bf16[2,160,1280]{2,1,0:T(8,128)(2,1)S(1)}, u32[]{:S(2)}, u32[]{:S(2)}) collective-permute-start(bf16[2,160,1280]{2,1,0:T(8,128)(2,1)S(1)} %get-tuple-element.63), channel_id=1, source_target_pairs={{0,12},{1,49},{4,0},{5,53},{8,4},{9,57},{12,8},{13,61},{16,28},{17... | collective-permute-start | bytes 2457608 | tf_op jit(solution)/shard_map/ppermute | solution.py:50
  118.0 9.9 %collective-permute-start.10 = (bf16[160,1280]{1,0:T(8,128)(2,1)S(1)}, bf16[160,1280]{1,0:T(8,128)(2,1)S(1)}, u32[]{:S(2)}, u32[]{:S(2)}) collective-permute-start(bf16[160,1280]{1,0:T(8,128)(2,1)S(1)} %shard_map.88.near.one), channel_id=1, source_target_pairs={{0,64},{64,0},{1,65},{65,1},{2,66},{66,2},{3,67},{67,3},{4,68},{68... | collective-permute-start | bytes 1228808 | tf_op jit(solution)/shard_map/ppermute | solution.py:39
  129.5 24.4 %collective-permute-start.33 = (bf16[160,1280]{1,0:T(8,128)(2,1)S(1)}, bf16[160,1280]{1,0:T(8,128)(2,1)S(1)}, u32[]{:S(2)}, u32[]{:S(2)}) collective-permute-start(bf16[160,1280]{1,0:T(8,128)(2,1)S(1)} %shard_map.99.refs_0_), channel_id=1, source_target_pairs={{0,16},{1,5},{4,20},{5,9},{8,24},{9,13},{12,28},{13,1},{16,32},{17... | collective-permute-start | bytes 1228808 | tf_op jit(solution)/shard_map/ppermute | solution.py:50
  131.3 25.1 %collective-permute-start.34 = (bf16[160,1280]{1,0:T(8,128)(2,1)S(1)}, bf16[160,1280]{1,0:T(8,128)(2,1)S(1)}, u32[]{:S(2)}, u32[]{:S(2)}) collective-permute-start(bf16[160,1280]{1,0:T(8,128)(2,1)S(1)} %shard_map.99.refs_0_), channel_id=1, source_target_pairs={{0,32},{1,9},{4,36},{5,13},{8,40},{9,1},{12,44},{13,5},{16,48},{17... | collective-permute-start | bytes 1228808 | tf_op jit(solution)/shard_map/ppermute | solution.py:50
  134.4 22.0 %collective-permute-start.35 = (bf16[160,1280]{1,0:T(8,128)(2,1)S(1)}, bf16[160,1280]{1,0:T(8,128)(2,1)S(1)}, u32[]{:S(2)}, u32[]{:S(2)}) collective-permute-start(bf16[160,1280]{1,0:T(8,128)(2,1)S(1)} %shard_map.99.refs_0_), channel_id=1, source_target_pairs={{0,48},{1,13},{4,52},{5,1},{8,56},{9,5},{12,60},{13,9},{16,0},{17,... | collective-permute-start | bytes 1228808 | tf_op jit(solution)/shard_map/ppermute | solution.py:50
  136.0 21.2 %collective-permute-start.19 = (bf16[160,1280]{1,0:T(8,128)(2,1)S(1)}, bf16[160,1280]{1,0:T(8,128)(2,1)S(1)}, u32[]{:S(2)}, u32[]{:S(2)}) collective-permute-start(bf16[160,1280]{1,0:T(8,128)(2,1)S(1)} %get-tuple-element.65), channel_id=1, source_target_pairs={{0,16},{1,5},{4,20},{5,9},{8,24},{9,13},{12,28},{13,1},{16,32},{17... | collective-permute-start | bytes 1228808 | tf_op jit(solution)/shard_map/ppermute | solution.py:50
  138.1 26.0 %collective-permute-start.20 = (bf16[160,1280]{1,0:T(8,128)(2,1)S(1)}, bf16[160,1280]{1,0:T(8,128)(2,1)S(1)}, u32[]{:S(2)}, u32[]{:S(2)}) collective-permute-start(bf16[160,1280]{1,0:T(8,128)(2,1)S(1)} %get-tuple-element.66), channel_id=1, source_target_pairs={{0,32},{1,9},{4,36},{5,13},{8,40},{9,1},{12,44},{13,5},{16,48},{17... | collective-permute-start | bytes 1228808 | tf_op jit(solution)/shard_map/ppermute | solution.py:50
  153.9 14.3 %collective-permute-start.21 = (bf16[160,1280]{1,0:T(8,128)(2,1)S(1)}, bf16[160,1280]{1,0:T(8,128)(2,1)S(1)}, u32[]{:S(2)}, u32[]{:S(2)}) collective-permute-start(bf16[160,1280]{1,0:T(8,128)(2,1)S(1)} %get-tuple-element.67), channel_id=1, source_target_pairs={{0,48},{1,13},{4,52},{5,1},{8,56},{9,5},{12,60},{13,9},{16,0},{17,... | collective-permute-start | bytes 1228808 | tf_op jit(solution)/shard_map/ppermute | solution.py:50
  157.1 31.9 %collective-permute-start.36 = (bf16[2,160,1280]{2,1,0:T(8,128)(2,1)S(1)}, bf16[2,160,1280]{2,1,0:T(8,128)(2,1)S(1)}, u32[]{:S(2)}, u32[]{:S(2)}) collective-permute-start(bf16[2,160,1280]{2,1,0:T(8,128)(2,1)S(1)} %get-tuple-element.76.refs_0_), channel_id=1, source_target_pairs={{0,4},{1,17},{4,8},{5,21},{8,12},{9,25},{12,0},{13,29},{16,20},{17... | collective-permute-start | bytes 2457608 | tf_op jit(solution)/shard_map/ppermute | solution.py:50
  168.9 9.5 %collective-permute-start.22 = (bf16[160,1280]{1,0:T(8,128)(2,1)S(1)}, bf16[160,1280]{1,0:T(8,128)(2,1)S(1)}, u32[]{:S(2)}, u32[]{:S(2)}) collective-permute-start(bf16[160,1280]{1,0:T(8,128)(2,1)S(1)} %shard_map.95.far.one), channel_id=1, source_target_pairs={{0,64},{64,0},{1,65},{65,1},{2,66},{66,2},{3,67},{67,3},{4,68},{68... | collective-permute-start | bytes 1228808 | tf_op jit(solution)/shard_map/ppermute | solution.py:39
  169.0 37.3 %collective-permute-start.38 = (bf16[2,160,1280]{2,1,0:T(8,128)(2,1)S(1)}, bf16[2,160,1280]{2,1,0:T(8,128)(2,1)S(1)}, u32[]{:S(2)}, u32[]{:S(2)}) collective-permute-start(bf16[2,160,1280]{2,1,0:T(8,128)(2,1)S(1)} %get-tuple-element.77.refs_1_), channel_id=1, source_target_pairs={{0,12},{1,49},{4,0},{5,53},{8,4},{9,57},{12,8},{13,61},{16,28},{17... | collective-permute-start | bytes 2457608 | tf_op jit(solution)/shard_map/ppermute | solution.py:50
  180.0 14.8 %collective-permute-start.24 = (bf16[160,1280]{1,0:T(8,128)(2,1)S(1)}, bf16[160,1280]{1,0:T(8,128)(2,1)S(1)}, u32[]{:S(2)}, u32[]{:S(2)}) collective-permute-start(bf16[160,1280]{1,0:T(8,128)(2,1)S(1)} %shard_map.97.refs_0_), channel_id=1, source_target_pairs={{0,16},{1,5},{4,20},{5,9},{8,24},{9,13},{12,28},{13,1},{16,32},{17... | collective-permute-start | bytes 1228808 | tf_op jit(solution)/shard_map/ppermute | solution.py:50
  180.4 25.1 %collective-permute-start.25 = (bf16[160,1280]{1,0:T(8,128)(2,1)S(1)}, bf16[160,1280]{1,0:T(8,128)(2,1)S(1)}, u32[]{:S(2)}, u32[]{:S(2)}) collective-permute-start(bf16[160,1280]{1,0:T(8,128)(2,1)S(1)} %shard_map.97.refs_0_), channel_id=1, source_target_pairs={{0,32},{1,9},{4,36},{5,13},{8,40},{9,1},{12,44},{13,5},{16,48},{17... | collective-permute-start | bytes 1228808 | tf_op jit(solution)/shard_map/ppermute | solution.py:50
  186.5 19.0 %collective-permute-start.26 = (bf16[160,1280]{1,0:T(8,128)(2,1)S(1)}, bf16[160,1280]{1,0:T(8,128)(2,1)S(1)}, u32[]{:S(2)}, u32[]{:S(2)}) collective-permute-start(bf16[160,1280]{1,0:T(8,128)(2,1)S(1)} %shard_map.97.refs_0_), channel_id=1, source_target_pairs={{0,48},{1,13},{4,52},{5,1},{8,56},{9,5},{12,60},{13,9},{16,0},{17,... | collective-permute-start | bytes 1228808 | tf_op jit(solution)/shard_map/ppermute | solution.py:50
  189.0 20.6 %collective-permute-start.40 = (bf16[2,160,1280]{2,1,0:T(8,128)(2,1)S(1)}, bf16[2,160,1280]{2,1,0:T(8,128)(2,1)S(1)}, u32[]{:S(2)}, u32[]{:S(2)}) collective-permute-start(bf16[2,160,1280]{2,1,0:T(8,128)(2,1)S(1)} %get-tuple-element.77.refs_1_), channel_id=1, source_target_pairs={{0,4},{1,17},{4,8},{5,21},{8,12},{9,25},{12,0},{13,29},{16,20},{17... | collective-permute-start | bytes 2457608 | tf_op jit(solution)/shard_map/ppermute | solution.py:50
  194.8 16.8 %collective-permute-start.41 = (bf16[2,160,1280]{2,1,0:T(8,128)(2,1)S(1)}, bf16[2,160,1280]{2,1,0:T(8,128)(2,1)S(1)}, u32[]{:S(2)}, u32[]{:S(2)}) collective-permute-start(bf16[2,160,1280]{2,1,0:T(8,128)(2,1)S(1)} %get-tuple-element.76.refs_0_), channel_id=1, source_target_pairs={{0,12},{1,49},{4,0},{5,53},{8,4},{9,57},{12,8},{13,61},{16,28},{17... | collective-permute-start | bytes 2457608 | tf_op jit(solution)/shard_map/ppermute | solution.py:50
  205.5 13.6 %collective-permute-start.37 = (bf16[2,160,1280]{2,1,0:T(8,128)(2,1)S(1)}, bf16[2,160,1280]{2,1,0:T(8,128)(2,1)S(1)}, u32[]{:S(2)}, u32[]{:S(2)}) collective-permute-start(bf16[2,160,1280]{2,1,0:T(8,128)(2,1)S(1)} %collective-permute-done.36.refs_2_), channel_id=1, source_target_pairs={{0,4},{1,17},{4,8},{5,21},{8,12},{9,25},{12,0},{13,29},{16,20},{17... | collective-permute-start | bytes 2457608 | tf_op jit(solution)/shard_map/ppermute | solution.py:50
  206.2 21.6 %collective-permute-start.27 = (bf16[2,160,1280]{2,1,0:T(8,128)(2,1)S(1)}, bf16[2,160,1280]{2,1,0:T(8,128)(2,1)S(1)}, u32[]{:S(2)}, u32[]{:S(2)}) collective-permute-start(bf16[2,160,1280]{2,1,0:T(8,128)(2,1)S(1)} %get-tuple-element.72.refs_0_), channel_id=1, source_target_pairs={{0,4},{1,17},{4,8},{5,21},{8,12},{9,25},{12,0},{13,29},{16,20},{17... | collective-permute-start | bytes 2457608 | tf_op jit(solution)/shard_map/ppermute | solution.py:50
  206.3 21.5 %collective-permute-start.29 = (bf16[2,160,1280]{2,1,0:T(8,128)(2,1)S(1)}, bf16[2,160,1280]{2,1,0:T(8,128)(2,1)S(1)}, u32[]{:S(2)}, u32[]{:S(2)}) collective-permute-start(bf16[2,160,1280]{2,1,0:T(8,128)(2,1)S(1)} %get-tuple-element.73.refs_1_), channel_id=1, source_target_pairs={{0,12},{1,49},{4,0},{5,53},{8,4},{9,57},{12,8},{13,61},{16,28},{17... | collective-permute-start | bytes 2457608 | tf_op jit(solution)/shard_map/ppermute | solution.py:50
  209.6 27.4 %collective-permute-start.39 = (bf16[2,160,1280]{2,1,0:T(8,128)(2,1)S(1)}, bf16[2,160,1280]{2,1,0:T(8,128)(2,1)S(1)}, u32[]{:S(2)}, u32[]{:S(2)}) collective-permute-start(bf16[2,160,1280]{2,1,0:T(8,128)(2,1)S(1)} %collective-permute-done.38.refs_3_), channel_id=1, source_target_pairs={{0,12},{1,49},{4,0},{5,53},{8,4},{9,57},{12,8},{13,61},{16,28},{17... | collective-permute-start | bytes 2457608 | tf_op jit(solution)/shard_map/ppermute | solution.py:50
  211.6 27.2 %collective-permute-start.31 = (bf16[2,160,1280]{2,1,0:T(8,128)(2,1)S(1)}, bf16[2,160,1280]{2,1,0:T(8,128)(2,1)S(1)}, u32[]{:S(2)}, u32[]{:S(2)}) collective-permute-start(bf16[2,160,1280]{2,1,0:T(8,128)(2,1)S(1)} %get-tuple-element.73.refs_1_), channel_id=1, source_target_pairs={{0,4},{1,17},{4,8},{5,21},{8,12},{9,25},{12,0},{13,29},{16,20},{17... | collective-permute-start | bytes 2457608 | tf_op jit(solution)/shard_map/ppermute | solution.py:50
  219.0 19.7 %collective-permute-start.32 = (bf16[2,160,1280]{2,1,0:T(8,128)(2,1)S(1)}, bf16[2,160,1280]{2,1,0:T(8,128)(2,1)S(1)}, u32[]{:S(2)}, u32[]{:S(2)}) collective-permute-start(bf16[2,160,1280]{2,1,0:T(8,128)(2,1)S(1)} %get-tuple-element.72.refs_0_), channel_id=1, source_target_pairs={{0,12},{1,49},{4,0},{5,53},{8,4},{9,57},{12,8},{13,61},{16,28},{17... | collective-permute-start | bytes 2457608 | tf_op jit(solution)/shard_map/ppermute | solution.py:50
  227.8 17.6 %collective-permute-start.28 = (bf16[2,160,1280]{2,1,0:T(8,128)(2,1)S(1)}, bf16[2,160,1280]{2,1,0:T(8,128)(2,1)S(1)}, u32[]{:S(2)}, u32[]{:S(2)}) collective-permute-start(bf16[2,160,1280]{2,1,0:T(8,128)(2,1)S(1)} %collective-permute-done.27.refs_2_), channel_id=1, source_target_pairs={{0,4},{1,17},{4,8},{5,21},{8,12},{9,25},{12,0},{13,29},{16,20},{17... | collective-permute-start | bytes 2457608 | tf_op jit(solution)/shard_map/ppermute | solution.py:50
  227.8 18.0 %collective-permute-start.30 = (bf16[2,160,1280]{2,1,0:T(8,128)(2,1)S(1)}, bf16[2,160,1280]{2,1,0:T(8,128)(2,1)S(1)}, u32[]{:S(2)}, u32[]{:S(2)}) collective-permute-start(bf16[2,160,1280]{2,1,0:T(8,128)(2,1)S(1)} %collective-permute-done.29.refs_3_), channel_id=1, source_target_pairs={{0,12},{1,49},{4,0},{5,53},{8,4},{9,57},{12,8},{13,61},{16,28},{17... | collective-permute-start | bytes 2457608 | tf_op jit(solution)/shard_map/ppermute | solution.py:50
